TPU v7x, 512 devices: a 4x2x32 block of a 4x8x32 slice. The times are simulated.
512 devices in a mesh: rep: 2 (over y), gx: 128 (over x, z), gy: 2 (over core).
Axes of the slice: x: 4, y: 2, z: 32, core: 2. Of those that a mesh axis runs over, the one named last changes fastest.
The devices are a block of a 4x8x32 slice.
Arguments:
- tokens: bfloat16 [768, 8192], P(('rep', 'gx'), 'gy'), parts along dimension 0, may hold values from -6 to 6
- segment_ids: int32 [768], P(('rep', 'gx')), parts along dimension 0, may hold values from 0 to 1, as said below
- gate_weight: bfloat16 [8192, 2, 13312], P(None, 'gy', 'gx'), may hold values from -0.0625 to 0.0625
- up_weight: bfloat16 [8192, 2, 13312], P(None, 'gy', 'gx'), may hold values from -0.0625 to 0.0625
- down_weight: bfloat16 [2, 13312, 8192], P('gy', None, 'gx'), may hold values from -0.0390625 to 0.0390625
Outputs:
- grouped: bfloat16 [768, 8192], P(('rep', 'gx'), 'gy'), parts along dimension 0
There are 2 independent parts, one for each index of `rep`. A program takes and returns all parts, laid end to end along the dimension named above; an argument that names none is the same for every part. Nothing has to cross between parts.
Inputs may be any that keep to these rules, and one draw needn't show every extreme that they name: `segment_ids`: exactly 320 entries are 0 and 64 entries are 1.
All inputs are finite; a program needn't handle non-finite values.
Results may differ from a plain program's by a relative error of at most 0.0049.
Values may be sent and summed in bfloat16 or wider, within the bound.
No kernel may reach another device: no remote copies, remote signals or barrier semaphores. Data moves between devices by JAX's collectives and lax.ppermute only.
A program may use at most 128 MiB of HBM per device.

v0:
```python
import jax
import jax.numpy as jnp
from jax import lax
from jax.sharding import Mesh
from jax.sharding import PartitionSpec as P

PREFILL = 320
GX = ("gx_0", "gx_1")
REP_GX = ("rep", "gx_0", "gx_1")


def gather_axes(shard, axes, dim):
    for axis in reversed(axes):
        shard = lax.all_gather(shard, axis, axis=dim, tiled=True)
    return shard


def from_everyone(shard, axis):
    copies = jnp.broadcast_to(shard, (lax.axis_size(axis), *shard.shape))
    return lax.all_to_all(copies, axis, split_axis=0, concat_axis=0, tiled=True)


def laid_out(blocks, dim):
    dims = list(blocks.shape[1:])
    dims[dim] *= blocks.shape[0]
    return jnp.moveaxis(blocks, 0, dim).reshape(dims)


def gathered_copies(shard, axis, dim):
    blocks = from_everyone(shard, axis)
    return laid_out(blocks, dim)


def all_blocks(shard, axes, sequence):
    blocks = shard[None]
    for k in sequence:
        blocks = lax.all_gather(blocks, axes[k], axis=0, tiled=True)
    current = [lax.axis_size(axes[k]) for k in reversed(sequence)]
    blocks = blocks.reshape(*current, *shard.shape)
    turned = sorted(range(len(sequence)), key=lambda place: sequence[len(sequence) - 1 - place])
    return blocks.transpose(*turned, *range(len(sequence), blocks.ndim)).reshape(-1, *shard.shape)


def gather_axes_2(shard, axes, sequence, dim):
    return laid_out(all_blocks(shard, axes, sequence), dim)


def cut_along(shard, dim, count):
    before, after = (shard.shape[:dim], shard.shape[dim + 1 :])
    return jnp.moveaxis(shard.reshape(*before, count, -1, *after), dim, 0)


def summed_on_arrival(shard, axis, dim):
    count = lax.axis_size(axis)
    blocks = lax.all_to_all(cut_along(shard, dim, count), axis, 0, 0, tiled=True)
    return jnp.sum(blocks, axis=0)


def grouped_target(token_kinds):
    decode_flag = token_kinds.astype(jnp.int32)
    prefill_flag = 1 - decode_flag
    prefill_rank = jnp.cumsum(prefill_flag) - 1
    decode_rank = jnp.cumsum(decode_flag) - 1
    return jnp.where(decode_flag == 0, prefill_rank, PREFILL + decode_rank)


def local(tokens, segment_ids, gate_weight, up_weight, down_weight):
    half_rows, token_kinds = (gather_axes(tokens, GX, 0), gather_axes(segment_ids, GX, 0))
    gathered = gathered_copies(half_rows, "gy", 1)
    gate_local = gate_weight.reshape(gate_weight.shape[0], -1)
    up_local = up_weight.reshape(up_weight.shape[0], -1)
    down_local = down_weight.reshape(-1, down_weight.shape[2])
    target = grouped_target(token_kinds)
    gate_value = jnp.dot(gathered, gate_local, preferred_element_type=jnp.float32)
    up_value = jnp.dot(gathered, up_local, preferred_element_type=jnp.float32)
    hidden = (jax.nn.silu(gate_value) * up_value).astype(jnp.bfloat16)
    partial_value = jnp.dot(
        gather_axes_2(hidden, GX, (0, 1), 1), down_local, preferred_element_type=jnp.float32
    )
    placed = jnp.zeros_like(partial_value).at[target].set(partial_value)
    switched = lax.all_to_all(placed, GX, split_axis=0, concat_axis=1, tiled=True)
    return summed_on_arrival(switched, "gy", 1).astype(jnp.bfloat16)


def solution(mesh):
    torus = Mesh(
        mesh.devices.reshape(mesh.shape["rep"], 4, 32, mesh.shape["gy"]),
        ("rep", "gx_0", "gx_1", "gy"),
    )
    placed = (P(REP_GX, "gy"), P(REP_GX), P(None, "gy", GX), P(None, "gy", GX), P("gy", None, GX))
    return jax.shard_map(
        local, mesh=torus, in_specs=placed, out_specs=P(REP_GX, "gy"), check_vma=False
    )
```

profile of v0, /device:TPU:33, one launch (start us, length us, event | category | flops | bytes accessed | tf_op | source)
XLA Modules:
  0.0 413.4 jit_solution(14316246672419341581)
XLA Ops:
  6.5 0.0 copy-start
  6.6 0.0 all-gather.5.cloned.1.call-start
  6.6 88.2 %all-gather.1 = bf16[32,3,4096]{2,1,0:T(4,128)(2,1)S(1)} all-gather(bf16[1,3,4096]{2,1,0:T(4,128)(2,1)} %bitcast.53), channel_id=1, replica_groups=mesh['rep'=2,'gx_0'=4,'gx_1'=32,'gy'=2] {'gx_1'}, dimensions={0}, use_global_device_ids=true | all-gather | bytes 811008 | tf_op jit(solution)/shard_map/all_gather | solution.py:14
  94.7 1.4 reshape.89
  96.1 0.1 all-gather.5.cloned.1.call-update
  96.2 0.1 all-gather.7.cloned.1.call-start
  96.3 53.2 %all-gather.5.cloned.1.call-done = bf16[384,4096]{1,0:T(8,128)(2,1)} async-done(((bf16[96,4096]{1,0:T(8,128)(2,1)}), bf16[384,4096]{1,0:T(8,128)(2,1)}) %all-gather.5.cloned.1.call-update) | async-done | bytes 3145744 | tf_op jit(solution)/shard_map/all_gather | solution.py:14
  149.5 4.7 %copy.14 = bf16[384,4096]{0,1:T(8,128)(2,1)} copy(bf16[384,4096]{1,0:T(8,128)(2,1)} %all-gather.5.cloned.1.call-done) | data formatting | bytes 6291456 | tf_op jit(solution)/shard_map/all_gather | solution.py:14
  154.2 2.4 broadcast_in_dim.14
  156.6 9.3 %all_to_all.26 = bf16[2,384,4096]{1,2,0:T(8,128)(2,1)S(1)} all-to-all(bf16[2,384,4096]{1,2,0:T(8,128)(2,1)S(1)} %broadcast_in_dim.14), channel_id=1, replica_groups=mesh['rep'=2,'gx_0'=4,'gx_1'=32,'gy'=2] {'gy'}, dimensions={0} | all-to-all | bytes 12582912 | tf_op jit(solution)/shard_map/all_to_all | solution.py:20
  165.9 0.0 copy-done
  165.9 0.0 copy-start.1
  165.9 1.2 fusion.4
  167.1 0.2 copy-done.1
  167.3 0.0 copy-start.3
  167.3 1.2 fusion.9
  168.5 9.7 %all-gather = bf16[1536,104]{0,1:T(8,128)(2,1)S(1)} all-gather(bf16[384,104]{0,1:T(8,128)(2,1)S(1)} %fusion.9), channel_id=2, replica_groups=mesh['rep'=2,'gx_0'=4,'gx_1'=32,'gy'=2] {'gx_0'}, dimensions={0}, use_global_device_ids=true | all-gather | bytes 399360 | tf_op jit(solution)/shard_map/all_gather | solution.py:37
  178.2 0.7 copy.23
  179.0 0.1 all-gather.7.cloned.1.call-update
  179.0 1.3 dynamic-slice
  180.3 1.3 dynamic-slice.1
  182.9 0.0 copy-done.3
  182.9 0.2 dynamic-update-slice
  183.1 33.9 %all-reduce = s32[96]{0:T(128)S(1)} all-reduce(s32[96]{0:T(128)S(1)} %dynamic-update-slice), channel_id=1, replica_groups=mesh['rep'=2,'gx_0'=4,'gx_1'=32,'gy'=2] {'gx_1'}, use_global_device_ids=true, to_apply=%add | all-reduce | flops 96 | bytes 768
  217.0 0.2 dynamic-update-slice.1
  217.2 5.6 %all-reduce.1 = s32[384]{0:T(512)S(1)} all-reduce(s32[384]{0:T(512)S(1)} %dynamic-update-slice.1), channel_id=1, replica_groups=mesh['rep'=2,'gx_0'=4,'gx_1'=32,'gy'=2] {'gx_0'}, use_global_device_ids=true, to_apply=%add.1 | all-reduce | flops 384 | bytes 3072
  222.8 0.3 reduce-window.16
  223.1 0.1 slice.14
  223.2 0.3 reduce-window.24
  223.5 0.1 slice.16
  223.7 0.1 slice_reduce_fusion
  223.8 0.1 compare_select_fusion
  223.9 96.5 %all-gather.7.cloned.1.call-done = bf16[128,384,104]{1,2,0:T(8,128)(2,1)} async-done(((bf16[4,384,104]{1,2,0:T(8,128)(2,1)}), bf16[128,384,104]{1,2,0:T(8,128)(2,1)}) %all-gather.7.cloned.1.call-update) | async-done | bytes 10223632 | tf_op jit(solution)/shard_map/all_gather | solution.py:37
  320.3 0.0 copy-start.2
  320.3 8.9 %copy.16 = bf16[4,32,384,104]{2,3,1,0:T(8,128)(2,1)} copy(bf16[4,32,384,104]{2,3,0,1:T(8,128)(2,1)} %bitcast.47) | data formatting | bytes 20447232 | tf_op jit(solution)/shard_map/transpose | solution.py:41
  329.2 0.0 copy-done.2
  329.2 6.2 %fusion = f32[384,64]{1,0:T(8,128)} fusion(bf16[384,13312]{0,1:T(8,128)(2,1)} %bitcast.48, bf16[1,13312,64]{1,2,0:T(8,128)(2,1)S(1)} %copy-done.2), kind=kOutput, calls=%fused_computation.1 | convolution fusion | flops 654311424 | bytes 12025856 | tf_op jit(solution)/shard_map/dot_general | solution.py:77
  335.4 1.9 scatter_custom_fusion
  337.3 0.1 all_to_all.19
  337.4 0.2 reshape.98
  337.6 45.1 %all_to_all.27 = f32[128,1,192]{2,1,0:T(1,128)S(1)} all-to-all(f32[128,1,192]{2,1,0:T(1,128)S(1)} %reshape.98), channel_id=1, replica_groups=mesh['rep'=2,'gx_0'=4,'gx_1'=32,'gy'=2] {'gx_0','gx_1'}, dimensions={0} | all-to-all | bytes 196608 | tf_op jit(solution)/shard_map/all_to_all | solution.py:81
  382.7 0.5 broadcast.39
  383.2 1.0 reduce.4
  384.2 0.1 reshape.99
  384.3 0.1 reshape.71
  384.5 0.1 copy.19
  384.6 21.4 %all_to_all.28 = f32[2,3,4096]{2,1,0:T(4,128)S(1)} all-to-all(f32[2,3,4096]{2,1,0:T(4,128)S(1)} %copy.19), channel_id=1, replica_groups=mesh['rep'=2,'gx_0'=4,'gx_1'=32,'gy'=2] {'gy'}, dimensions={0} | all-to-all | bytes 196608 | tf_op jit(solution)/shard_map/all_to_all | solution.py:55
  405.9 0.6 reduce_sum.9
  (6 shorter events, 0.1 us)
Async XLA Ops:
  6.5 159.3 %copy-start = (bf16[8192,1,104]{0,2,1:T(8,128)(2,1)S(1)}, bf16[8192,1,104]{0,2,1:T(8,128)(2,1)}, u32[]{:S(2)}) copy-start(bf16[8192,1,104]{0,2,1:T(8,128)(2,1)} %param.7) | copy-start | bytes 5111812
  6.6 142.9 %all-gather.5.cloned.1.call-start = ((), (), s32[]{:S(2)}) async-start(), calls=%async_computation.3 | async-start | bytes 3932160 | tf_op jit(solution)/shard_map/all_gather | solution.py:14
  96.2 224.2 %all-gather.7.cloned.1.call-start = ((), (), s32[]{:S(2)}) async-start(), calls=%async_computation.4 | async-start | bytes 10543104 | tf_op jit(solution)/shard_map/all_gather | solution.py:37
  165.9 1.5 copy-start.1
  167.3 15.6 %copy-start.3 = (s32[3]{0:T(128)S(1)}, s32[3]{0:T(128)}, u32[]{:S(2)}) copy-start(s32[3]{0:T(128)} %param.6) | copy-start | bytes 40
  320.3 8.9 %copy-start.2 = (bf16[1,13312,64]{1,2,0:T(8,128)(2,1)S(1)}, bf16[1,13312,64]{1,2,0:T(8,128)(2,1)}, u32[]{:S(2)}) copy-start(bf16[1,13312,64]{1,2,0:T(8,128)(2,1)} %param.9) | copy-start | bytes 5111812
Sparse Core Ops, SparseCore 0:
  96.3 53.1 all-gather.4
  179.1 141.1 all-gather.6
where the time goes:
time: 414 us; the launch traced here: 413 us
  blocking collectives  213 us (51%)
  waiting for transfers between devices  150 us (36%)
  local copies, waits for them, and re-layouts  24.7 us (6%)
  between operations  14.8 us (4%)
  matrix products  8.6 us (2%)
    all_gather x1, waiting for transfers between devices, all_blocks(): blocks = lax.all_gather(blocks, axes[k], axis=0, tiled=True)  96.5 us
    all_gather x1, blocking collectives, gather_axes(): shard = lax.all_gather(shard, axis, axis=dim, tiled=True)  88.2 us
    all_gather x1, waiting for transfers between devices, gather_axes(): shard = lax.all_gather(shard, axis, axis=dim, tiled=True)  53.2 us
    all_to_all x1, blocking collectives, local(): lax.all_to_all(placed, GX, split_axis=0, concat_axis=1, tiled=True)  45.1 us
    unnamed x2, blocking collectives  39.5 us
    all_to_all x1, blocking collectives, summed_on_arrival(): lax.all_to_all(cut_along(shard, dim, count), axis, 0, 0, tiled=True)  21.4 us
    all_gather x1, blocking collectives, all_blocks(): blocks = lax.all_gather(blocks, axes[k], axis=0, tiled=True)  9.68 us
    all_to_all x1, blocking collectives, from_everyone(): return lax.all_to_all(copies, axis, split_axis=0, concat_axis=0, tiled=True)  9.27 us
  transfers between devices with their start and end apart: 2, of which 2 were waited for; matrix products, arithmetic and copies ran while one was open for 1% of the time, Pallas kernels for 0%

commit v1 on v0

v1 whole, which is shorter than its diff:
```python
import functools

import jax
import jax.numpy as jnp
from jax import lax
from jax.experimental import pallas as pl
from jax.sharding import Mesh
from jax.sharding import PartitionSpec as P

PREFILL = 320
X, ZO, ZI = 4, 8, 4
GX = ("x", "zo", "zi")
REP_GX = ("rep", "x", "zo", "zi")
LANES = 128
STEPS = (0, 1, 3, 2)
F32 = jnp.float32
BF16 = jnp.bfloat16


def shifted(value, axis, by):
    count = lax.axis_size(axis)
    return lax.ppermute(value, axis, [(i, (i + by) % count) for i in range(count)])


def exchanged(blocks, axes):
    return lax.all_to_all(blocks, axes, split_axis=0, concat_axis=0, tiled=True)


def cut_kernel(depth, rows_ref, out_ref):
    for zi in range(ZI):
        pieces = [
            rows_ref[:, (zo * ZI + zi) * depth : (zo * ZI + zi + 1) * depth] for zo in range(ZO)
        ]
        out_ref[0, zi] = jnp.concatenate(pieces, axis=1)


def cut_rows(down):
    features, rows = down.shape
    depth = rows // (X * ZO * ZI)
    return pl.pallas_call(
        functools.partial(cut_kernel, depth),
        grid=(X,),
        in_specs=[pl.BlockSpec((features, rows // X), lambda i: (0, i))],
        out_specs=pl.BlockSpec((1, ZI, features, ZO * depth), lambda i: (i, 0, 0, 0)),
        out_shape=jax.ShapeDtypeStruct((X, ZI, features, ZO * depth), down.dtype),
        name="cut_rows",
    )(down)


def place_kernel(kinds_ref, order_ref, order_row_ref, slot_ref, place_ref):
    kinds = kinds_ref[...].astype(F32)
    order = order_ref[...]
    earlier = (order_row_ref[...] < order[:, :1]).astype(BF16)
    decode_before = jnp.dot(earlier, kinds.astype(BF16), preferred_element_type=F32)
    target = jnp.where(kinds > 0.5, PREFILL + decode_before, order - decode_before)
    place_ref[...] = (target[:, :1] == slot_ref[...]).astype(BF16)


def placement(kinds, x, own_tokens):
    count = kinds.shape[0]
    chunk = count // X
    k = jnp.arange(count) // chunk
    steps = jnp.array(STEPS, jnp.int32)[k]
    order = (((x - steps) % X) * chunk + jnp.arange(count) % chunk).astype(F32)
    slot = jnp.arange(count).reshape(X, ZO, ZI, own_tokens).transpose(0, 2, 1, 3).reshape(1, count)
    return pl.pallas_call(
        place_kernel,
        out_shape=jax.ShapeDtypeStruct((count, count), BF16),
        name="placement",
    )(kinds, jnp.broadcast_to(order[:, None], (count, LANES)), order[None], slot.astype(F32))


def hidden_kernel(own_ref, other_ref, place_ref, out_ref):
    value = own_ref[...] + other_ref[...]
    width = value.shape[1] // 2
    gate_value, up_value = value[:, :width], value[:, width:]
    hidden = gate_value / (1 + jnp.exp(-gate_value)) * up_value
    placed = jnp.dot(hidden.T.astype(BF16), place_ref[...], preferred_element_type=F32)
    out_ref[...] = placed.astype(BF16)


def placed_hidden(own_value, other_value, place):
    width = own_value.shape[1] // 2
    return pl.pallas_call(
        hidden_kernel,
        out_shape=jax.ShapeDtypeStruct((width, place.shape[1]), BF16),
        name="placed_hidden",
    )(own_value, other_value, place)


def local(tokens, segment_ids, gate_weight, up_weight, down_weight):
    x, gy = lax.axis_index("x"), lax.axis_index("gy")
    own_tokens, half = tokens.shape
    group = exchanged(cut_rows(down_weight[0].T).reshape(X * ZI, down_weight.shape[2], -1), ("x", "zi"))

    kinds = jnp.broadcast_to(segment_ids.astype(tokens.dtype)[:, None], (own_tokens, LANES))
    wide = jnp.concatenate([tokens, kinds], 1)
    column = lax.all_gather(wide, ("zo", "zi"), axis=0, tiled=True)
    chunks = [column] + [shifted(column, "x", by) for by in STEPS[1:]]

    gate, up = gate_weight[:, 0].T, up_weight[:, 0].T

    def rows_of(which):
        at = which * half
        return jnp.concatenate([lax.dynamic_slice_in_dim(w, at, half, 1) for w in (gate, up)], 0)

    own_rows = rows_of(gy)
    other_rows = shifted(rows_of(1 - gy), "gy", 1)

    def values(rows):
        return jnp.concatenate(
            [
                lax.dot_general(chunk[:, :half], rows, (((1,), (1,)), ((), ())), preferred_element_type=F32)
                for chunk in chunks
            ],
            0,
        )

    other_value = shifted(values(other_rows), "gy", 1)
    own_value = values(own_rows)
    place = placement(jnp.concatenate([chunk[:, half:] for chunk in chunks], 0), x, own_tokens)
    placed = placed_hidden(own_value, other_value, place)

    gathered = lax.all_gather(placed, "zo", axis=0, tiled=True)
    features = group.shape[0] * group.shape[1]
    partial = lax.dot_general(
        gathered, group.reshape(features, -1), (((0,), (1,)), ((), ())), preferred_element_type=F32
    )
    slots = partial.shape[0]
    own_half, other_half = (
        lax.dynamic_slice_in_dim(partial, k * (features // 2), features // 2, 1) for k in (gy, 1 - gy)
    )
    summed = (own_half + shifted(other_half, "gy", 1)).astype(BF16)
    arrived = exchanged(summed.reshape(X * ZI, slots // (X * ZI), -1), ("x", "zi"))
    reduced = jnp.sum(arrived.astype(F32), axis=0).astype(BF16)
    owned = exchanged(reduced.reshape(ZO, own_tokens, -1), "zo")
    owned = owned.reshape(ZO, own_tokens, X // 2, -1).transpose(1, 2, 0, 3)
    return owned.reshape(own_tokens, half)


def solution(mesh):
    torus = Mesh(
        mesh.devices.reshape(mesh.shape["rep"], X, ZO, ZI, mesh.shape["gy"]),
        ("rep", "x", "zo", "zi", "gy"),
    )
    placed = (P(REP_GX, "gy"), P(REP_GX), P(None, "gy", GX), P(None, "gy", GX), P("gy", None, GX))
    return jax.shard_map(
        local, mesh=torus, in_specs=placed, out_specs=P(REP_GX, "gy"), check_vma=False
    )
```

time: 414 us -> 307 us (0.74)
  waiting for transfers between devices: 150 us -> 12.6 us
  starting transfers between devices: 0.07 us -> 82.4 us
  blocking collectives: 213 us -> 172 us
  local copies, waits for them, and re-layouts: 24.7 us -> 9.09 us
  between operations: 14.8 us -> 0.26 us
  Pallas kernels: 0 us -> 8.52 us
  matrix products: 8.6 us -> 16.6 us
    all_gather x2 -> x0, waiting for transfers between devices: 150 us -> none  [the longest x1 96.5 us: all_blocks(): blocks = lax.all_gather(blocks, axes[k], axis=0, tiled=True)]
    ppermute x0 -> x6, starting transfers between devices: none -> 70.1 us  [shifted(): lax.ppermute(value, axis, [(i, (i + by) % count) for i in range(count)])]
    unnamed x2 -> x0, blocking collectives: 39.5 us -> none
    all_to_all x3 -> x2, blocking collectives: 75.7 us -> 51.8 us  [exchanged(): return lax.all_to_all(blocks, axes, split_axis=0, concat_axis=0, tiled=True)]
    all_gather x2, blocking collectives: 97.8 us -> 120 us  [the longest x1 79.4 us: local(): column = lax.all_gather(wide, ('zo', 'zi'), axis=0, tiled=True)]
    ppermute x0 -> x6, waiting for transfers between devices: none -> 12.5 us  [shifted(): lax.ppermute(value, axis, [(i, (i + by) % count) for i in range(count)])]
    all_to_all x0 -> x1, starting transfers between devices: none -> 12.3 us  [exchanged(): return lax.all_to_all(blocks, axes, split_axis=0, concat_axis=0, tiled=True)]
    transpose x2 -> x1, local copies, waits for them, and re-layouts: 8.97 us -> 0.01 us  [local(): owned = owned.reshape(ZO, own_tokens, X // 2, -1).transpose(1, 2, 0, 3)]
  transfers between devices with their start and end apart: 2 -> 7, of which waited for: 2 -> 4; matrix products, arithmetic and copies ran while one was open for 1% -> 8% of each run, Pallas kernels for 0% -> 1%
where the time goes in v1:
time: 307 us; the launch traced here: 305 us
  blocking collectives  172 us (56%)
  starting transfers between devices  82.4 us (27%)
  matrix products  16.6 us (5%)
  waiting for transfers between devices  12.6 us (4%)
  local copies, waits for them, and re-layouts  9.09 us (3%)
  Pallas kernels  8.52 us (3%)
  other arithmetic  3.65 us (1%)
    all_gather x1, blocking collectives, local(): column = lax.all_gather(wide, ('zo', 'zi'), axis=0, tiled=True)  79.4 us
    ppermute x6, starting transfers between devices, shifted(): lax.ppermute(value, axis, [(i, (i + by) % count) for i in range(count)])  70.1 us
    all_to_all x2, blocking collectives, exchanged(): return lax.all_to_all(blocks, axes, split_axis=0, concat_axis=0, tiled=True)  51.8 us
    all_gather x1, blocking collectives, local(): gathered = lax.all_gather(placed, 'zo', axis=0, tiled=True)  40.6 us
    dot_general x8, matrix products, values(): lax.dot_general(chunk[:, :half], rows, (((1,), (1,)), ((), ())), preferre...  14.1 us
    ppermute x6, waiting for transfers between devices, shifted(): lax.ppermute(value, axis, [(i, (i + by) % count) for i in range(count)])  12.5 us
    all_to_all x1, starting transfers between devices, exchanged(): return lax.all_to_all(blocks, axes, split_axis=0, concat_axis=0, tiled=True)  12.3 us
  transfers between devices with their start and end apart: 7, of which 4 were waited for; matrix products, arithmetic and copies ran while one was open for 8% of the time, Pallas kernels for 1%

profile of v1, /device:TPU:33, one launch (start us, length us, event | category | flops | bytes accessed | tf_op | source)
XLA Modules:
  0.0 304.9 jit_solution(14035422375985039351)
XLA Ops:
  0.0 4.2 %cut_rows.1 = bf16[4,4,64,832]{3,2,1,0:T(8,128)(2,1)} custom-call(bf16[64,13312]{1,0:T(8,128)(2,1)} %bitcast.44), custom_call_target="tpu_custom_call" | custom-call | tf_op jit(solution)/shard_map/cut_rows/pallas_call | solution.py:40
  4.2 12.3 %all-to-all-start = ((bf16[16,64,832]{2,1,0:T(8,128)(2,1)}), bf16[16,64,832]{2,1,0:T(8,128)(2,1)}, u32[]{:S(2)}, u32[]{:S(2)}) async-start(bf16[16,64,832]{2,1,0:T(8,128)(2,1)} %bitcast.43), calls=%async_computation | async-start | bytes 3670016 | tf_op jit(solution)/shard_map/all_to_all | solution.py:26
  16.6 1.4 dynamic-slice_bitcast_fusion
  18.1 1.4 pad_maximum_fusion.1
  19.4 36.1 %collective-permute-start.3 = (bf16[208,4096]{1,0:T(8,128)(2,1)}, bf16[208,4096]{1,0:T(8,128)(2,1)S(1)}, u32[]{:S(2)}, u32[]{:S(2)}) collective-permute-start(bf16[208,4096]{1,0:T(8,128)(2,1)} %pad_maximum_fusion.1), channel_id=1, source_target_pairs={{0,1},{1,0},{2,3},{3,2},{4,5},{5,4},{6,7},{7,6},{8,9},{9,8},{10,11... | collective-permute-start | bytes 5111816 | tf_op jit(solution)/shard_map/ppermute | solution.py:22
  55.5 0.1 broadcast_in_dim.4
  55.6 79.4 %all-gather = bf16[32,3,4224]{2,1,0:T(4,128)(2,1)S(1)} all-gather(bf16[1,3,4224]{2,1,0:T(4,128)(2,1)S(1)} %maximum_bitcast_fusion), channel_id=1, replica_groups=mesh['rep'=2,'x'=4,'zo'=8,'zi'=4,'gy'=2] {'zo','zi'}, dimensions={0}, use_global_device_ids=true | all-gather | bytes 836352 | tf_op jit(solution)/shard_map/all_gather | solution.py:98
  135.0 1.5 reshape.296
  136.5 3.0 collective-permute-start
  139.5 3.5 %collective-permute-start.1 = (bf16[96,4224]{1,0:T(8,128)(2,1)}, bf16[96,4224]{1,0:T(8,128)(2,1)}, u32[]{:S(2)}, u32[]{:S(2)}) collective-permute-start(bf16[96,4224]{1,0:T(8,128)(2,1)} %reshape.296), channel_id=1, source_target_pairs={{0,192},{64,0},{128,64},{192,128},{1,193},{65,1},{129,65},{193,129... | collective-permute-start | bytes 2433032 | tf_op jit(solution)/shard_map/ppermute | solution.py:22
  143.0 3.1 %collective-permute-start.2 = (bf16[96,4224]{1,0:T(8,128)(2,1)}, bf16[96,4224]{1,0:T(8,128)(2,1)}, u32[]{:S(2)}, u32[]{:S(2)}) collective-permute-start(bf16[96,4224]{1,0:T(8,128)(2,1)} %reshape.296), channel_id=1, source_target_pairs={{0,128},{64,192},{128,0},{192,64},{1,129},{65,193},{129,1},{193,65... | collective-permute-start | bytes 2433032 | tf_op jit(solution)/shard_map/ppermute | solution.py:22
  146.2 0.8 slice.45
  146.9 0.8 reshape.270.slot_ref
  147.8 0.6 fusion.27.order_row_ref
  148.4 2.4 fusion.14
  150.8 0.2 collective-permute-done
  151.0 0.7 slice.46
  151.8 7.8 %collective-permute-done.1 = bf16[96,4224]{1,0:T(8,128)(2,1)} collective-permute-done((bf16[96,4224]{1,0:T(8,128)(2,1)}, bf16[96,4224]{1,0:T(8,128)(2,1)}, u32[]{:S(2)}, u32[]{:S(2)}) %collective-permute-start.1) | collective-permute-done | bytes 811040 | tf_op jit(solution)/shard_map/ppermute | solution.py:22
  159.5 0.7 slice.47
  160.3 2.7 collective-permute-done.2
  163.0 0.7 slice.48
  163.7 0.7 pad_maximum_fusion.4.kinds_ref
  164.4 0.8 broadcast_in_dim.5.order_ref
  165.2 2.1 placement.1.place_ref
  167.2 1.8 fusion.10
  169.1 1.8 fusion.6
  170.9 0.0 collective-permute-done.3
  170.9 1.8 fusion.8
  172.7 1.8 fusion.4
  174.5 1.9 fusion
  176.4 0.7 fusion.12
  177.2 18.7 %collective-permute-start.4 = (f32[384,208]{1,0:T(8,128)S(1)}, f32[384,208]{1,0:T(8,128)S(1)}, u32[]{:S(2)}, u32[]{:S(2)}) collective-permute-start(f32[384,208]{1,0:T(8,128)S(1)} %pad_maximum_fusion.3), channel_id=1, source_target_pairs={{0,1},{1,0},{2,3},{3,2},{4,5},{5,4},{6,7},{7,6},{8,9},{9,8},{10,11... | collective-permute-start | bytes 958472 | tf_op jit(solution)/shard_map/ppermute | solution.py:22
  195.9 1.8 fusion.2
  197.7 0.8 pad_maximum_fusion.2.own_ref
  198.5 0.0 collective-permute-done.4.other_ref
  198.5 0.7 copy-done.5
  199.3 2.2 placed_hidden.1
  201.5 40.6 %all_gather.7 = bf16[832,384]{1,0:T(8,128)(2,1)S(1)} all-gather(bf16[104,384]{1,0:T(8,128)(2,1)} %placed_hidden.1), channel_id=1, replica_groups=mesh['rep'=2,'x'=4,'zo'=8,'zi'=4,'gy'=2] {'zo'}, dimensions={0}, use_global_device_ids=true | all-gather | bytes 718848 | tf_op jit(solution)/shard_map/all_gather | solution.py:124
  242.1 0.0 all-to-all-done
  242.1 2.5 fusion.29
  244.6 0.1 constant_dynamic-slice_fusion
  244.7 5.6 %collective-permute-start.5 = (f32[384,512]{1,0:T(8,128)S(1)}, f32[384,512]{1,0:T(8,128)S(1)}, u32[]{:S(2)}, u32[]{:S(2)}) collective-permute-start(f32[384,512]{1,0:T(8,128)S(1)} %constant_dynamic-slice_fusion), channel_id=1, source_target_pairs={{0,1},{1,0},{2,3},{3,2},{4,5},{5,4},{6,7},{7,6},{8,9},{9,8},{10,11... | collective-permute-start | bytes 2359304 | tf_op jit(solution)/shard_map/ppermute | solution.py:22
  250.3 1.9 collective-permute-done.5
  252.2 0.1 add_convert_fusion
  252.3 19.6 %all_to_all.15 = bf16[16,24,512]{2,1,0:T(8,128)(2,1)S(1)} all-to-all(bf16[16,24,512]{2,1,0:T(8,128)(2,1)S(1)} %bitcast.45), channel_id=1, replica_groups=mesh['rep'=2,'x'=4,'zo'=8,'zi'=4,'gy'=2] {'x','zi'}, dimensions={0} | all-to-all | bytes 786432 | tf_op jit(solution)/shard_map/all_to_all | solution.py:26
  271.9 0.1 reduce_sum.12
  272.0 32.2 %all_to_all.16 = bf16[8,3,512]{2,1,0:T(4,128)(2,1)S(1)} all-to-all(bf16[8,3,512]{2,1,0:T(4,128)(2,1)S(1)} %reshape.267), channel_id=1, replica_groups=mesh['rep'=2,'x'=4,'zo'=8,'zi'=4,'gy'=2] {'zo'}, dimensions={0} | all-to-all | bytes 49152 | tf_op jit(solution)/shard_map/all_to_all | solution.py:26
  304.3 0.6 copy.14
  (24 shorter events, 0.2 us)
Async XLA Ops:
  4.2 12.4 %copy-start.1 = (bf16[8192,1,104]{0,2,1:T(8,128)(2,1)S(1)}, bf16[8192,1,104]{0,2,1:T(8,128)(2,1)}, u32[]{:S(2)}) copy-start(bf16[8192,1,104]{0,2,1:T(8,128)(2,1)} %param.9) | copy-start | bytes 5111812
  4.2 12.4 %copy-start.2 = (bf16[8192,1,104]{0,2,1:T(8,128)(2,1)S(1)}, bf16[8192,1,104]{0,2,1:T(8,128)(2,1)}, u32[]{:S(2)}) copy-start(bf16[8192,1,104]{0,2,1:T(8,128)(2,1)} %param.8) | copy-start | bytes 5111812
  4.2 237.9 %all-to-all-start = ((bf16[16,64,832]{2,1,0:T(8,128)(2,1)}), bf16[16,64,832]{2,1,0:T(8,128)(2,1)}, u32[]{:S(2)}, u32[]{:S(2)}) async-start(bf16[16,64,832]{2,1,0:T(8,128)(2,1)} %bitcast.43), calls=%async_computation | async-start | bytes 3670016 | tf_op jit(solution)/shard_map/all_to_all | solution.py:26
  18.1 37.5 %copy-start.7 = (s32[3]{0:T(128)S(1)}, s32[3]{0:T(128)}, u32[]{:S(2)}) copy-start(s32[3]{0:T(128)} %param.7) | copy-start | bytes 40
  18.1 37.6 %copy-start.6 = (bf16[3,4096]{1,0:T(4,128)(2,1)S(1)}, bf16[3,4096]{1,0:T(4,128)(2,1)}, u32[]{:S(2)}) copy-start(bf16[3,4096]{1,0:T(4,128)(2,1)} %param.6) | copy-start | bytes 73732
  19.4 151.5 %collective-permute-start.3 = (bf16[208,4096]{1,0:T(8,128)(2,1)}, bf16[208,4096]{1,0:T(8,128)(2,1)S(1)}, u32[]{:S(2)}, u32[]{:S(2)}) collective-permute-start(bf16[208,4096]{1,0:T(8,128)(2,1)} %pad_maximum_fusion.1), channel_id=1, source_target_pairs={{0,1},{1,0},{2,3},{3,2},{4,5},{5,4},{6,7},{7,6},{8,9},{9,8},{10,11... | collective-permute-start | bytes 5111816 | tf_op jit(solution)/shard_map/ppermute | solution.py:22
  136.5 14.5 %collective-permute-start = (bf16[96,4224]{1,0:T(8,128)(2,1)}, bf16[96,4224]{1,0:T(8,128)(2,1)}, u32[]{:S(2)}, u32[]{:S(2)}) collective-permute-start(bf16[96,4224]{1,0:T(8,128)(2,1)} %reshape.296), channel_id=1, source_target_pairs={{0,64},{64,128},{128,192},{192,0},{1,65},{65,129},{129,193},{193,1... | collective-permute-start | bytes 2433032 | tf_op jit(solution)/shard_map/ppermute | solution.py:22
  139.5 20.1 %collective-permute-start.1 = (bf16[96,4224]{1,0:T(8,128)(2,1)}, bf16[96,4224]{1,0:T(8,128)(2,1)}, u32[]{:S(2)}, u32[]{:S(2)}) collective-permute-start(bf16[96,4224]{1,0:T(8,128)(2,1)} %reshape.296), channel_id=1, source_target_pairs={{0,192},{64,0},{128,64},{192,128},{1,193},{65,1},{129,65},{193,129... | collective-permute-start | bytes 2433032 | tf_op jit(solution)/shard_map/ppermute | solution.py:22
  143.0 19.9 %collective-permute-start.2 = (bf16[96,4224]{1,0:T(8,128)(2,1)}, bf16[96,4224]{1,0:T(8,128)(2,1)}, u32[]{:S(2)}, u32[]{:S(2)}) collective-permute-start(bf16[96,4224]{1,0:T(8,128)(2,1)} %reshape.296), channel_id=1, source_target_pairs={{0,128},{64,192},{128,0},{192,64},{1,129},{65,193},{129,1},{193,65... | collective-permute-start | bytes 2433032 | tf_op jit(solution)/shard_map/ppermute | solution.py:22
  148.4 18.9 %copy-start.3 = (bf16[104,4096]{1,0:T(8,128)(2,1)S(1)}, bf16[104,4096]{1,0:T(8,128)(2,1)}, u32[]{:S(2)}) copy-start(bf16[104,4096]{1,0:T(8,128)(2,1)} %get-tuple-element.8) | copy-start | bytes 2555908
  148.4 18.9 %copy-start.4 = (bf16[104,4096]{1,0:T(8,128)(2,1)S(1)}, bf16[104,4096]{1,0:T(8,128)(2,1)}, u32[]{:S(2)}) copy-start(bf16[104,4096]{1,0:T(8,128)(2,1)} %get-tuple-element.9) | copy-start | bytes 2555908
  174.5 1.9 copy-start
  177.2 21.3 %collective-permute-start.4 = (f32[384,208]{1,0:T(8,128)S(1)}, f32[384,208]{1,0:T(8,128)S(1)}, u32[]{:S(2)}, u32[]{:S(2)}) collective-permute-start(f32[384,208]{1,0:T(8,128)S(1)} %pad_maximum_fusion.3), channel_id=1, source_target_pairs={{0,1},{1,0},{2,3},{3,2},{4,5},{5,4},{6,7},{7,6},{8,9},{9,8},{10,11... | collective-permute-start | bytes 958472 | tf_op jit(solution)/shard_map/ppermute | solution.py:22
  198.5 0.8 copy-start.5
  244.7 7.5 %collective-permute-start.5 = (f32[384,512]{1,0:T(8,128)S(1)}, f32[384,512]{1,0:T(8,128)S(1)}, u32[]{:S(2)}, u32[]{:S(2)}) collective-permute-start(f32[384,512]{1,0:T(8,128)S(1)} %constant_dynamic-slice_fusion), channel_id=1, source_target_pairs={{0,1},{1,0},{2,3},{3,2},{4,5},{5,4},{6,7},{7,6},{8,9},{9,8},{10,11... | collective-permute-start | bytes 2359304 | tf_op jit(solution)/shard_map/ppermute | solution.py:22

commit v2 on v1

v2 whole, which is shorter than its diff:
```python
import functools

import jax
import jax.numpy as jnp
from jax import lax
from jax.experimental import pallas as pl
from jax.experimental.pallas import tpu as pltpu
from jax.sharding import Mesh
from jax.sharding import PartitionSpec as P


PREFILL = 320
X, ZO, ZI = 4, 8, 4
GX = ("x", "zo", "zi")
REP_GX = ("rep", "x", "zo", "zi")
LANES = 128
STEPS = (0, 1, 3, 2)
F32 = jnp.float32
BF16 = jnp.bfloat16


def shifted(value, axis, by):
    count = lax.axis_size(axis)
    return lax.ppermute(value, axis, [(i, (i + by) % count) for i in range(count)])


def exchanged(blocks, axes):
    return lax.all_to_all(blocks, axes, split_axis=0, concat_axis=0, tiled=True)


def copy_kernel(rows_ref, out_ref):
    out_ref[0] = rows_ref[...]


def cut_by_x(down):
    features, rows = down.shape
    return pl.pallas_call(
        copy_kernel,
        grid=(X,),
        in_specs=[pl.BlockSpec((features, rows // X), lambda i: (0, i))],
        out_specs=pl.BlockSpec((1, features, rows // X), lambda i: (i, 0, 0)),
        out_shape=jax.ShapeDtypeStruct((X, features, rows // X), down.dtype),
        name="cut_by_x",
    )(down)


def cut_kernel(depth, gy_ref, rows_ref, out_ref):
    for zi in range(ZI):
        pieces = [rows_ref[0, :, (zo * ZI + zi) * depth : (zo * ZI + zi + 1) * depth] for zo in range(ZO)]
        out_ref[zi, 0] = jnp.concatenate(pieces, axis=1)


def cut_by_zi(blocks, gy):
    count, features, rows = blocks.shape
    depth = rows // (ZO * ZI)
    return pl.pallas_call(
        functools.partial(cut_kernel, depth),
        grid_spec=pltpu.PrefetchScalarGridSpec(
            num_scalar_prefetch=1,
            grid=(count,),
            in_specs=[
                pl.BlockSpec((1, features, rows), lambda i, gy: (lax.rem(i + gy[0] * (X // 2), X), 0, 0))
            ],
            out_specs=pl.BlockSpec((ZI, 1, features, ZO * depth), lambda i, gy: (0, i, 0, 0)),
        ),
        out_shape=jax.ShapeDtypeStruct((ZI, count, features, ZO * depth), blocks.dtype),
        name="cut_by_zi",
    )(gy, blocks)


def values_kernel(chunk_ref, own_rows_ref, other_rows_ref, own_ref, other_ref):
    chunk = chunk_ref[...]
    for rows, out in ((other_rows_ref, other_ref), (own_rows_ref, own_ref)):
        out[...] = lax.dot_general(chunk, rows[...], (((1,), (1,)), ((), ())), preferred_element_type=F32)


def values(chunk, own_rows, other_rows):
    count, (columns, half) = chunk.shape[0], own_rows.shape
    out = jax.ShapeDtypeStruct((count, columns), F32)
    whole = pl.BlockSpec((columns, half), lambda i: (0, 0))
    out_spec = pl.BlockSpec((count, columns), lambda i: (0, 0))
    return pl.pallas_call(
        values_kernel,
        grid=(1,),
        in_specs=[pl.BlockSpec((count, half), lambda i: (0, 0)), whole, whole],
        out_specs=[out_spec, out_spec],
        out_shape=[out, out],
        name="values",
    )(chunk, own_rows, other_rows)


def place_kernel(*refs):
    *kinds_refs, order_ref, order_row_ref, slot_ref, place_ref = refs
    kinds = jnp.concatenate([ref[...] for ref in kinds_refs], 0)
    order = order_ref[...]
    earlier = (order_row_ref[...] < order[:, :1]).astype(BF16)
    decode_before = jnp.dot(earlier, kinds, preferred_element_type=F32)
    target = jnp.where(kinds.astype(F32) > 0.5, PREFILL + decode_before, order - decode_before)
    place_ref[...] = (target[:, :1] == slot_ref[...]).astype(BF16)


def token_order(x, chunk):
    count = X * chunk
    steps = jnp.array(STEPS, jnp.int32)[jnp.arange(count) // chunk]
    order = (((x - steps) % X) * chunk + jnp.arange(count) % chunk).astype(F32)
    return jnp.broadcast_to(order[:, None], (count, LANES)), order[None]


def placement(chunks, half, order, order_row, own_tokens):
    chunk = chunks[0].shape[0]
    count = X * chunk
    slot = jnp.arange(count).reshape(X, ZO, ZI, own_tokens).transpose(0, 2, 1, 3).reshape(1, count)
    kinds = pl.BlockSpec((chunk, LANES), lambda i: (0, half // LANES))
    one_row = pl.BlockSpec((1, count), lambda i: (0, 0))
    return pl.pallas_call(
        place_kernel,
        grid=(1,),
        in_specs=[kinds] * X + [pl.BlockSpec((count, LANES), lambda i: (0, 0)), one_row, one_row],
        out_specs=pl.BlockSpec((count, count), lambda i: (0, 0)),
        out_shape=jax.ShapeDtypeStruct((count, count), BF16),
        name="placement",
    )(*chunks, order, order_row, slot.astype(F32))


def hidden_kernel(*refs):
    *own_refs, other_ref, place_ref, out_ref = refs
    value = jnp.concatenate([ref[...] for ref in own_refs], 0) + other_ref[...]
    width = value.shape[1] // 2
    gate_value, up_value = value[:, :width], value[:, width:]
    hidden = gate_value / (1 + jnp.exp(-gate_value)) * up_value
    placed = jnp.dot(hidden.T.astype(BF16), place_ref[...], preferred_element_type=F32)
    out_ref[...] = placed.astype(BF16)


def placed_hidden(own_values, other_value, place):
    width = other_value.shape[1] // 2
    return pl.pallas_call(
        hidden_kernel,
        out_shape=jax.ShapeDtypeStruct((width, place.shape[1]), BF16),
        name="placed_hidden",
    )(*own_values, other_value, place)


def block(tokens, segment_ids, gate_weight, up_weight, down_weight):
    x, gy = lax.axis_index("x"), lax.axis_index("gy")
    own_tokens, half = tokens.shape
    down = exchanged(cut_by_x(down_weight[0].T), "x")

    kinds = jnp.broadcast_to(segment_ids.astype(tokens.dtype)[:, None], (own_tokens, LANES))
    wide = jnp.concatenate([tokens, kinds], 1)
    order, order_row = token_order(x, own_tokens * ZO * ZI)
    column = lax.all_gather(wide, ("zo", "zi"), axis=0, tiled=True)
    column, gate, up = lax.optimization_barrier((column, gate_weight, up_weight))
    gate, up = gate[:, 0].T, up[:, 0].T
    chunks = [column]
    for by in STEPS[1:]:
        chunks.append(shifted(column, "x", by))

    group = cut_by_zi(down, gy.reshape(1))
    group = exchanged(group, "zi")

    def rows_of(which):
        at = which * half
        return jnp.concatenate([lax.dynamic_slice_in_dim(w, at, half, 1) for w in (gate, up)], 0)

    own_rows = rows_of(gy)
    other_rows = shifted(rows_of(1 - gy), "gy", 1)

    own_values, other_values = [], []
    for by, chunk in zip(STEPS, chunks, strict=True):
        own_value, other_value = values(chunk, own_rows, other_rows)
        own_values.append(own_value)
        other_values.append(other_value)
    other_value = shifted(jnp.concatenate(other_values, 0), "gy", 1)
    place = placement(chunks, half, order, order_row, own_tokens)
    placed = placed_hidden(own_values, other_value, place)

    gathered = lax.all_gather(placed, "zo", axis=0, tiled=True)

    depth = group.shape[3]
    partial = lax.dot_general(
        gathered, group.reshape(-1, depth), (((0,), (1,)), ((), ())), preferred_element_type=F32
    )
    width = partial.shape[1] // (2 * ZI)

    def half_of(which):
        return jnp.concatenate(
            [partial[:, (2 * k + which) * width : (2 * k + which + 1) * width] for k in range(ZI)], 1
        )

    other_half = shifted(half_of(1), "gy", 1)
    summed = (half_of(0) + other_half).astype(BF16)
    slots = summed.shape[0]
    arrived = exchanged(summed.reshape(X * ZI, slots // (X * ZI), -1), ("x", "zi"))
    reduced = jnp.sum(arrived.astype(F32), axis=0).astype(BF16)
    owned = exchanged(reduced.reshape(ZO, own_tokens, -1), "zo")
    owned = owned.reshape(ZO, own_tokens, ZI, X // 2, -1).transpose(1, 3, 0, 2, 4)
    return owned.reshape(own_tokens, half)


def solution(mesh):
    torus = Mesh(
        mesh.devices.reshape(mesh.shape["rep"], X, ZO, ZI, mesh.shape["gy"]),
        ("rep", "x", "zo", "zi", "gy"),
    )
    placed = (P(REP_GX, "gy"), P(REP_GX), P(None, "gy", GX), P(None, "gy", GX), P("gy", None, GX))
    return jax.shard_map(block, mesh=torus, in_specs=placed, out_specs=P(REP_GX, "gy"), check_vma=False)
```

time: 307 us -> 346 us (1.13)
  blocking collectives: 172 us -> 210 us
  starting transfers between devices: 82.4 us -> 52.9 us
  waiting for transfers between devices: 12.6 us -> 33 us
  Pallas kernels: 8.52 us -> 28.5 us
  matrix products: 16.6 us -> 2.53 us
    all_gather x2, blocking collectives: 120 us -> 160 us  [the longest x1 118 us: block(): column = lax.all_gather(wide, ('zo', 'zi'), axis=0, tiled=True)]
    ppermute x6, starting transfers between devices: 70.1 us -> 31.4 us  [shifted(): lax.ppermute(value, axis, [(i, (i + by) % count) for i in range(count)])]
    pallas_call x2 -> x7, Pallas kernels: 6.3 us -> 26.2 us  [the longest x4 16.3 us: values(): pl.pallas_call(values_kernel, grid=(1,), in_specs=[pl.BlockSpec((count, h...]
    dot_general x9 -> x1, matrix products: 16.6 us -> 2.53 us  [block(): lax.dot_general(gathered, group.reshape(-1, depth), (((0,), (1,)), ((), (...]
    all_to_all x1 -> x2, waiting for transfers between devices: 0.01 us -> 13.3 us  [exchanged(): return lax.all_to_all(blocks, axes, split_axis=0, concat_axis=0, tiled=True)]
    all_to_all x1 -> x2, starting transfers between devices: 12.3 us -> 21.5 us  [exchanged(): return lax.all_to_all(blocks, axes, split_axis=0, concat_axis=0, tiled=True)]
    ppermute x6, waiting for transfers between devices: 12.5 us -> 19.7 us  [shifted(): lax.ppermute(value, axis, [(i, (i + by) % count) for i in range(count)])]
  transfers between devices with their start and end apart: 7 -> 8, of which waited for: 4 -> 4; matrix products, arithmetic and copies ran while one was open for 8% -> 3% of each run, Pallas kernels for 1% -> 6%
where the time goes in v2:
time: 346 us; the launch traced here: 343 us
  blocking collectives  210 us (61%)
  starting transfers between devices  52.9 us (15%)
  waiting for transfers between devices  33 us (10%)
  Pallas kernels  28.5 us (8%)
  local copies, waits for them, and re-layouts  10.1 us (3%)
  other arithmetic  5.7 us (2%)
    all_gather x1, blocking collectives, block(): column = lax.all_gather(wide, ('zo', 'zi'), axis=0, tiled=True)  118 us
    all_to_all x2, blocking collectives, exchanged(): return lax.all_to_all(blocks, axes, split_axis=0, concat_axis=0, tiled=True)  50.1 us
    all_gather x1, blocking collectives, block(): gathered = lax.all_gather(placed, 'zo', axis=0, tiled=True)  41.9 us
    ppermute x6, starting transfers between devices, shifted(): lax.ppermute(value, axis, [(i, (i + by) % count) for i in range(count)])  31.4 us
    all_to_all x2, starting transfers between devices, exchanged(): return lax.all_to_all(blocks, axes, split_axis=0, concat_axis=0, tiled=True)  21.5 us
    ppermute x6, waiting for transfers between devices, shifted(): lax.ppermute(value, axis, [(i, (i + by) % count) for i in range(count)])  19.7 us
    pallas_call x4, Pallas kernels, values(): pl.pallas_call(values_kernel, grid=(1,), in_specs=[pl.BlockSpec((count, h...  16.3 us
    all_to_all x2, waiting for transfers between devices, exchanged(): return lax.all_to_all(blocks, axes, split_axis=0, concat_axis=0, tiled=True)  13.3 us
  transfers between devices with their start and end apart: 8, of which 4 were waited for; matrix products, arithmetic and copies ran while one was open for 3% of the time, Pallas kernels for 6%

profile of v2, /device:TPU:33, one launch (start us, length us, event | category | flops | bytes accessed | tf_op | source)
XLA Modules:
  0.0 343.3 jit_solution(10179022352036287305)
XLA Ops:
  0.0 3.6 %cut_by_x.1 = bf16[4,64,3328]{2,1,0:T(8,128)(2,1)} custom-call(bf16[64,13312]{1,0:T(8,128)(2,1)} %bitcast.35), custom_call_target="tpu_custom_call" | custom-call | tf_op jit(solution)/shard_map/cut_by_x/pallas_call | solution.py:37
  3.6 5.1 %all-to-all-start = ((bf16[4,64,3328]{2,1,0:T(8,128)(2,1)}), bf16[4,64,3328]{2,1,0:T(8,128)(2,1)S(1)}, u32[]{:S(2)}, u32[]{:S(2)}) async-start(bf16[4,64,3328]{2,1,0:T(8,128)(2,1)} %cut_by_x.1), calls=%async_computation | async-start | bytes 3407872 | tf_op jit(solution)/shard_map/all_to_all | solution.py:28
  8.7 13.3 %all-to-all-done.rows_ref = bf16[4,64,3328]{2,1,0:T(8,128)(2,1)S(1)} async-done(((bf16[4,64,3328]{2,1,0:T(8,128)(2,1)}), bf16[4,64,3328]{2,1,0:T(8,128)(2,1)S(1)}, u32[]{:S(2)}, u32[]{:S(2)}) %all-to-all-start) | async-done | bytes 1703968 | tf_op jit(solution)/shard_map/all_to_all | solution.py:28
  22.0 1.2 copy-done.2
  23.2 4.2 %cut_by_zi.1 = bf16[4,4,64,832]{3,2,1,0:T(8,128)(2,1)} custom-call(s32[1]{0:T(128)} %bitcast.10.gy_ref, bf16[4,64,3328]{2,1,0:T(8,128)(2,1)} %copy-done.2), custom_call_target="tpu_custom_call" | custom-call | tf_op jit(solution)/shard_map/cut_by_zi/pallas_call | solution.py:56
  27.4 16.4 %all-to-all-start.1 = ((bf16[4,4,64,832]{3,2,1,0:T(8,128)(2,1)}), bf16[4,4,64,832]{3,2,1,0:T(8,128)(2,1)}, u32[]{:S(2)}, u32[]{:S(2)}) async-start(bf16[4,4,64,832]{3,2,1,0:T(8,128)(2,1)} %cut_by_zi.1), calls=%async_computation.1 | async-start | bytes 3670016 | tf_op jit(solution)/shard_map/all_to_all | solution.py:28
  43.8 0.1 broadcast_in_dim.4
  43.9 0.0 copy-done.7
  43.9 118.4 %all-gather = bf16[32,3,4224]{2,1,0:T(4,128)(2,1)S(1)} all-gather(bf16[1,3,4224]{2,1,0:T(4,128)(2,1)S(1)} %maximum_bitcast_fusion), channel_id=1, replica_groups=mesh['rep'=2,'x'=4,'zo'=8,'zi'=4,'gy'=2] {'zo','zi'}, dimensions={0}, use_global_device_ids=true | all-gather | bytes 836352 | tf_op jit(solution)/shard_map/all_gather | solution.py:152
  162.3 0.7 reshape.296.chunk_ref.refs_0_
  163.0 3.5 %dynamic-slice_bitcast_fusion = (bf16[104,4096]{1,0:T(8,128)(2,1)S(1)}, bf16[104,4096]{1,0:T(8,128)(2,1)S(1)}, bf16[104,4096]{1,0:T(8,128)(2,1)}, bf16[104,4096]{1,0:T(8,128)(2,1)S(1)}) fusion(bf16[8192,1,104]{0,2,1:T(8,128)(2,1)} %param.9, s32[]{:T(128)S(6)} %select_n.68, s32[]{:T(128)S(6)} %select_n.67, bf16[8192,1,104]{0,2,1:T(8,128)(2,1)} %param.8), kind=kLoop, calls=%fused_computation.2 | loop fusion | bytes 6815752 | tf_op jit(solution)/shard_map/dynamic_slice | solution.py:164
  166.5 1.4 pad_maximum_fusion.1
  167.9 16.2 %collective-permute-start = (bf16[208,4096]{1,0:T(8,128)(2,1)}, bf16[208,4096]{1,0:T(8,128)(2,1)S(1)}, u32[]{:S(2)}, u32[]{:S(2)}) collective-permute-start(bf16[208,4096]{1,0:T(8,128)(2,1)} %pad_maximum_fusion.1), channel_id=1, source_target_pairs={{0,1},{1,0},{2,3},{3,2},{4,5},{5,4},{6,7},{7,6},{8,9},{9,8},{10,11... | collective-permute-start | bytes 5111816 | tf_op jit(solution)/shard_map/ppermute | solution.py:24
  184.1 2.3 collective-permute-start.3
  186.4 4.3 %collective-permute-start.2 = (bf16[96,4224]{1,0:T(8,128)(2,1)S(1)}, bf16[96,4224]{1,0:T(8,128)(2,1)}, u32[]{:S(2)}, u32[]{:S(2)}) collective-permute-start(bf16[96,4224]{1,0:T(8,128)(2,1)S(1)} %reshape.296.chunk_ref.refs_0_), channel_id=1, source_target_pairs={{0,192},{64,0},{128,64},{192,128},{1,193},{65,1},{129,65},{193,129... | collective-permute-start | bytes 2433032 | tf_op jit(solution)/shard_map/ppermute | solution.py:24
  190.7 2.0 collective-permute-start.1
  192.7 0.8 reshape.270.refs_6_
  193.5 2.5 pad_maximum_fusion.own_rows_ref
  196.0 0.0 collective-permute-done.other_rows_ref
  196.0 1.2 copy-done
  197.3 4.1 %values.4 = (f32[96,208]{1,0:T(8,128)}, f32[96,208]{1,0:T(8,128)}) custom-call(bf16[96,4224]{1,0:T(8,128)(2,1)} %copy-done.1, bf16[208,4096]{1,0:T(8,128)(2,1)} %pad_maximum_fusion.own_rows_ref, bf16[208,4096]{1,0:T(8,128)(2,1)} %copy-done), custom_call_target="tpu_custom_call" | custom-call | tf_op jit(solution)/shard_map/values/pallas_call | solution.py:82
  201.3 6.0 %collective-permute-done.3.chunk_ref.refs_3_ = bf16[96,4224]{1,0:T(8,128)(2,1)} collective-permute-done((bf16[96,4224]{1,0:T(8,128)(2,1)S(1)}, bf16[96,4224]{1,0:T(8,128)(2,1)}, u32[]{:S(2)}, u32[]{:S(2)}) %collective-permute-start.3) | collective-permute-done | bytes 811040 | tf_op jit(solution)/shard_map/ppermute | solution.py:24
  207.3 4.1 %values.7 = (f32[96,208]{1,0:T(8,128)}, f32[96,208]{1,0:T(8,128)}) custom-call(bf16[96,4224]{1,0:T(8,128)(2,1)} %collective-permute-done.3.chunk_ref.refs_3_, bf16[208,4096]{1,0:T(8,128)(2,1)} %pad_maximum_fusion.own_rows_ref, bf16[208,4096]{1,0:T(8,128)(2,1)} %copy-done), custom_call_target="tpu_custom_call" | custom-call | tf_op jit(solution)/shard_map/values/pallas_call | solution.py:82
  211.4 11.8 %collective-permute-done.2.chunk_ref.refs_2_ = bf16[96,4224]{1,0:T(8,128)(2,1)} collective-permute-done((bf16[96,4224]{1,0:T(8,128)(2,1)S(1)}, bf16[96,4224]{1,0:T(8,128)(2,1)}, u32[]{:S(2)}, u32[]{:S(2)}) %collective-permute-start.2) | collective-permute-done | bytes 811040 | tf_op jit(solution)/shard_map/ppermute | solution.py:24
  223.2 4.1 %values.6 = (f32[96,208]{1,0:T(8,128)}, f32[96,208]{1,0:T(8,128)}) custom-call(bf16[96,4224]{1,0:T(8,128)(2,1)} %collective-permute-done.2.chunk_ref.refs_2_, bf16[208,4096]{1,0:T(8,128)(2,1)} %pad_maximum_fusion.own_rows_ref, bf16[208,4096]{1,0:T(8,128)(2,1)} %copy-done), custom_call_target="tpu_custom_call" | custom-call | tf_op jit(solution)/shard_map/values/pallas_call | solution.py:82
  227.3 0.0 collective-permute-done.1.chunk_ref.refs_1_
  227.3 4.1 %values.5 = (f32[96,208]{1,0:T(8,128)}, f32[96,208]{1,0:T(8,128)}) custom-call(bf16[96,4224]{1,0:T(8,128)(2,1)} %collective-permute-done.1.chunk_ref.refs_1_, bf16[208,4096]{1,0:T(8,128)(2,1)} %pad_maximum_fusion.own_rows_ref, bf16[208,4096]{1,0:T(8,128)(2,1)} %copy-done), custom_call_target="tpu_custom_call" | custom-call | tf_op jit(solution)/shard_map/values/pallas_call | solution.py:82
  231.4 0.9 pad_maximum_fusion.3
  232.4 2.8 collective-permute-start.4
  235.2 0.6 fusion.12.refs_5_
  235.8 0.8 broadcast_in_dim.5.refs_4_
  236.6 2.1 placement.1.refs_5_
  238.7 0.0 collective-permute-done.4.refs_4_
  238.7 0.8 copy-done.3
  239.5 2.3 placed_hidden.1
  241.7 41.9 %all_gather.7 = bf16[832,384]{1,0:T(8,128)(2,1)S(1)} all-gather(bf16[104,384]{1,0:T(8,128)(2,1)} %placed_hidden.1), channel_id=1, replica_groups=mesh['rep'=2,'x'=4,'zo'=8,'zi'=4,'gy'=2] {'zo'}, dimensions={0}, use_global_device_ids=true | all-gather | bytes 718848 | tf_op jit(solution)/shard_map/all_gather | solution.py:178
  283.7 0.0 all-to-all-done.1
  283.7 2.5 fusion.15
  286.2 0.1 fusion.14
  286.3 0.1 pad_maximum_fusion.2
  286.4 3.8 %collective-permute-start.5 = (f32[384,512]{1,0:T(8,128)S(1)}, f32[384,512]{1,0:T(8,128)S(1)}, u32[]{:S(2)}, u32[]{:S(2)}) collective-permute-start(f32[384,512]{1,0:T(8,128)S(1)} %pad_maximum_fusion.2), channel_id=1, source_target_pairs={{0,1},{1,0},{2,3},{3,2},{4,5},{5,4},{6,7},{7,6},{8,9},{9,8},{10,11... | collective-permute-start | bytes 2359304 | tf_op jit(solution)/shard_map/ppermute | solution.py:24
  290.2 1.9 collective-permute-done.5
  292.1 0.1 fusion
  292.2 16.9 %all_to_all.20 = bf16[16,24,512]{2,1,0:T(8,128)(2,1)S(1)} all-to-all(bf16[16,24,512]{2,1,0:T(8,128)(2,1)S(1)} %bitcast.36), channel_id=1, replica_groups=mesh['rep'=2,'x'=4,'zo'=8,'zi'=4,'gy'=2] {'x','zi'}, dimensions={0} | all-to-all | bytes 786432 | tf_op jit(solution)/shard_map/all_to_all | solution.py:28
  309.1 0.1 reduce_sum.12
  309.2 33.2 %all_to_all.21 = bf16[8,3,512]{2,1,0:T(4,128)(2,1)S(1)} all-to-all(bf16[8,3,512]{2,1,0:T(4,128)(2,1)S(1)} %reshape.267), channel_id=1, replica_groups=mesh['rep'=2,'x'=4,'zo'=8,'zi'=4,'gy'=2] {'zo'}, dimensions={0} | all-to-all | bytes 49152 | tf_op jit(solution)/shard_map/all_to_all | solution.py:28
  342.4 0.1 reshape.268
  342.5 0.7 reshape.269
  (22 shorter events, 0.2 us)
Async XLA Ops:
  3.6 18.4 %all-to-all-start = ((bf16[4,64,3328]{2,1,0:T(8,128)(2,1)}), bf16[4,64,3328]{2,1,0:T(8,128)(2,1)S(1)}, u32[]{:S(2)}, u32[]{:S(2)}) async-start(bf16[4,64,3328]{2,1,0:T(8,128)(2,1)} %cut_by_x.1), calls=%async_computation | async-start | bytes 3407872 | tf_op jit(solution)/shard_map/all_to_all | solution.py:28
  22.0 1.2 copy-start.2
  27.4 16.4 %copy-start.8 = (s32[3]{0:T(128)S(1)}, s32[3]{0:T(128)}, u32[]{:S(2)}) copy-start(s32[3]{0:T(128)} %param.7) | copy-start | bytes 40
  27.4 16.5 %copy-start.7 = (bf16[3,4096]{1,0:T(4,128)(2,1)S(1)}, bf16[3,4096]{1,0:T(4,128)(2,1)}, u32[]{:S(2)}) copy-start(bf16[3,4096]{1,0:T(4,128)(2,1)} %param.6) | copy-start | bytes 73732
  27.4 256.3 %all-to-all-start.1 = ((bf16[4,4,64,832]{3,2,1,0:T(8,128)(2,1)}), bf16[4,4,64,832]{3,2,1,0:T(8,128)(2,1)}, u32[]{:S(2)}, u32[]{:S(2)}) async-start(bf16[4,4,64,832]{3,2,1,0:T(8,128)(2,1)} %cut_by_zi.1), calls=%async_computation.1 | async-start | bytes 3670016 | tf_op jit(solution)/shard_map/all_to_all | solution.py:28
  163.0 27.7 %copy-start.1 = (bf16[96,4224]{1,0:T(8,128)(2,1)}, bf16[96,4224]{1,0:T(8,128)(2,1)S(1)}, u32[]{:S(2)}) copy-start(bf16[96,4224]{1,0:T(8,128)(2,1)S(1)} %reshape.296.chunk_ref.refs_0_) | copy-start | bytes 2433028
  167.9 28.1 %collective-permute-start = (bf16[208,4096]{1,0:T(8,128)(2,1)}, bf16[208,4096]{1,0:T(8,128)(2,1)S(1)}, u32[]{:S(2)}, u32[]{:S(2)}) collective-permute-start(bf16[208,4096]{1,0:T(8,128)(2,1)} %pad_maximum_fusion.1), channel_id=1, source_target_pairs={{0,1},{1,0},{2,3},{3,2},{4,5},{5,4},{6,7},{7,6},{8,9},{9,8},{10,11... | collective-permute-start | bytes 5111816 | tf_op jit(solution)/shard_map/ppermute | solution.py:24
  184.1 23.2 %collective-permute-start.3 = (bf16[96,4224]{1,0:T(8,128)(2,1)S(1)}, bf16[96,4224]{1,0:T(8,128)(2,1)}, u32[]{:S(2)}, u32[]{:S(2)}) collective-permute-start(bf16[96,4224]{1,0:T(8,128)(2,1)S(1)} %reshape.296.chunk_ref.refs_0_), channel_id=1, source_target_pairs={{0,128},{64,192},{128,0},{192,64},{1,129},{65,193},{129,1},{193,65... | collective-permute-start | bytes 2433032 | tf_op jit(solution)/shard_map/ppermute | solution.py:24
  186.4 36.8 %collective-permute-start.2 = (bf16[96,4224]{1,0:T(8,128)(2,1)S(1)}, bf16[96,4224]{1,0:T(8,128)(2,1)}, u32[]{:S(2)}, u32[]{:S(2)}) collective-permute-start(bf16[96,4224]{1,0:T(8,128)(2,1)S(1)} %reshape.296.chunk_ref.refs_0_), channel_id=1, source_target_pairs={{0,192},{64,0},{128,64},{192,128},{1,193},{65,1},{129,65},{193,129... | collective-permute-start | bytes 2433032 | tf_op jit(solution)/shard_map/ppermute | solution.py:24
  190.7 36.6 %collective-permute-start.1 = (bf16[96,4224]{1,0:T(8,128)(2,1)S(1)}, bf16[96,4224]{1,0:T(8,128)(2,1)}, u32[]{:S(2)}, u32[]{:S(2)}) collective-permute-start(bf16[96,4224]{1,0:T(8,128)(2,1)S(1)} %reshape.296.chunk_ref.refs_0_), channel_id=1, source_target_pairs={{0,64},{64,128},{128,192},{192,0},{1,65},{65,129},{129,193},{193,1... | collective-permute-start | bytes 2433032 | tf_op jit(solution)/shard_map/ppermute | solution.py:24
  196.0 1.2 copy-start
  227.3 4.2 %copy-start.4 = (f32[96,208]{1,0:T(8,128)S(1)}, f32[96,208]{1,0:T(8,128)}, u32[]{:S(2)}) copy-start(f32[96,208]{1,0:T(8,128)} %get-tuple-element.23) | copy-start | bytes 239620
  227.3 4.2 %copy-start.5 = (f32[96,208]{1,0:T(8,128)S(1)}, f32[96,208]{1,0:T(8,128)}, u32[]{:S(2)}) copy-start(f32[96,208]{1,0:T(8,128)} %get-tuple-element.26) | copy-start | bytes 239620
  227.3 4.2 %copy-start.6 = (f32[96,208]{1,0:T(8,128)S(1)}, f32[96,208]{1,0:T(8,128)}, u32[]{:S(2)}) copy-start(f32[96,208]{1,0:T(8,128)} %get-tuple-element.25) | copy-start | bytes 239620
  232.4 6.3 %collective-permute-start.4 = (f32[384,208]{1,0:T(8,128)S(1)}, f32[384,208]{1,0:T(8,128)S(1)}, u32[]{:S(2)}, u32[]{:S(2)}) collective-permute-start(f32[384,208]{1,0:T(8,128)S(1)} %pad_maximum_fusion.3), channel_id=1, source_target_pairs={{0,1},{1,0},{2,3},{3,2},{4,5},{5,4},{6,7},{7,6},{8,9},{9,8},{10,11... | collective-permute-start | bytes 958472 | tf_op jit(solution)/shard_map/ppermute | solution.py:24
  238.7 0.8 copy-start.3
  286.4 5.7 %collective-permute-start.5 = (f32[384,512]{1,0:T(8,128)S(1)}, f32[384,512]{1,0:T(8,128)S(1)}, u32[]{:S(2)}, u32[]{:S(2)}) collective-permute-start(f32[384,512]{1,0:T(8,128)S(1)} %pad_maximum_fusion.2), channel_id=1, source_target_pairs={{0,1},{1,0},{2,3},{3,2},{4,5},{5,4},{6,7},{7,6},{8,9},{9,8},{10,11... | collective-permute-start | bytes 2359304 | tf_op jit(solution)/shard_map/ppermute | solution.py:24

commit v3 on v2

v3 whole, which is shorter than its diff:
```python
import functools

import jax
import jax.numpy as jnp
import numpy as np
from jax import lax
from jax.experimental import pallas as pl
from jax.experimental.pallas import tpu as pltpu
from jax.sharding import Mesh
from jax.sharding import PartitionSpec as P


PREFILL = 320
X, ZO, ZI = 4, 8, 4
GX = ("x", "zo", "zi")
REP_GX = ("rep", "x", "zo", "zi")
LANES = 128
STEPS = (0, 1, 3, 2)
F32 = jnp.float32
BF16 = jnp.bfloat16


def shifted(value, axis, by):
    count = lax.axis_size(axis)
    return lax.ppermute(value, axis, [(i, (i + by) % count) for i in range(count)])


def exchanged(blocks, axes):
    return lax.all_to_all(blocks, axes, split_axis=0, concat_axis=0, tiled=True)


HBM = pl.BlockSpec(memory_space=pl.ANY)


def run_copies(copies):
    for copy in copies:
        copy.start()
    for copy in copies:
        copy.wait()


def cut_by_x_kernel(rows_ref, out_ref, sems):
    rows = out_ref.shape[2]
    run_copies(
        [
            pltpu.make_async_copy(rows_ref.at[:, pl.ds(k * rows, rows)], out_ref.at[k], sems.at[k])
            for k in range(X)
        ]
    )


def cut_by_x(down):
    features, rows = down.shape
    return pl.pallas_call(
        cut_by_x_kernel,
        in_specs=[HBM],
        out_specs=HBM,
        out_shape=jax.ShapeDtypeStruct((X, features, rows // X), down.dtype),
        scratch_shapes=[pltpu.SemaphoreType.DMA((X,))],
        name="cut_by_x",
    )(down)


def split_kernel(gy_ref, gate_ref, up_ref, own_ref, other_ref, sems):
    half = own_ref.shape[2]
    gy = gy_ref[0]
    copies = []
    for k, ref in enumerate((gate_ref, up_ref)):
        for j, (out, which) in enumerate(((other_ref, 1 - gy), (own_ref, gy))):
            columns = pl.ds(pl.multiple_of(which * half, LANES), half)
            copies.append(pltpu.make_async_copy(ref.at[:, columns], out.at[k], sems.at[2 * k + j]))
    run_copies(copies)


def split_rows(gate, up, gy):
    columns, both = gate.shape
    out = jax.ShapeDtypeStruct((2, columns, both // 2), gate.dtype)
    own, other = pl.pallas_call(
        split_kernel,
        in_specs=[pl.BlockSpec(memory_space=pltpu.SMEM), HBM, HBM],
        out_specs=[HBM, HBM],
        out_shape=[out, out],
        scratch_shapes=[pltpu.SemaphoreType.DMA((4,))],
        name="split_rows",
    )(gy, gate, up)
    return own.reshape(2 * columns, -1), other.reshape(2 * columns, -1)


def cut_kernel(depth, gy_ref, rows_ref, out_ref):
    for zi in range(ZI):
        pieces = [rows_ref[0, :, (zo * ZI + zi) * depth : (zo * ZI + zi + 1) * depth] for zo in range(ZO)]
        out_ref[zi, 0] = jnp.concatenate(pieces, axis=1)


def cut_by_zi(blocks, gy):
    count, features, rows = blocks.shape
    depth = rows // (ZO * ZI)
    return pl.pallas_call(
        functools.partial(cut_kernel, depth),
        grid_spec=pltpu.PrefetchScalarGridSpec(
            num_scalar_prefetch=1,
            grid=(count,),
            in_specs=[
                pl.BlockSpec((1, features, rows), lambda i, gy: (lax.rem(i + gy[0] * (X // 2), X), 0, 0))
            ],
            out_specs=pl.BlockSpec((ZI, 1, features, ZO * depth), lambda i, gy: (0, i, 0, 0)),
        ),
        out_shape=jax.ShapeDtypeStruct((ZI, count, features, ZO * depth), blocks.dtype),
        name="cut_by_zi",
    )(gy, blocks)


def values_kernel(*refs):
    *chunk_refs, own_rows_ref, other_rows_ref, own_ref, other_ref = refs
    step = pl.program_id(0)
    chunks = jnp.concatenate([ref[...] for ref in chunk_refs], 0)
    for rows, out in ((other_rows_ref, other_ref), (own_rows_ref, own_ref)):
        term = lax.dot_general(chunks, rows[...], (((1,), (1,)), ((), ())), preferred_element_type=F32)

        @pl.when(step == 0)
        def _():
            out[...] = term

        @pl.when(step > 0)
        def _():
            out[...] += term


def values(chunks, own_rows, other_rows, steps=4):
    count, (columns, half) = chunks[0].shape[0], own_rows.shape
    depth = half // steps
    out = jax.ShapeDtypeStruct((len(chunks) * count, columns), F32)
    rows = pl.BlockSpec((columns, depth), lambda i: (0, i))
    out_spec = pl.BlockSpec(out.shape, lambda i: (0, 0))
    return pl.pallas_call(
        values_kernel,
        grid=(steps,),
        in_specs=[pl.BlockSpec((count, depth), lambda i: (0, i))] * len(chunks) + [rows, rows],
        out_specs=[out_spec, out_spec],
        out_shape=[out, out],
        name="values",
    )(*chunks, own_rows, other_rows)


def place_kernel(x_ref, *refs):
    *kinds_refs, slot_ref, place_ref = refs
    chunk, count = kinds_refs[0].shape[0], slot_ref.shape[1]
    starts = [lax.rem(x_ref[0] + X - by, X) * chunk for by in STEPS]
    lane = lax.broadcasted_iota(jnp.int32, (1, count), 1)
    order_row = lane + starts[0]
    for k in range(1, X):
        order_row = jnp.where(lane < k * chunk, order_row, lane - k * chunk + starts[k])
    kinds = jnp.concatenate([ref[...] for ref in kinds_refs], 0)
    place = lax.broadcasted_iota(jnp.int32, (chunk, LANES), 0)
    order = jnp.concatenate([place + start for start in starts], 0)
    earlier = (order_row.astype(F32) < order[:, :1].astype(F32)).astype(BF16)
    decode_before = jnp.dot(earlier, kinds, preferred_element_type=F32)
    target = jnp.where(kinds.astype(F32) > 0.5, PREFILL + decode_before, order.astype(F32) - decode_before)
    place_ref[...] = (target[:, :1] == slot_ref[...]).astype(BF16)


def placement(chunks, half, x, own_tokens):
    chunk = chunks[0].shape[0]
    count = X * chunk
    slot = np.arange(count).reshape(X, ZO, ZI, own_tokens).transpose(0, 2, 1, 3).reshape(1, count)
    kinds = pl.BlockSpec((chunk, LANES), lambda i: (0, half // LANES))
    return pl.pallas_call(
        place_kernel,
        grid=(1,),
        in_specs=[pl.BlockSpec(memory_space=pltpu.SMEM)]
        + [kinds] * X
        + [pl.BlockSpec((1, count), lambda i: (0, 0))],
        out_specs=pl.BlockSpec((count, count), lambda i: (0, 0)),
        out_shape=jax.ShapeDtypeStruct((count, count), BF16),
        name="placement",
    )(x, *chunks, slot.astype(np.float32))


def hidden_kernel(own_ref, other_ref, place_ref, out_ref):
    value = own_ref[...] + other_ref[...]
    width = value.shape[1] // 2
    gate_value, up_value = value[:, :width], value[:, width:]
    hidden = gate_value / (1 + jnp.exp(-gate_value)) * up_value
    placed = jnp.dot(hidden.T.astype(BF16), place_ref[...], preferred_element_type=F32)
    out_ref[...] = placed.astype(BF16)


def placed_hidden(own_value, other_value, place):
    width = other_value.shape[1] // 2
    return pl.pallas_call(
        hidden_kernel,
        out_shape=jax.ShapeDtypeStruct((width, place.shape[1]), BF16),
        name="placed_hidden",
    )(own_value, other_value, place)


def block(tokens, segment_ids, gate_weight, up_weight, down_weight):
    x, gy = lax.axis_index("x"), lax.axis_index("gy")
    own_tokens, half = tokens.shape
    down = exchanged(cut_by_x(down_weight[0].T), "x")

    kinds = jnp.broadcast_to(segment_ids.astype(tokens.dtype)[:, None], (own_tokens, LANES))
    wide = jnp.concatenate([tokens, kinds], 1)
    column = lax.all_gather(wide, ("zo", "zi"), axis=0, tiled=True)
    column, gate, up = lax.optimization_barrier((column, gate_weight, up_weight))
    gate, up = gate[:, 0].T, up[:, 0].T
    chunks = [column]
    for by in STEPS[1:]:
        chunks.append(shifted(column, "x", by))

    group = cut_by_zi(down, gy.reshape(1))
    group = exchanged(group, "zi")

    own_rows, other_rows = split_rows(gate, up, gy.reshape(1))
    other_rows = shifted(other_rows, "gy", 1)

    own_value, other_value = values(chunks, own_rows, other_rows)
    other_value = shifted(other_value, "gy", 1)
    place = placement(chunks, half, x.reshape(1), own_tokens)
    placed = placed_hidden(own_value, other_value, place)

    gathered = lax.all_gather(placed, "zo", axis=0, tiled=True)

    depth = group.shape[3]
    partial = lax.dot_general(
        gathered, group.reshape(-1, depth), (((0,), (1,)), ((), ())), preferred_element_type=F32
    )
    width = partial.shape[1] // (2 * ZI)

    def half_of(which):
        return jnp.concatenate(
            [partial[:, (2 * k + which) * width : (2 * k + which + 1) * width] for k in range(ZI)], 1
        )

    other_half = shifted(half_of(1), "gy", 1)
    summed = (half_of(0) + other_half).astype(BF16)
    slots = summed.shape[0]
    arrived = exchanged(summed.reshape(X * ZI, slots // (X * ZI), -1), ("x", "zi"))
    reduced = jnp.sum(arrived.astype(F32), axis=0).astype(BF16)
    owned = exchanged(reduced.reshape(ZO, own_tokens, -1), "zo")
    owned = owned.reshape(ZO, own_tokens, ZI, X // 2, -1).transpose(1, 3, 0, 2, 4)
    return owned.reshape(own_tokens, half)


def solution(mesh):
    torus = Mesh(
        mesh.devices.reshape(mesh.shape["rep"], X, ZO, ZI, mesh.shape["gy"]),
        ("rep", "x", "zo", "zi", "gy"),
    )
    placed = (P(REP_GX, "gy"), P(REP_GX), P(None, "gy", GX), P(None, "gy", GX), P("gy", None, GX))
    return jax.shard_map(block, mesh=torus, in_specs=placed, out_specs=P(REP_GX, "gy"), check_vma=False)
```

time: 346 us -> 495 us (1.43)
  Pallas kernels: 28.5 us -> 173 us
  waiting for transfers between devices: 33 us -> 46.7 us
  other arithmetic: 5.7 us -> 0.25 us
  local copies, waits for them, and re-layouts: 10.1 us -> 5.11 us
    pallas_call x6 -> x4, Pallas kernels: 22.1 us -> 167 us  [the longest x1 104 us: split_rows(): pl.pallas_call(split_kernel, in_specs=[pl.BlockSpec(memory_space=pltpu.SM...]
    ppermute x6, waiting for transfers between devices: 19.7 us -> 33.5 us  [shifted(): lax.ppermute(value, axis, [(i, (i + by) % count) for i in range(count)])]
  transfers between devices with their start and end apart: 8 -> 8, of which waited for: 4 -> 3; matrix products, arithmetic and copies ran while one was open for 3% -> 0% of each run, Pallas kernels for 6% -> 24%
where the time goes in v3:
time: 495 us; the launch traced here: 493 us
  blocking collectives  212 us (43%)
  Pallas kernels  173 us (35%)
  starting transfers between devices  53.3 us (11%)
  waiting for transfers between devices  46.7 us (9%)
  local copies, waits for them, and re-layouts  5.11 us (1%)
    all_gather x1, blocking collectives, block(): column = lax.all_gather(wide, ('zo', 'zi'), axis=0, tiled=True)  118 us
    pallas_call x1, Pallas kernels, split_rows(): pl.pallas_call(split_kernel, in_specs=[pl.BlockSpec(memory_space=pltpu.SM...  104 us
    pallas_call x1, Pallas kernels, cut_by_x(): pl.pallas_call(cut_by_x_kernel, in_specs=[HBM], out_specs=HBM, out_shape=...  52.8 us
    all_to_all x2, blocking collectives, exchanged(): return lax.all_to_all(blocks, axes, split_axis=0, concat_axis=0, tiled=True)  50.6 us
    all_gather x1, blocking collectives, block(): gathered = lax.all_gather(placed, 'zo', axis=0, tiled=True)  43.1 us
    ppermute x6, waiting for transfers between devices, shifted(): lax.ppermute(value, axis, [(i, (i + by) % count) for i in range(count)])  33.5 us
    ppermute x6, starting transfers between devices, shifted(): lax.ppermute(value, axis, [(i, (i + by) % count) for i in range(count)])  31.8 us
    all_to_all x2, starting transfers between devices, exchanged(): return lax.all_to_all(blocks, axes, split_axis=0, concat_axis=0, tiled=True)  21.5 us
  transfers between devices with their start and end apart: 8, of which 3 were waited for; matrix products, arithmetic and copies ran while one was open for 0% of the time, Pallas kernels for 24%

profile of v3, /device:TPU:33, one launch (start us, length us, event | category | flops | bytes accessed | tf_op | source)
XLA Modules:
  0.0 493.2 jit_solution(9603391980287123894)
XLA Ops:
  0.0 52.8 %cut_by_x.1 = bf16[4,64,3328]{2,1,0:T(8,128)(2,1)} custom-call(bf16[64,13312]{1,0:T(8,128)(2,1)} %bitcast.22), custom_call_target="tpu_custom_call" | custom-call | tf_op jit(solution)/shard_map/cut_by_x/pallas_call | solution.py:54
  52.8 5.1 %all-to-all-start = ((bf16[4,64,3328]{2,1,0:T(8,128)(2,1)}), bf16[4,64,3328]{2,1,0:T(8,128)(2,1)S(1)}, u32[]{:S(2)}, u32[]{:S(2)}) async-start(bf16[4,64,3328]{2,1,0:T(8,128)(2,1)} %cut_by_x.1), calls=%async_computation | async-start | bytes 3407872 | tf_op jit(solution)/shard_map/all_to_all | solution.py:29
  57.9 13.3 %all-to-all-done.rows_ref = bf16[4,64,3328]{2,1,0:T(8,128)(2,1)S(1)} async-done(((bf16[4,64,3328]{2,1,0:T(8,128)(2,1)}), bf16[4,64,3328]{2,1,0:T(8,128)(2,1)S(1)}, u32[]{:S(2)}, u32[]{:S(2)}) %all-to-all-start) | async-done | bytes 1703968 | tf_op jit(solution)/shard_map/all_to_all | solution.py:29
  71.1 0.0 copy-start.1
  71.1 1.2 copy-done.1
  72.4 4.2 cut_by_zi.1
  76.6 0.0 copy-start.7
  76.6 0.0 copy-start.6
  76.6 16.4 %all-to-all-start.1 = ((bf16[4,4,64,832]{3,2,1,0:T(8,128)(2,1)}), bf16[4,4,64,832]{3,2,1,0:T(8,128)(2,1)}, u32[]{:S(2)}, u32[]{:S(2)}) async-start(bf16[4,4,64,832]{3,2,1,0:T(8,128)(2,1)} %cut_by_zi.1), calls=%async_computation.1 | async-start | bytes 3670016 | tf_op jit(solution)/shard_map/all_to_all | solution.py:29
  93.0 0.0 copy-done.7
  93.0 0.1 broadcast_in_dim.2
  93.1 0.0 copy-done.6
  93.1 118.4 %all-gather = bf16[32,3,4224]{2,1,0:T(4,128)(2,1)S(1)} all-gather(bf16[1,3,4224]{2,1,0:T(4,128)(2,1)S(1)} %maximum_bitcast_fusion), channel_id=1, replica_groups=mesh['rep'=2,'x'=4,'zo'=8,'zi'=4,'gy'=2] {'zo','zi'}, dimensions={0}, use_global_device_ids=true | all-gather | bytes 836352 | tf_op jit(solution)/shard_map/all_gather | solution.py:204
  211.5 0.7 reshape.39.refs_0_
  212.2 0.0 copy-start
  212.2 104.4 %split_rows.1 = (bf16[2,104,4096]{2,1,0:T(8,128)(2,1)}, bf16[2,104,4096]{2,1,0:T(8,128)(2,1)}) custom-call(s32[1]{0:T(128)} %bitcast.1.gy_ref, bf16[104,8192]{1,0:T(8,128)(2,1)} %bitcast.23, bf16[104,8192]{1,0:T(8,128)(2,1)} %bitcast.24), custom_call_target="tpu_custom_call" | custom-call | tf_op jit(solution)/shard_map/split_rows/pallas_call | solution.py:78
  316.6 16.2 %collective-permute-start.3 = (bf16[208,4096]{1,0:T(8,128)(2,1)}, bf16[208,4096]{1,0:T(8,128)(2,1)}, u32[]{:S(2)}, u32[]{:S(2)}) collective-permute-start(bf16[208,4096]{1,0:T(8,128)(2,1)} %bitcast.28), channel_id=1, source_target_pairs={{0,1},{1,0},{2,3},{3,2},{4,5},{5,4},{6,7},{7,6},{8,9},{9,8},{10,11... | collective-permute-start | bytes 5111816 | tf_op jit(solution)/shard_map/ppermute | solution.py:25
  332.9 2.2 collective-permute-start
  335.1 4.3 collective-permute-start.1
  339.4 0.0 copy-done
  339.4 2.0 collective-permute-start.2
  341.4 31.6 %collective-permute-done.refs_1_ = bf16[96,4224]{1,0:T(8,128)(2,1)S(1)} collective-permute-done((bf16[96,4224]{1,0:T(8,128)(2,1)S(1)}, bf16[96,4224]{1,0:T(8,128)(2,1)S(1)}, u32[]{:S(2)}, u32[]{:S(2)}) %collective-permute-start) | collective-permute-done | bytes 811040 | tf_op jit(solution)/shard_map/ppermute | solution.py:25
  373.0 0.0 collective-permute-done.1.refs_2_
  373.0 0.0 collective-permute-done.2.refs_3_
  373.0 0.0 copy-start.4
  373.0 0.0 collective-permute-done.3.refs_5_
  373.0 0.9 copy-done.2
  373.9 0.3 copy-done.3
  374.2 0.2 copy-done.4
  374.4 7.5 %values.1 = (f32[384,208]{1,0:T(8,128)}, f32[384,208]{1,0:T(8,128)}) custom-call(bf16[96,4224]{1,0:T(8,128)(2,1)} %copy-done, bf16[96,4224]{1,0:T(8,128)(2,1)} %copy-done.2, bf16[96,4224]{1,0:T(8,128)(2,1)} %copy-done.3, bf16[96,4224]{1,0:T(8,128)(2,1)} %copy-done.4, bf16[208,4096]{1,0:T(8,128)(2,1)} %bitcast.25, ...), custom_call_target="tpu_custom_call" | custom-call | tf_op jit(solution)/shard_map/values/pallas_call | solution.py:135
  381.9 3.8 collective-permute-start.4
  385.7 1.9 placement.1.place_ref
  387.7 0.0 collective-permute-done.4.other_ref
  387.7 0.7 copy-done.5
  388.4 2.2 placed_hidden.1
  390.6 43.1 %all_gather.7 = bf16[832,384]{1,0:T(8,128)(2,1)S(1)} all-gather(bf16[104,384]{1,0:T(8,128)(2,1)} %placed_hidden.1), channel_id=1, replica_groups=mesh['rep'=2,'x'=4,'zo'=8,'zi'=4,'gy'=2] {'zo'}, dimensions={0}, use_global_device_ids=true | all-gather | bytes 718848 | tf_op jit(solution)/shard_map/all_gather | solution.py:222
  433.7 0.0 all-to-all-done.1
  433.7 2.5 fusion.2
  436.2 0.1 fusion.1
  436.3 0.1 pad_maximum_fusion
  436.4 3.3 collective-permute-start.5
  439.7 1.9 collective-permute-done.5
  441.6 0.1 fusion
  441.7 17.7 %all_to_all.20 = bf16[16,24,512]{2,1,0:T(8,128)(2,1)S(1)} all-to-all(bf16[16,24,512]{2,1,0:T(8,128)(2,1)S(1)} %bitcast.26), channel_id=1, replica_groups=mesh['rep'=2,'x'=4,'zo'=8,'zi'=4,'gy'=2] {'x','zi'}, dimensions={0} | all-to-all | bytes 786432 | tf_op jit(solution)/shard_map/all_to_all | solution.py:29
  459.3 0.1 reduce_sum.12
  459.4 33.0 %all_to_all.21 = bf16[8,3,512]{2,1,0:T(4,128)(2,1)S(1)} all-to-all(bf16[8,3,512]{2,1,0:T(4,128)(2,1)S(1)} %reshape.35), channel_id=1, replica_groups=mesh['rep'=2,'x'=4,'zo'=8,'zi'=4,'gy'=2] {'zo'}, dimensions={0} | all-to-all | bytes 49152 | tf_op jit(solution)/shard_map/all_to_all | solution.py:29
  492.4 0.1 reshape.36
  492.5 0.7 reshape.37
  (8 shorter events, 0.1 us)
Async XLA Ops:
  52.8 18.4 %all-to-all-start = ((bf16[4,64,3328]{2,1,0:T(8,128)(2,1)}), bf16[4,64,3328]{2,1,0:T(8,128)(2,1)S(1)}, u32[]{:S(2)}, u32[]{:S(2)}) async-start(bf16[4,64,3328]{2,1,0:T(8,128)(2,1)} %cut_by_x.1), calls=%async_computation | async-start | bytes 3407872 | tf_op jit(solution)/shard_map/all_to_all | solution.py:29
  71.1 1.2 copy-start.1
  76.6 16.4 %copy-start.7 = (s32[3]{0:T(128)S(1)}, s32[3]{0:T(128)}, u32[]{:S(2)}) copy-start(s32[3]{0:T(128)} %param.7) | copy-start | bytes 40
  76.6 16.5 %copy-start.6 = (bf16[3,4096]{1,0:T(4,128)(2,1)S(1)}, bf16[3,4096]{1,0:T(4,128)(2,1)}, u32[]{:S(2)}) copy-start(bf16[3,4096]{1,0:T(4,128)(2,1)} %param.6) | copy-start | bytes 73732
  76.6 357.1 %all-to-all-start.1 = ((bf16[4,4,64,832]{3,2,1,0:T(8,128)(2,1)}), bf16[4,4,64,832]{3,2,1,0:T(8,128)(2,1)}, u32[]{:S(2)}, u32[]{:S(2)}) async-start(bf16[4,4,64,832]{3,2,1,0:T(8,128)(2,1)} %cut_by_zi.1), calls=%async_computation.1 | async-start | bytes 3670016 | tf_op jit(solution)/shard_map/all_to_all | solution.py:29
  212.2 127.2 %copy-start = (bf16[96,4224]{1,0:T(8,128)(2,1)}, bf16[96,4224]{1,0:T(8,128)(2,1)S(1)}, u32[]{:S(2)}) copy-start(bf16[96,4224]{1,0:T(8,128)(2,1)S(1)} %reshape.39.refs_0_) | copy-start | bytes 2433028
  316.6 56.4 %collective-permute-start.3 = (bf16[208,4096]{1,0:T(8,128)(2,1)}, bf16[208,4096]{1,0:T(8,128)(2,1)}, u32[]{:S(2)}, u32[]{:S(2)}) collective-permute-start(bf16[208,4096]{1,0:T(8,128)(2,1)} %bitcast.28), channel_id=1, source_target_pairs={{0,1},{1,0},{2,3},{3,2},{4,5},{5,4},{6,7},{7,6},{8,9},{9,8},{10,11... | collective-permute-start | bytes 5111816 | tf_op jit(solution)/shard_map/ppermute | solution.py:25
  332.9 40.1 %collective-permute-start = (bf16[96,4224]{1,0:T(8,128)(2,1)S(1)}, bf16[96,4224]{1,0:T(8,128)(2,1)S(1)}, u32[]{:S(2)}, u32[]{:S(2)}) collective-permute-start(bf16[96,4224]{1,0:T(8,128)(2,1)S(1)} %reshape.39.refs_0_), channel_id=1, source_target_pairs={{0,64},{64,128},{128,192},{192,0},{1,65},{65,129},{129,193},{193,1... | collective-permute-start | bytes 2433032 | tf_op jit(solution)/shard_map/ppermute | solution.py:25
  335.1 37.9 %collective-permute-start.1 = (bf16[96,4224]{1,0:T(8,128)(2,1)S(1)}, bf16[96,4224]{1,0:T(8,128)(2,1)S(1)}, u32[]{:S(2)}, u32[]{:S(2)}) collective-permute-start(bf16[96,4224]{1,0:T(8,128)(2,1)S(1)} %reshape.39.refs_0_), channel_id=1, source_target_pairs={{0,192},{64,0},{128,64},{192,128},{1,193},{65,1},{129,65},{193,129... | collective-permute-start | bytes 2433032 | tf_op jit(solution)/shard_map/ppermute | solution.py:25
  339.4 33.6 %collective-permute-start.2 = (bf16[96,4224]{1,0:T(8,128)(2,1)S(1)}, bf16[96,4224]{1,0:T(8,128)(2,1)S(1)}, u32[]{:S(2)}, u32[]{:S(2)}) collective-permute-start(bf16[96,4224]{1,0:T(8,128)(2,1)S(1)} %reshape.39.refs_0_), channel_id=1, source_target_pairs={{0,128},{64,192},{128,0},{192,64},{1,129},{65,193},{129,1},{193,65... | collective-permute-start | bytes 2433032 | tf_op jit(solution)/shard_map/ppermute | solution.py:25
  373.0 0.9 copy-start.2
  373.0 1.2 copy-start.3
  373.0 1.4 copy-start.4
  381.9 5.7 %collective-permute-start.4 = (f32[384,208]{1,0:T(8,128)}, f32[384,208]{1,0:T(8,128)S(1)}, u32[]{:S(2)}, u32[]{:S(2)}) collective-permute-start(f32[384,208]{1,0:T(8,128)} %get-tuple-element.18), channel_id=1, source_target_pairs={{0,1},{1,0},{2,3},{3,2},{4,5},{5,4},{6,7},{7,6},{8,9},{9,8},{10,11... | collective-permute-start | bytes 958472 | tf_op jit(solution)/shard_map/ppermute | solution.py:25
  387.7 0.7 copy-start.5
  436.4 5.2 %collective-permute-start.5 = (f32[384,512]{1,0:T(8,128)S(1)}, f32[384,512]{1,0:T(8,128)S(1)}, u32[]{:S(2)}, u32[]{:S(2)}) collective-permute-start(f32[384,512]{1,0:T(8,128)S(1)} %pad_maximum_fusion), channel_id=1, source_target_pairs={{0,1},{1,0},{2,3},{3,2},{4,5},{5,4},{6,7},{7,6},{8,9},{9,8},{10,11... | collective-permute-start | bytes 2359304 | tf_op jit(solution)/shard_map/ppermute | solution.py:25

commit v4 on v3

--- a/solution.py
+++ b/solution.py
@@ -32,58 +32,37 @@
 HBM = pl.BlockSpec(memory_space=pl.ANY)
 
 
-def run_copies(copies):
-    for copy in copies:
+def cut_by_x_kernel(rows_ref, out_ref, held, in_sems, out_sems):
+    rows = out_ref.shape[2]
+    ins = [
+        pltpu.make_async_copy(rows_ref.at[:, pl.ds(k * rows, rows)], held.at[k], in_sems.at[k])
+        for k in range(X)
+    ]
+    outs = [pltpu.make_async_copy(held.at[k], out_ref.at[k], out_sems.at[k]) for k in range(X)]
+    for copy in ins:
         copy.start()
-    for copy in copies:
+    for arrive, leave in zip(ins, outs, strict=True):
+        arrive.wait()
+        leave.start()
+    for copy in outs:
         copy.wait()
-
-
-def cut_by_x_kernel(rows_ref, out_ref, sems):
-    rows = out_ref.shape[2]
-    run_copies(
-        [
-            pltpu.make_async_copy(rows_ref.at[:, pl.ds(k * rows, rows)], out_ref.at[k], sems.at[k])
-            for k in range(X)
-        ]
-    )
 
 
 def cut_by_x(down):
     features, rows = down.shape
+    shape = (X, features, rows // X)
     return pl.pallas_call(
         cut_by_x_kernel,
         in_specs=[HBM],
         out_specs=HBM,
-        out_shape=jax.ShapeDtypeStruct((X, features, rows // X), down.dtype),
-        scratch_shapes=[pltpu.SemaphoreType.DMA((X,))],
+        out_shape=jax.ShapeDtypeStruct(shape, down.dtype),
+        scratch_shapes=[
+            pltpu.VMEM(shape, down.dtype),
+            pltpu.SemaphoreType.DMA((X,)),
+            pltpu.SemaphoreType.DMA((X,)),
+        ],
         name="cut_by_x",
     )(down)
-
-
-def split_kernel(gy_ref, gate_ref, up_ref, own_ref, other_ref, sems):
-    half = own_ref.shape[2]
-    gy = gy_ref[0]
-    copies = []
-    for k, ref in enumerate((gate_ref, up_ref)):
-        for j, (out, which) in enumerate(((other_ref, 1 - gy), (own_ref, gy))):
-            columns = pl.ds(pl.multiple_of(which * half, LANES), half)
-            copies.append(pltpu.make_async_copy(ref.at[:, columns], out.at[k], sems.at[2 * k + j]))
-    run_copies(copies)
-
-
-def split_rows(gate, up, gy):
-    columns, both = gate.shape
-    out = jax.ShapeDtypeStruct((2, columns, both // 2), gate.dtype)
-    own, other = pl.pallas_call(
-        split_kernel,
-        in_specs=[pl.BlockSpec(memory_space=pltpu.SMEM), HBM, HBM],
-        out_specs=[HBM, HBM],
-        out_shape=[out, out],
-        scratch_shapes=[pltpu.SemaphoreType.DMA((4,))],
-        name="split_rows",
-    )(gy, gate, up)
-    return own.reshape(2 * columns, -1), other.reshape(2 * columns, -1)
 
 
 def cut_kernel(depth, gy_ref, rows_ref, out_ref):
@@ -108,38 +87,6 @@
         out_shape=jax.ShapeDtypeStruct((ZI, count, features, ZO * depth), blocks.dtype),
         name="cut_by_zi",
     )(gy, blocks)
-
-
-def values_kernel(*refs):
-    *chunk_refs, own_rows_ref, other_rows_ref, own_ref, other_ref = refs
-    step = pl.program_id(0)
-    chunks = jnp.concatenate([ref[...] for ref in chunk_refs], 0)
-    for rows, out in ((other_rows_ref, other_ref), (own_rows_ref, own_ref)):
-        term = lax.dot_general(chunks, rows[...], (((1,), (1,)), ((), ())), preferred_element_type=F32)
-
-        @pl.when(step == 0)
-        def _():
-            out[...] = term
-
-        @pl.when(step > 0)
-        def _():
-            out[...] += term
-
-
-def values(chunks, own_rows, other_rows, steps=4):
-    count, (columns, half) = chunks[0].shape[0], own_rows.shape
-    depth = half // steps
-    out = jax.ShapeDtypeStruct((len(chunks) * count, columns), F32)
-    rows = pl.BlockSpec((columns, depth), lambda i: (0, i))
-    out_spec = pl.BlockSpec(out.shape, lambda i: (0, 0))
-    return pl.pallas_call(
-        values_kernel,
-        grid=(steps,),
-        in_specs=[pl.BlockSpec((count, depth), lambda i: (0, i))] * len(chunks) + [rows, rows],
-        out_specs=[out_spec, out_spec],
-        out_shape=[out, out],
-        name="values",
-    )(*chunks, own_rows, other_rows)
 
 
 def place_kernel(x_ref, *refs):
@@ -176,22 +123,51 @@
     )(x, *chunks, slot.astype(np.float32))
 
 
-def hidden_kernel(own_ref, other_ref, place_ref, out_ref):
-    value = own_ref[...] + other_ref[...]
-    width = value.shape[1] // 2
-    gate_value, up_value = value[:, :width], value[:, width:]
-    hidden = gate_value / (1 + jnp.exp(-gate_value)) * up_value
-    placed = jnp.dot(hidden.T.astype(BF16), place_ref[...], preferred_element_type=F32)
-    out_ref[...] = placed.astype(BF16)
-
-
-def placed_hidden(own_value, other_value, place):
-    width = other_value.shape[1] // 2
+def hidden_kernel(gy_ref, *refs):
+    own_refs, other_refs = refs[:X], refs[X : 2 * X]
+    gate_own, gate_other, up_own, up_other, place_ref, out_ref, gate_sum, up_sum = refs[2 * X :]
+    step = pl.program_id(0)
+    own, other = (jnp.concatenate([ref[...] for ref in part], 0) for part in (own_refs, other_refs))
+    across = (((1,), (1,)), ((), ()))
+    for total, rows, other_rows in ((gate_sum, gate_own, gate_other), (up_sum, up_own, up_other)):
+        term = lax.dot_general(rows[...], own, across, preferred_element_type=F32)
+        term += lax.dot_general(other_rows[...], other, across, preferred_element_type=F32)
+
+        @pl.when(step == 0)
+        def _():
+            total[...] = term
+
+        @pl.when(step > 0)
+        def _():
+            total[...] += term
+
+    @pl.when(step == pl.num_programs(0) - 1)
+    def _():
+        gate_value = gate_sum[...]
+        hidden = (gate_value / (1 + jnp.exp(-gate_value)) * up_sum[...]).astype(BF16)
+        out_ref[...] = jnp.dot(hidden, place_ref[...], preferred_element_type=F32).astype(BF16)
+
+
+def placed_hidden(chunks, other_chunks, gate, up, place, gy, steps=4):
+    columns, features = gate.shape
+    half = features // 2
+    depth = half // steps
+    chunk, slots = chunks[0].shape[0], place.shape[1]
+    tokens = pl.BlockSpec((chunk, depth), lambda i, gy: (0, i))
+    own = pl.BlockSpec((columns, depth), lambda i, gy: (0, gy[0] * steps + i))
+    other = pl.BlockSpec((columns, depth), lambda i, gy: (0, (1 - gy[0]) * steps + i))
     return pl.pallas_call(
         hidden_kernel,
-        out_shape=jax.ShapeDtypeStruct((width, place.shape[1]), BF16),
+        grid_spec=pltpu.PrefetchScalarGridSpec(
+            num_scalar_prefetch=1,
+            grid=(steps,),
+            in_specs=[tokens] * (2 * X) + [own, other, own, other] + [pl.BlockSpec(place.shape, lambda i, gy: (0, 0))],
+            out_specs=pl.BlockSpec((columns, slots), lambda i, gy: (0, 0)),
+            scratch_shapes=[pltpu.VMEM((columns, slots), F32)] * 2,
+        ),
+        out_shape=jax.ShapeDtypeStruct((columns, slots), BF16),
         name="placed_hidden",
-    )(own_value, other_value, place)
+    )(gy, *chunks, *other_chunks, gate, gate, up, up, place)
 
 
 def block(tokens, segment_ids, gate_weight, up_weight, down_weight):
@@ -202,22 +178,19 @@
     kinds = jnp.broadcast_to(segment_ids.astype(tokens.dtype)[:, None], (own_tokens, LANES))
     wide = jnp.concatenate([tokens, kinds], 1)
     column = lax.all_gather(wide, ("zo", "zi"), axis=0, tiled=True)
-    column, gate, up = lax.optimization_barrier((column, gate_weight, up_weight))
-    gate, up = gate[:, 0].T, up[:, 0].T
+    gate, up = gate_weight[:, 0].T, up_weight[:, 0].T
     chunks = [column]
     for by in STEPS[1:]:
         chunks.append(shifted(column, "x", by))
+    other_chunks = []
+    for by, chunk in zip(STEPS, chunks, strict=True):
+        other_chunks.append(shifted(chunk, "gy", 1))
 
     group = cut_by_zi(down, gy.reshape(1))
     group = exchanged(group, "zi")
 
-    own_rows, other_rows = split_rows(gate, up, gy.reshape(1))
-    other_rows = shifted(other_rows, "gy", 1)
-
-    own_value, other_value = values(chunks, own_rows, other_rows)
-    other_value = shifted(other_value, "gy", 1)
     place = placement(chunks, half, x.reshape(1), own_tokens)
-    placed = placed_hidden(own_value, other_value, place)
+    placed = placed_hidden(chunks, other_chunks, gate, up, place, gy.reshape(1))
 
     gathered = lax.all_gather(placed, "zo", axis=0, tiled=True)
 

time: 495 us -> 321 us (0.65)
  Pallas kernels: 173 us -> 17.4 us
  waiting for transfers between devices: 46.7 us -> 15.6 us
  starting transfers between devices: 53.3 us -> 69.7 us
    pallas_call x3 -> x1, Pallas kernels: 114 us -> 9.02 us  [placed_hidden(): pl.pallas_call(hidden_kernel, grid_spec=pltpu.PrefetchScalarGridSpec(num_...]
    pallas_call x1, Pallas kernels: 52.8 us -> 2.29 us  [cut_by_x(): pl.pallas_call(cut_by_x_kernel, in_specs=[HBM], out_specs=HBM, out_shape=...]
    ppermute x6 -> x8, waiting for transfers between devices: 33.5 us -> 2.38 us  [shifted(): lax.ppermute(value, axis, [(i, (i + by) % count) for i in range(count)])]
    ppermute x6 -> x8, starting transfers between devices: 31.8 us -> 48.1 us  [shifted(): lax.ppermute(value, axis, [(i, (i + by) % count) for i in range(count)])]
  transfers between devices with their start and end apart: 8 -> 10, of which waited for: 3 -> 3; matrix products, arithmetic and copies ran while one was open for 0% -> 0% of each run, Pallas kernels for 24% -> 3%
where the time goes in v4:
time: 321 us; the launch traced here: 319 us
  blocking collectives  210 us (65%)
  starting transfers between devices  69.7 us (22%)
  Pallas kernels  17.4 us (5%)
  waiting for transfers between devices  15.6 us (5%)
    all_gather x1, blocking collectives, block(): column = lax.all_gather(wide, ('zo', 'zi'), axis=0, tiled=True)  118 us
    ppermute x8, starting transfers between devices, shifted(): lax.ppermute(value, axis, [(i, (i + by) % count) for i in range(count)])  48.1 us
    all_to_all x2, blocking collectives, exchanged(): return lax.all_to_all(blocks, axes, split_axis=0, concat_axis=0, tiled=True)  48.1 us
    all_gather x1, blocking collectives, block(): gathered = lax.all_gather(placed, 'zo', axis=0, tiled=True)  43.8 us
    all_to_all x2, starting transfers between devices, exchanged(): return lax.all_to_all(blocks, axes, split_axis=0, concat_axis=0, tiled=True)  21.5 us
    all_to_all x2, waiting for transfers between devices, exchanged(): return lax.all_to_all(blocks, axes, split_axis=0, concat_axis=0, tiled=True)  13.3 us
    pallas_call x1, Pallas kernels, placed_hidden(): pl.pallas_call(hidden_kernel, grid_spec=pltpu.PrefetchScalarGridSpec(num_...  9.02 us
  transfers between devices with their start and end apart: 10, of which 3 were waited for; matrix products, arithmetic and copies ran while one was open for 0% of the time, Pallas kernels for 3%

profile of v4, /device:TPU:33, one launch (start us, length us, event | category | flops | bytes accessed | tf_op | source)
XLA Modules:
  0.0 319.0 jit_solution(6954510141408172193)
XLA Ops:
  0.0 2.3 cut_by_x.1
  2.3 5.1 %all-to-all-start = ((bf16[4,64,3328]{2,1,0:T(8,128)(2,1)}), bf16[4,64,3328]{2,1,0:T(8,128)(2,1)S(1)}, u32[]{:S(2)}, u32[]{:S(2)}) async-start(bf16[4,64,3328]{2,1,0:T(8,128)(2,1)} %cut_by_x.1), calls=%async_computation | async-start | bytes 3407872 | tf_op jit(solution)/shard_map/all_to_all | solution.py:29
  7.4 13.3 %all-to-all-done.rows_ref = bf16[4,64,3328]{2,1,0:T(8,128)(2,1)S(1)} async-done(((bf16[4,64,3328]{2,1,0:T(8,128)(2,1)}), bf16[4,64,3328]{2,1,0:T(8,128)(2,1)S(1)}, u32[]{:S(2)}, u32[]{:S(2)}) %all-to-all-start) | async-done | bytes 1703968 | tf_op jit(solution)/shard_map/all_to_all | solution.py:29
  20.7 1.2 copy-done.1
  21.9 4.2 %cut_by_zi.1 = bf16[4,4,64,832]{3,2,1,0:T(8,128)(2,1)} custom-call(s32[1]{0:T(128)} %bitcast.gy_ref, bf16[4,64,3328]{2,1,0:T(8,128)(2,1)} %copy-done.1), custom_call_target="tpu_custom_call" | custom-call | tf_op jit(solution)/shard_map/cut_by_zi/pallas_call | solution.py:77
  26.0 16.4 %all-to-all-start.1 = ((bf16[4,4,64,832]{3,2,1,0:T(8,128)(2,1)}), bf16[4,4,64,832]{3,2,1,0:T(8,128)(2,1)}, u32[]{:S(2)}, u32[]{:S(2)}) async-start(bf16[4,4,64,832]{3,2,1,0:T(8,128)(2,1)} %cut_by_zi.1), calls=%async_computation.1 | async-start | bytes 3670016 | tf_op jit(solution)/shard_map/all_to_all | solution.py:29
  42.5 0.0 copy-done.6
  42.5 0.1 broadcast_in_dim.2
  42.5 0.0 copy-done.5
  42.6 118.4 %all-gather = bf16[32,3,4224]{2,1,0:T(4,128)(2,1)S(1)} all-gather(bf16[1,3,4224]{2,1,0:T(4,128)(2,1)S(1)} %maximum_bitcast_fusion), channel_id=1, replica_groups=mesh['rep'=2,'x'=4,'zo'=8,'zi'=4,'gy'=2] {'zo','zi'}, dimensions={0}, use_global_device_ids=true | all-gather | bytes 836352 | tf_op jit(solution)/shard_map/all_gather | solution.py:180
  161.0 0.7 reshape.31.refs_0_
  161.7 0.0 copy-start
  161.7 2.3 collective-permute-start.2
  164.0 4.3 %collective-permute-start.1 = (bf16[96,4224]{1,0:T(8,128)(2,1)S(1)}, bf16[96,4224]{1,0:T(8,128)(2,1)S(1)}, u32[]{:S(2)}, u32[]{:S(2)}) collective-permute-start(bf16[96,4224]{1,0:T(8,128)(2,1)S(1)} %reshape.31.refs_0_), channel_id=1, source_target_pairs={{0,192},{64,0},{128,64},{192,128},{1,193},{65,1},{129,65},{193,129... | collective-permute-start | bytes 2433032 | tf_op jit(solution)/shard_map/ppermute | solution.py:25
  168.3 2.0 collective-permute-start
  170.3 16.8 %collective-permute-start.3 = (bf16[96,4224]{1,0:T(8,128)(2,1)S(1)}, bf16[96,4224]{1,0:T(8,128)(2,1)}, u32[]{:S(2)}, u32[]{:S(2)}) collective-permute-start(bf16[96,4224]{1,0:T(8,128)(2,1)S(1)} %reshape.31.refs_0_), channel_id=1, source_target_pairs={{0,1},{1,0},{2,3},{3,2},{4,5},{5,4},{6,7},{7,6},{8,9},{9,8},{10,11... | collective-permute-start | bytes 2433032 | tf_op jit(solution)/shard_map/ppermute | solution.py:25
  187.1 0.0 collective-permute-done.2.refs_3_
  187.1 0.0 copy-start.2
  187.1 9.3 %collective-permute-start.6 = (bf16[96,4224]{1,0:T(8,128)(2,1)S(1)}, bf16[96,4224]{1,0:T(8,128)(2,1)}, u32[]{:S(2)}, u32[]{:S(2)}) collective-permute-start(bf16[96,4224]{1,0:T(8,128)(2,1)S(1)} %collective-permute-done.2.refs_3_), channel_id=1, source_target_pairs={{0,1},{1,0},{2,3},{3,2},{4,5},{5,4},{6,7},{7,6},{8,9},{9,8},{10,11... | collective-permute-start | bytes 2433032 | tf_op jit(solution)/shard_map/ppermute | solution.py:25
  196.4 0.0 collective-permute-done.1.refs_2_
  196.4 0.0 copy-start.3
  196.4 7.1 %collective-permute-start.5 = (bf16[96,4224]{1,0:T(8,128)(2,1)S(1)}, bf16[96,4224]{1,0:T(8,128)(2,1)}, u32[]{:S(2)}, u32[]{:S(2)}) collective-permute-start(bf16[96,4224]{1,0:T(8,128)(2,1)S(1)} %collective-permute-done.1.refs_2_), channel_id=1, source_target_pairs={{0,1},{1,0},{2,3},{3,2},{4,5},{5,4},{6,7},{7,6},{8,9},{9,8},{10,11... | collective-permute-start | bytes 2433032 | tf_op jit(solution)/shard_map/ppermute | solution.py:25
  203.5 0.0 collective-permute-done.refs_1_
  203.5 0.0 copy-start.4
  203.6 2.0 collective-permute-start.4
  205.5 0.0 copy-done
  205.5 0.0 copy-done.2
  205.5 0.0 copy-done.3
  205.5 0.0 copy-done.4
  205.6 1.9 placement.1.refs_12_
  207.5 0.0 collective-permute-done.3.refs_4_
  207.5 0.0 collective-permute-done.6.refs_7_
  207.5 0.0 collective-permute-done.5.refs_6_
  207.5 0.5 collective-permute-done.4.refs_5_
  207.9 9.0 %placed_hidden.1 = bf16[104,384]{1,0:T(8,128)(2,1)} custom-call(s32[1]{0:T(128)} %bitcast.gy_ref, bf16[96,4224]{1,0:T(8,128)(2,1)} %copy-done, bf16[96,4224]{1,0:T(8,128)(2,1)} %copy-done.4, bf16[96,4224]{1,0:T(8,128)(2,1)} %copy-done.3, bf16[96,4224]{1,0:T(8,128)(2,1)} %copy-done.2, bf16[96,4224]{1,0:T(8,128)(2,1)} %collective-permute-done.3.refs_4_, ...), custom_call_target="tpu_custom_call" | custom-call | tf_op jit(solution)/shard_map/placed_hidden/pallas_call | solution.py:159
  216.9 43.8 %all_gather.7 = bf16[832,384]{1,0:T(8,128)(2,1)S(1)} all-gather(bf16[104,384]{1,0:T(8,128)(2,1)} %placed_hidden.1), channel_id=1, replica_groups=mesh['rep'=2,'x'=4,'zo'=8,'zi'=4,'gy'=2] {'zo'}, dimensions={0}, use_global_device_ids=true | all-gather | bytes 718848 | tf_op jit(solution)/shard_map/all_gather | solution.py:195
  260.8 0.0 all-to-all-done.1
  260.8 2.5 fusion.2
  263.3 0.1 fusion.1
  263.5 0.1 pad_maximum_fusion
  263.5 4.4 %collective-permute-start.7 = (f32[384,512]{1,0:T(8,128)S(1)}, f32[384,512]{1,0:T(8,128)S(1)}, u32[]{:S(2)}, u32[]{:S(2)}) collective-permute-start(f32[384,512]{1,0:T(8,128)S(1)} %pad_maximum_fusion), channel_id=1, source_target_pairs={{0,1},{1,0},{2,3},{3,2},{4,5},{5,4},{6,7},{7,6},{8,9},{9,8},{10,11... | collective-permute-start | bytes 2359304 | tf_op jit(solution)/shard_map/ppermute | solution.py:25
  268.0 1.9 collective-permute-done.7
  269.9 0.1 fusion
  270.0 16.6 %all_to_all.20 = bf16[16,24,512]{2,1,0:T(8,128)(2,1)S(1)} all-to-all(bf16[16,24,512]{2,1,0:T(8,128)(2,1)S(1)} %bitcast.25), channel_id=1, replica_groups=mesh['rep'=2,'x'=4,'zo'=8,'zi'=4,'gy'=2] {'x','zi'}, dimensions={0} | all-to-all | bytes 786432 | tf_op jit(solution)/shard_map/all_to_all | solution.py:29
  286.5 0.1 reduce_sum.12
  286.6 31.5 %all_to_all.21 = bf16[8,3,512]{2,1,0:T(4,128)(2,1)S(1)} all-to-all(bf16[8,3,512]{2,1,0:T(4,128)(2,1)S(1)} %reshape.27), channel_id=1, replica_groups=mesh['rep'=2,'x'=4,'zo'=8,'zi'=4,'gy'=2] {'zo'}, dimensions={0} | all-to-all | bytes 49152 | tf_op jit(solution)/shard_map/all_to_all | solution.py:29
  318.2 0.1 reshape.28
  318.3 0.7 reshape.29
  (8 shorter events, 0.1 us)
Async XLA Ops:
  2.3 18.4 %all-to-all-start = ((bf16[4,64,3328]{2,1,0:T(8,128)(2,1)}), bf16[4,64,3328]{2,1,0:T(8,128)(2,1)S(1)}, u32[]{:S(2)}, u32[]{:S(2)}) async-start(bf16[4,64,3328]{2,1,0:T(8,128)(2,1)} %cut_by_x.1), calls=%async_computation | async-start | bytes 3407872 | tf_op jit(solution)/shard_map/all_to_all | solution.py:29
  20.7 1.2 copy-start.1
  26.0 16.4 %copy-start.6 = (s32[3]{0:T(128)S(1)}, s32[3]{0:T(128)}, u32[]{:S(2)}) copy-start(s32[3]{0:T(128)} %param.7) | copy-start | bytes 40
  26.0 16.5 %copy-start.5 = (bf16[3,4096]{1,0:T(4,128)(2,1)S(1)}, bf16[3,4096]{1,0:T(4,128)(2,1)}, u32[]{:S(2)}) copy-start(bf16[3,4096]{1,0:T(4,128)(2,1)} %param.6) | copy-start | bytes 73732
  26.0 234.8 %all-to-all-start.1 = ((bf16[4,4,64,832]{3,2,1,0:T(8,128)(2,1)}), bf16[4,4,64,832]{3,2,1,0:T(8,128)(2,1)}, u32[]{:S(2)}, u32[]{:S(2)}) async-start(bf16[4,4,64,832]{3,2,1,0:T(8,128)(2,1)} %cut_by_zi.1), calls=%async_computation.1 | async-start | bytes 3670016 | tf_op jit(solution)/shard_map/all_to_all | solution.py:29
  161.7 43.8 %copy-start = (bf16[96,4224]{1,0:T(8,128)(2,1)}, bf16[96,4224]{1,0:T(8,128)(2,1)S(1)}, u32[]{:S(2)}) copy-start(bf16[96,4224]{1,0:T(8,128)(2,1)S(1)} %reshape.31.refs_0_) | copy-start | bytes 2433028
  161.7 25.3 %collective-permute-start.2 = (bf16[96,4224]{1,0:T(8,128)(2,1)S(1)}, bf16[96,4224]{1,0:T(8,128)(2,1)S(1)}, u32[]{:S(2)}, u32[]{:S(2)}) collective-permute-start(bf16[96,4224]{1,0:T(8,128)(2,1)S(1)} %reshape.31.refs_0_), channel_id=1, source_target_pairs={{0,128},{64,192},{128,0},{192,64},{1,129},{65,193},{129,1},{193,65... | collective-permute-start | bytes 2433032 | tf_op jit(solution)/shard_map/ppermute | solution.py:25
  164.0 32.4 %collective-permute-start.1 = (bf16[96,4224]{1,0:T(8,128)(2,1)S(1)}, bf16[96,4224]{1,0:T(8,128)(2,1)S(1)}, u32[]{:S(2)}, u32[]{:S(2)}) collective-permute-start(bf16[96,4224]{1,0:T(8,128)(2,1)S(1)} %reshape.31.refs_0_), channel_id=1, source_target_pairs={{0,192},{64,0},{128,64},{192,128},{1,193},{65,1},{129,65},{193,129... | collective-permute-start | bytes 2433032 | tf_op jit(solution)/shard_map/ppermute | solution.py:25
  168.3 35.2 %collective-permute-start = (bf16[96,4224]{1,0:T(8,128)(2,1)S(1)}, bf16[96,4224]{1,0:T(8,128)(2,1)S(1)}, u32[]{:S(2)}, u32[]{:S(2)}) collective-permute-start(bf16[96,4224]{1,0:T(8,128)(2,1)S(1)} %reshape.31.refs_0_), channel_id=1, source_target_pairs={{0,64},{64,128},{128,192},{192,0},{1,65},{65,129},{129,193},{193,1... | collective-permute-start | bytes 2433032 | tf_op jit(solution)/shard_map/ppermute | solution.py:25
  170.3 37.2 %collective-permute-start.3 = (bf16[96,4224]{1,0:T(8,128)(2,1)S(1)}, bf16[96,4224]{1,0:T(8,128)(2,1)}, u32[]{:S(2)}, u32[]{:S(2)}) collective-permute-start(bf16[96,4224]{1,0:T(8,128)(2,1)S(1)} %reshape.31.refs_0_), channel_id=1, source_target_pairs={{0,1},{1,0},{2,3},{3,2},{4,5},{5,4},{6,7},{7,6},{8,9},{9,8},{10,11... | collective-permute-start | bytes 2433032 | tf_op jit(solution)/shard_map/ppermute | solution.py:25
  187.1 18.5 %copy-start.2 = (bf16[96,4224]{1,0:T(8,128)(2,1)}, bf16[96,4224]{1,0:T(8,128)(2,1)S(1)}, u32[]{:S(2)}) copy-start(bf16[96,4224]{1,0:T(8,128)(2,1)S(1)} %collective-permute-done.2.refs_3_) | copy-start | bytes 2433028
  187.1 20.4 %collective-permute-start.6 = (bf16[96,4224]{1,0:T(8,128)(2,1)S(1)}, bf16[96,4224]{1,0:T(8,128)(2,1)}, u32[]{:S(2)}, u32[]{:S(2)}) collective-permute-start(bf16[96,4224]{1,0:T(8,128)(2,1)S(1)} %collective-permute-done.2.refs_3_), channel_id=1, source_target_pairs={{0,1},{1,0},{2,3},{3,2},{4,5},{5,4},{6,7},{7,6},{8,9},{9,8},{10,11... | collective-permute-start | bytes 2433032 | tf_op jit(solution)/shard_map/ppermute | solution.py:25
  196.4 9.1 %copy-start.3 = (bf16[96,4224]{1,0:T(8,128)(2,1)}, bf16[96,4224]{1,0:T(8,128)(2,1)S(1)}, u32[]{:S(2)}) copy-start(bf16[96,4224]{1,0:T(8,128)(2,1)S(1)} %collective-permute-done.1.refs_2_) | copy-start | bytes 2433028
  196.4 11.0 %collective-permute-start.5 = (bf16[96,4224]{1,0:T(8,128)(2,1)S(1)}, bf16[96,4224]{1,0:T(8,128)(2,1)}, u32[]{:S(2)}, u32[]{:S(2)}) collective-permute-start(bf16[96,4224]{1,0:T(8,128)(2,1)S(1)} %collective-permute-done.1.refs_2_), channel_id=1, source_target_pairs={{0,1},{1,0},{2,3},{3,2},{4,5},{5,4},{6,7},{7,6},{8,9},{9,8},{10,11... | collective-permute-start | bytes 2433032 | tf_op jit(solution)/shard_map/ppermute | solution.py:25
  203.5 2.0 copy-start.4
  203.6 4.4 %collective-permute-start.4 = (bf16[96,4224]{1,0:T(8,128)(2,1)S(1)}, bf16[96,4224]{1,0:T(8,128)(2,1)}, u32[]{:S(2)}, u32[]{:S(2)}) collective-permute-start(bf16[96,4224]{1,0:T(8,128)(2,1)S(1)} %collective-permute-done.refs_1_), channel_id=1, source_target_pairs={{0,1},{1,0},{2,3},{3,2},{4,5},{5,4},{6,7},{7,6},{8,9},{9,8},{10,11... | collective-permute-start | bytes 2433032 | tf_op jit(solution)/shard_map/ppermute | solution.py:25
  263.5 6.3 %collective-permute-start.7 = (f32[384,512]{1,0:T(8,128)S(1)}, f32[384,512]{1,0:T(8,128)S(1)}, u32[]{:S(2)}, u32[]{:S(2)}) collective-permute-start(f32[384,512]{1,0:T(8,128)S(1)} %pad_maximum_fusion), channel_id=1, source_target_pairs={{0,1},{1,0},{2,3},{3,2},{4,5},{5,4},{6,7},{7,6},{8,9},{9,8},{10,11... | collective-permute-start | bytes 2359304 | tf_op jit(solution)/shard_map/ppermute | solution.py:25

commit v5 on v4

--- a/solution.py
+++ b/solution.py
@@ -32,6 +32,16 @@
 HBM = pl.BlockSpec(memory_space=pl.ANY)
 
 
+def pass_on(ins, outs):
+    for copy in ins:
+        copy.start()
+    for arrive, leave in zip(ins, outs, strict=True):
+        arrive.wait()
+        leave.start()
+    for copy in outs:
+        copy.wait()
+
+
 def cut_by_x_kernel(rows_ref, out_ref, held, in_sems, out_sems):
     rows = out_ref.shape[2]
     ins = [
@@ -39,13 +49,7 @@
         for k in range(X)
     ]
     outs = [pltpu.make_async_copy(held.at[k], out_ref.at[k], out_sems.at[k]) for k in range(X)]
-    for copy in ins:
-        copy.start()
-    for arrive, leave in zip(ins, outs, strict=True):
-        arrive.wait()
-        leave.start()
-    for copy in outs:
-        copy.wait()
+    pass_on(ins, outs)
 
 
 def cut_by_x(down):
@@ -63,6 +67,37 @@
         ],
         name="cut_by_x",
     )(down)
+
+
+def split_kernel(gy_ref, gate_ref, up_ref, own_ref, other_ref, held, in_sems, out_sems):
+    half = own_ref.shape[2]
+    gy = gy_ref[0]
+    ins, outs = [], []
+    for k, ref in enumerate((gate_ref, up_ref)):
+        for j, (out, which) in enumerate(((other_ref, 1 - gy), (own_ref, gy))):
+            slot = 2 * k + j
+            columns = pl.ds(pl.multiple_of(which * half, LANES), half)
+            ins.append(pltpu.make_async_copy(ref.at[:, columns], held.at[slot], in_sems.at[slot]))
+            outs.append(pltpu.make_async_copy(held.at[slot], out.at[k], out_sems.at[slot]))
+    pass_on(ins, outs)
+
+
+def split_rows(gate, up, gy):
+    columns, both = gate.shape
+    out = jax.ShapeDtypeStruct((2, columns, both // 2), gate.dtype)
+    own, other = pl.pallas_call(
+        split_kernel,
+        in_specs=[pl.BlockSpec(memory_space=pltpu.SMEM), HBM, HBM],
+        out_specs=[HBM, HBM],
+        out_shape=[out, out],
+        scratch_shapes=[
+            pltpu.VMEM((4, columns, both // 2), gate.dtype),
+            pltpu.SemaphoreType.DMA((4,)),
+            pltpu.SemaphoreType.DMA((4,)),
+        ],
+        name="split_rows",
+    )(gy, gate, up)
+    return own.reshape(2 * columns, -1), other.reshape(2 * columns, -1)
 
 
 def cut_kernel(depth, gy_ref, rows_ref, out_ref):
@@ -123,51 +158,52 @@
     )(x, *chunks, slot.astype(np.float32))
 
 
-def hidden_kernel(gy_ref, *refs):
-    own_refs, other_refs = refs[:X], refs[X : 2 * X]
-    gate_own, gate_other, up_own, up_other, place_ref, out_ref, gate_sum, up_sum = refs[2 * X :]
+def values_kernel(*refs):
+    *chunk_refs, own_rows_ref, other_rows_ref, own_ref, other_ref = refs
     step = pl.program_id(0)
-    own, other = (jnp.concatenate([ref[...] for ref in part], 0) for part in (own_refs, other_refs))
-    across = (((1,), (1,)), ((), ()))
-    for total, rows, other_rows in ((gate_sum, gate_own, gate_other), (up_sum, up_own, up_other)):
-        term = lax.dot_general(rows[...], own, across, preferred_element_type=F32)
-        term += lax.dot_general(other_rows[...], other, across, preferred_element_type=F32)
+    chunks = jnp.concatenate([ref[...] for ref in chunk_refs], 0)
+    for rows, out in ((other_rows_ref, other_ref), (own_rows_ref, own_ref)):
+        term = lax.dot_general(rows[...], chunks, (((1,), (1,)), ((), ())), preferred_element_type=F32)
 
         @pl.when(step == 0)
         def _():
-            total[...] = term
+            out[...] = term
 
         @pl.when(step > 0)
         def _():
-            total[...] += term
-
-    @pl.when(step == pl.num_programs(0) - 1)
-    def _():
-        gate_value = gate_sum[...]
-        hidden = (gate_value / (1 + jnp.exp(-gate_value)) * up_sum[...]).astype(BF16)
-        out_ref[...] = jnp.dot(hidden, place_ref[...], preferred_element_type=F32).astype(BF16)
-
-
-def placed_hidden(chunks, other_chunks, gate, up, place, gy, steps=4):
-    columns, features = gate.shape
-    half = features // 2
+            out[...] += term
+
+
+def values(chunks, own_rows, other_rows, steps=4):
+    count, (columns, half) = chunks[0].shape[0], own_rows.shape
     depth = half // steps
-    chunk, slots = chunks[0].shape[0], place.shape[1]
-    tokens = pl.BlockSpec((chunk, depth), lambda i, gy: (0, i))
-    own = pl.BlockSpec((columns, depth), lambda i, gy: (0, gy[0] * steps + i))
-    other = pl.BlockSpec((columns, depth), lambda i, gy: (0, (1 - gy[0]) * steps + i))
+    out = jax.ShapeDtypeStruct((columns, X * count), F32)
+    rows = pl.BlockSpec((columns, depth), lambda i: (0, i))
+    out_spec = pl.BlockSpec(out.shape, lambda i: (0, 0))
+    return pl.pallas_call(
+        values_kernel,
+        grid=(steps,),
+        in_specs=[pl.BlockSpec((count, depth), lambda i: (0, i))] * X + [rows, rows],
+        out_specs=[out_spec, out_spec],
+        out_shape=[out, out],
+        name="values",
+    )(*chunks, own_rows, other_rows)
+
+
+def hidden_kernel(own_ref, other_ref, place_ref, out_ref):
+    value = own_ref[...] + other_ref[...]
+    width = value.shape[0] // 2
+    gate_value, up_value = value[:width], value[width:]
+    hidden = (gate_value / (1 + jnp.exp(-gate_value)) * up_value).astype(BF16)
+    out_ref[...] = jnp.dot(hidden, place_ref[...], preferred_element_type=F32).astype(BF16)
+
+
+def placed_hidden(own_value, other_value, place):
     return pl.pallas_call(
         hidden_kernel,
-        grid_spec=pltpu.PrefetchScalarGridSpec(
-            num_scalar_prefetch=1,
-            grid=(steps,),
-            in_specs=[tokens] * (2 * X) + [own, other, own, other] + [pl.BlockSpec(place.shape, lambda i, gy: (0, 0))],
-            out_specs=pl.BlockSpec((columns, slots), lambda i, gy: (0, 0)),
-            scratch_shapes=[pltpu.VMEM((columns, slots), F32)] * 2,
-        ),
-        out_shape=jax.ShapeDtypeStruct((columns, slots), BF16),
+        out_shape=jax.ShapeDtypeStruct((own_value.shape[0] // 2, place.shape[1]), BF16),
         name="placed_hidden",
-    )(gy, *chunks, *other_chunks, gate, gate, up, up, place)
+    )(own_value, other_value, place)
 
 
 def block(tokens, segment_ids, gate_weight, up_weight, down_weight):
@@ -182,15 +218,16 @@
     chunks = [column]
     for by in STEPS[1:]:
         chunks.append(shifted(column, "x", by))
-    other_chunks = []
-    for by, chunk in zip(STEPS, chunks, strict=True):
-        other_chunks.append(shifted(chunk, "gy", 1))
-
     group = cut_by_zi(down, gy.reshape(1))
     group = exchanged(group, "zi")
 
+    own_rows, other_rows = split_rows(gate, up, gy.reshape(1))
+    other_rows = shifted(other_rows, "gy", 1)
+
+    own_value, other_value = values(chunks, own_rows, other_rows)
+    other_value = shifted(other_value, "gy", 1)
     place = placement(chunks, half, x.reshape(1), own_tokens)
-    placed = placed_hidden(chunks, other_chunks, gate, up, place, gy.reshape(1))
+    placed = placed_hidden(own_value, other_value, place)
 
     gathered = lax.all_gather(placed, "zo", axis=0, tiled=True)
 

time: 321 us -> 323 us (level)
  blocking collectives: 210 us -> 178 us
  waiting for transfers between devices: 15.6 us -> 31.6 us
  starting transfers between devices: 69.7 us -> 82.9 us
    all_gather x1, blocking collectives: 118 us -> 84.1 us  [block(): column = lax.all_gather(wide, ('zo', 'zi'), axis=0, tiled=True)]
    ppermute x8 -> x6, waiting for transfers between devices: 2.38 us -> 18.4 us  [shifted(): lax.ppermute(value, axis, [(i, (i + by) % count) for i in range(count)])]
    ppermute x8 -> x6, starting transfers between devices: 48.1 us -> 61.5 us  [shifted(): lax.ppermute(value, axis, [(i, (i + by) % count) for i in range(count)])]
    pallas_call x1 -> x3, Pallas kernels: 9.02 us -> 11.8 us  [the longest x1 6.71 us: values(): pl.pallas_call(values_kernel, grid=(steps,), in_specs=[pl.BlockSpec((coun...]
  transfers between devices with their start and end apart: 10 -> 8, of which waited for: 3 -> 5; matrix products, arithmetic and copies ran while one was open for 0% -> 0% of each run, Pallas kernels for 3% -> 4%
where the time goes in v5:
time: 323 us; the launch traced here: 321 us
  blocking collectives  178 us (55%)
  starting transfers between devices  82.9 us (26%)
  waiting for transfers between devices  31.6 us (10%)
  Pallas kernels  20.2 us (6%)
  local copies, waits for them, and re-layouts  4.58 us (1%)
    all_gather x1, blocking collectives, block(): column = lax.all_gather(wide, ('zo', 'zi'), axis=0, tiled=True)  84.1 us
    ppermute x6, starting transfers between devices, shifted(): lax.ppermute(value, axis, [(i, (i + by) % count) for i in range(count)])  61.5 us
    all_to_all x2, blocking collectives, exchanged(): return lax.all_to_all(blocks, axes, split_axis=0, concat_axis=0, tiled=True)  50.5 us
    all_gather x1, blocking collectives, block(): gathered = lax.all_gather(placed, 'zo', axis=0, tiled=True)  43.9 us
    all_to_all x2, starting transfers between devices, exchanged(): return lax.all_to_all(blocks, axes, split_axis=0, concat_axis=0, tiled=True)  21.4 us
    ppermute x6, waiting for transfers between devices, shifted(): lax.ppermute(value, axis, [(i, (i + by) % count) for i in range(count)])  18.4 us
    all_to_all x2, waiting for transfers between devices, exchanged(): return lax.all_to_all(blocks, axes, split_axis=0, concat_axis=0, tiled=True)  13.3 us
    pallas_call x1, Pallas kernels, values(): pl.pallas_call(values_kernel, grid=(steps,), in_specs=[pl.BlockSpec((coun...  6.71 us
  transfers between devices with their start and end apart: 8, of which 5 were waited for; matrix products, arithmetic and copies ran while one was open for 0% of the time, Pallas kernels for 4%

profile of v5, /device:TPU:33, one launch (start us, length us, event | category | flops | bytes accessed | tf_op | source)
XLA Modules:
  0.0 320.7 jit_solution(14934532981303060105)
XLA Ops:
  0.0 2.3 cut_by_x.1
  2.3 5.1 %all-to-all-start = ((bf16[4,64,3328]{2,1,0:T(8,128)(2,1)}), bf16[4,64,3328]{2,1,0:T(8,128)(2,1)S(1)}, u32[]{:S(2)}, u32[]{:S(2)}) async-start(bf16[4,64,3328]{2,1,0:T(8,128)(2,1)} %cut_by_x.1), calls=%async_computation | async-start | bytes 3407872 | tf_op jit(solution)/shard_map/all_to_all | solution.py:29
  7.4 13.3 %all-to-all-done.rows_ref = bf16[4,64,3328]{2,1,0:T(8,128)(2,1)S(1)} async-done(((bf16[4,64,3328]{2,1,0:T(8,128)(2,1)}), bf16[4,64,3328]{2,1,0:T(8,128)(2,1)S(1)}, u32[]{:S(2)}, u32[]{:S(2)}) %all-to-all-start) | async-done | bytes 1703968 | tf_op jit(solution)/shard_map/all_to_all | solution.py:29
  20.7 0.0 copy-start.1
  20.7 1.2 copy-done.1
  21.9 4.2 %cut_by_zi.1 = bf16[4,4,64,832]{3,2,1,0:T(8,128)(2,1)} custom-call(s32[1]{0:T(128)} %bitcast.1.gy_ref, bf16[4,64,3328]{2,1,0:T(8,128)(2,1)} %copy-done.1), custom_call_target="tpu_custom_call" | custom-call | tf_op jit(solution)/shard_map/cut_by_zi/pallas_call | solution.py:112
  26.1 16.3 %all-to-all-start.1 = ((bf16[4,4,64,832]{3,2,1,0:T(8,128)(2,1)}), bf16[4,4,64,832]{3,2,1,0:T(8,128)(2,1)}, u32[]{:S(2)}, u32[]{:S(2)}) async-start(bf16[4,4,64,832]{3,2,1,0:T(8,128)(2,1)} %cut_by_zi.1), calls=%async_computation.1 | async-start | bytes 3670016 | tf_op jit(solution)/shard_map/all_to_all | solution.py:29
  42.4 0.0 copy-start.7
  42.4 0.0 copy-start.6
  42.4 3.1 split_rows.1
  45.5 31.2 %collective-permute-start.3 = (bf16[208,4096]{1,0:T(8,128)(2,1)}, bf16[208,4096]{1,0:T(8,128)(2,1)}, u32[]{:S(2)}, u32[]{:S(2)}) collective-permute-start(bf16[208,4096]{1,0:T(8,128)(2,1)} %bitcast.28), channel_id=1, source_target_pairs={{0,1},{1,0},{2,3},{3,2},{4,5},{5,4},{6,7},{7,6},{8,9},{9,8},{10,11... | collective-permute-start | bytes 5111816 | tf_op jit(solution)/shard_map/ppermute | solution.py:25
  76.7 0.0 copy-done.7
  76.7 0.1 broadcast_in_dim.2
  76.8 0.0 copy-done.6
  76.8 84.1 %all-gather = bf16[32,3,4224]{2,1,0:T(4,128)(2,1)S(1)} all-gather(bf16[1,3,4224]{2,1,0:T(4,128)(2,1)S(1)} %maximum_bitcast_fusion), channel_id=1, replica_groups=mesh['rep'=2,'x'=4,'zo'=8,'zi'=4,'gy'=2] {'zo','zi'}, dimensions={0}, use_global_device_ids=true | all-gather | bytes 836352 | tf_op jit(solution)/shard_map/all_gather | solution.py:216
  160.9 0.7 reshape.39.refs_0_
  161.6 0.0 copy-start
  161.6 2.2 collective-permute-start
  163.9 4.3 %collective-permute-start.1 = (bf16[96,4224]{1,0:T(8,128)(2,1)S(1)}, bf16[96,4224]{1,0:T(8,128)(2,1)S(1)}, u32[]{:S(2)}, u32[]{:S(2)}) collective-permute-start(bf16[96,4224]{1,0:T(8,128)(2,1)S(1)} %reshape.39.refs_0_), channel_id=1, source_target_pairs={{0,192},{64,0},{128,64},{192,128},{1,193},{65,1},{129,65},{193,129... | collective-permute-start | bytes 2433032 | tf_op jit(solution)/shard_map/ppermute | solution.py:25
  168.2 2.0 collective-permute-start.2
  170.2 13.1 %collective-permute-done.refs_1_ = bf16[96,4224]{1,0:T(8,128)(2,1)S(1)} collective-permute-done((bf16[96,4224]{1,0:T(8,128)(2,1)S(1)}, bf16[96,4224]{1,0:T(8,128)(2,1)S(1)}, u32[]{:S(2)}, u32[]{:S(2)}) %collective-permute-start) | collective-permute-done | bytes 811040 | tf_op jit(solution)/shard_map/ppermute | solution.py:25
  183.3 0.0 copy-start.2
  183.3 2.2 collective-permute-done.1.refs_2_
  185.5 1.2 collective-permute-done.2.refs_3_
  186.7 0.0 collective-permute-done.3.refs_5_
  186.7 0.0 copy-done
  186.7 0.0 copy-done.2
  186.7 0.0 copy-done.3
  186.7 0.9 copy-done.4
  187.6 6.7 %values.1 = (f32[208,384]{1,0:T(8,128)}, f32[208,384]{1,0:T(8,128)}) custom-call(bf16[96,4224]{1,0:T(8,128)(2,1)} %copy-done, bf16[96,4224]{1,0:T(8,128)(2,1)} %copy-done.2, bf16[96,4224]{1,0:T(8,128)(2,1)} %copy-done.3, bf16[96,4224]{1,0:T(8,128)(2,1)} %copy-done.4, bf16[208,4096]{1,0:T(8,128)(2,1)} %bitcast.25, ...), custom_call_target="tpu_custom_call" | custom-call | tf_op jit(solution)/shard_map/values/pallas_call | solution.py:183
  194.3 19.4 %collective-permute-start.4 = (f32[208,384]{1,0:T(8,128)}, f32[208,384]{1,0:T(8,128)S(1)}, u32[]{:S(2)}, u32[]{:S(2)}) collective-permute-start(f32[208,384]{1,0:T(8,128)} %get-tuple-element.12), channel_id=1, source_target_pairs={{0,1},{1,0},{2,3},{3,2},{4,5},{5,4},{6,7},{7,6},{8,9},{9,8},{10,11... | collective-permute-start | bytes 958472 | tf_op jit(solution)/shard_map/ppermute | solution.py:25
  213.7 1.9 placement.1.place_ref
  215.6 0.0 collective-permute-done.4.other_ref
  215.6 0.7 copy-done.5
  216.3 2.0 placed_hidden.1
  218.3 43.9 %all_gather.7 = bf16[832,384]{1,0:T(8,128)(2,1)S(1)} all-gather(bf16[104,384]{1,0:T(8,128)(2,1)} %placed_hidden.1), channel_id=1, replica_groups=mesh['rep'=2,'x'=4,'zo'=8,'zi'=4,'gy'=2] {'zo'}, dimensions={0}, use_global_device_ids=true | all-gather | bytes 718848 | tf_op jit(solution)/shard_map/all_gather | solution.py:232
  262.2 0.0 all-to-all-done.1
  262.2 2.5 fusion.2
  264.7 0.1 fusion.1
  264.9 0.1 pad_maximum_fusion
  264.9 2.4 collective-permute-start.5
  267.3 1.9 collective-permute-done.5
  269.2 0.1 fusion
  269.3 18.2 %all_to_all.20 = bf16[16,24,512]{2,1,0:T(8,128)(2,1)S(1)} all-to-all(bf16[16,24,512]{2,1,0:T(8,128)(2,1)S(1)} %bitcast.26), channel_id=1, replica_groups=mesh['rep'=2,'x'=4,'zo'=8,'zi'=4,'gy'=2] {'x','zi'}, dimensions={0} | all-to-all | bytes 786432 | tf_op jit(solution)/shard_map/all_to_all | solution.py:29
  287.5 0.1 reduce_sum.12
  287.6 32.3 %all_to_all.21 = bf16[8,3,512]{2,1,0:T(4,128)(2,1)S(1)} all-to-all(bf16[8,3,512]{2,1,0:T(4,128)(2,1)S(1)} %reshape.35), channel_id=1, replica_groups=mesh['rep'=2,'x'=4,'zo'=8,'zi'=4,'gy'=2] {'zo'}, dimensions={0} | all-to-all | bytes 49152 | tf_op jit(solution)/shard_map/all_to_all | solution.py:29
  319.9 0.1 reshape.36
  320.0 0.7 reshape.37
  (8 shorter events, 0.1 us)
Async XLA Ops:
  2.3 18.4 %all-to-all-start = ((bf16[4,64,3328]{2,1,0:T(8,128)(2,1)}), bf16[4,64,3328]{2,1,0:T(8,128)(2,1)S(1)}, u32[]{:S(2)}, u32[]{:S(2)}) async-start(bf16[4,64,3328]{2,1,0:T(8,128)(2,1)} %cut_by_x.1), calls=%async_computation | async-start | bytes 3407872 | tf_op jit(solution)/shard_map/all_to_all | solution.py:29
  20.7 1.2 copy-start.1
  26.1 236.1 %all-to-all-start.1 = ((bf16[4,4,64,832]{3,2,1,0:T(8,128)(2,1)}), bf16[4,4,64,832]{3,2,1,0:T(8,128)(2,1)}, u32[]{:S(2)}, u32[]{:S(2)}) async-start(bf16[4,4,64,832]{3,2,1,0:T(8,128)(2,1)} %cut_by_zi.1), calls=%async_computation.1 | async-start | bytes 3670016 | tf_op jit(solution)/shard_map/all_to_all | solution.py:29
  42.4 34.3 %copy-start.7 = (s32[3]{0:T(128)S(1)}, s32[3]{0:T(128)}, u32[]{:S(2)}) copy-start(s32[3]{0:T(128)} %param.7) | copy-start | bytes 40
  42.4 34.4 %copy-start.6 = (bf16[3,4096]{1,0:T(4,128)(2,1)S(1)}, bf16[3,4096]{1,0:T(4,128)(2,1)}, u32[]{:S(2)}) copy-start(bf16[3,4096]{1,0:T(4,128)(2,1)} %param.6) | copy-start | bytes 73732
  45.5 141.2 %collective-permute-start.3 = (bf16[208,4096]{1,0:T(8,128)(2,1)}, bf16[208,4096]{1,0:T(8,128)(2,1)}, u32[]{:S(2)}, u32[]{:S(2)}) collective-permute-start(bf16[208,4096]{1,0:T(8,128)(2,1)} %bitcast.28), channel_id=1, source_target_pairs={{0,1},{1,0},{2,3},{3,2},{4,5},{5,4},{6,7},{7,6},{8,9},{9,8},{10,11... | collective-permute-start | bytes 5111816 | tf_op jit(solution)/shard_map/ppermute | solution.py:25
  161.6 25.0 %copy-start = (bf16[96,4224]{1,0:T(8,128)(2,1)}, bf16[96,4224]{1,0:T(8,128)(2,1)S(1)}, u32[]{:S(2)}) copy-start(bf16[96,4224]{1,0:T(8,128)(2,1)S(1)} %reshape.39.refs_0_) | copy-start | bytes 2433028
  161.6 21.6 %collective-permute-start = (bf16[96,4224]{1,0:T(8,128)(2,1)S(1)}, bf16[96,4224]{1,0:T(8,128)(2,1)S(1)}, u32[]{:S(2)}, u32[]{:S(2)}) collective-permute-start(bf16[96,4224]{1,0:T(8,128)(2,1)S(1)} %reshape.39.refs_0_), channel_id=1, source_target_pairs={{0,64},{64,128},{128,192},{192,0},{1,65},{65,129},{129,193},{193,1... | collective-permute-start | bytes 2433032 | tf_op jit(solution)/shard_map/ppermute | solution.py:25
  163.9 21.6 %collective-permute-start.1 = (bf16[96,4224]{1,0:T(8,128)(2,1)S(1)}, bf16[96,4224]{1,0:T(8,128)(2,1)S(1)}, u32[]{:S(2)}, u32[]{:S(2)}) collective-permute-start(bf16[96,4224]{1,0:T(8,128)(2,1)S(1)} %reshape.39.refs_0_), channel_id=1, source_target_pairs={{0,192},{64,0},{128,64},{192,128},{1,193},{65,1},{129,65},{193,129... | collective-permute-start | bytes 2433032 | tf_op jit(solution)/shard_map/ppermute | solution.py:25
  168.2 18.5 %collective-permute-start.2 = (bf16[96,4224]{1,0:T(8,128)(2,1)S(1)}, bf16[96,4224]{1,0:T(8,128)(2,1)S(1)}, u32[]{:S(2)}, u32[]{:S(2)}) collective-permute-start(bf16[96,4224]{1,0:T(8,128)(2,1)S(1)} %reshape.39.refs_0_), channel_id=1, source_target_pairs={{0,128},{64,192},{128,0},{192,64},{1,129},{65,193},{129,1},{193,65... | collective-permute-start | bytes 2433032 | tf_op jit(solution)/shard_map/ppermute | solution.py:25
  183.3 3.4 %copy-start.2 = (bf16[96,4224]{1,0:T(8,128)(2,1)}, bf16[96,4224]{1,0:T(8,128)(2,1)S(1)}, u32[]{:S(2)}) copy-start(bf16[96,4224]{1,0:T(8,128)(2,1)S(1)} %collective-permute-done.refs_1_) | copy-start | bytes 2433028
  185.5 1.2 copy-start.3
  186.7 0.9 copy-start.4
  194.3 21.3 %collective-permute-start.4 = (f32[208,384]{1,0:T(8,128)}, f32[208,384]{1,0:T(8,128)S(1)}, u32[]{:S(2)}, u32[]{:S(2)}) collective-permute-start(f32[208,384]{1,0:T(8,128)} %get-tuple-element.12), channel_id=1, source_target_pairs={{0,1},{1,0},{2,3},{3,2},{4,5},{5,4},{6,7},{7,6},{8,9},{9,8},{10,11... | collective-permute-start | bytes 958472 | tf_op jit(solution)/shard_map/ppermute | solution.py:25
  215.6 0.7 copy-start.5
  264.9 4.3 %collective-permute-start.5 = (f32[384,512]{1,0:T(8,128)S(1)}, f32[384,512]{1,0:T(8,128)S(1)}, u32[]{:S(2)}, u32[]{:S(2)}) collective-permute-start(f32[384,512]{1,0:T(8,128)S(1)} %pad_maximum_fusion), channel_id=1, source_target_pairs={{0,1},{1,0},{2,3},{3,2},{4,5},{5,4},{6,7},{7,6},{8,9},{9,8},{10,11... | collective-permute-start | bytes 2359304 | tf_op jit(solution)/shard_map/ppermute | solution.py:25

commit v6 on v5

--- a/solution.py
+++ b/solution.py
@@ -125,37 +125,44 @@
 
 
 def place_kernel(x_ref, *refs):
-    *kinds_refs, slot_ref, place_ref = refs
+    *kinds_refs, within_ref, within_row_ref, slot_ref, place_ref = refs
     chunk, count = kinds_refs[0].shape[0], slot_ref.shape[1]
-    starts = [lax.rem(x_ref[0] + X - by, X) * chunk for by in STEPS]
+    starts = [(lax.rem(x_ref[0] + X - by, X) * chunk).astype(F32) for by in STEPS]
     lane = lax.broadcasted_iota(jnp.int32, (1, count), 1)
-    order_row = lane + starts[0]
+    order_row = within_row_ref[...] + starts[0]
     for k in range(1, X):
-        order_row = jnp.where(lane < k * chunk, order_row, lane - k * chunk + starts[k])
+        order_row = jnp.where(lane < k * chunk, order_row, within_row_ref[...] + starts[k])
     kinds = jnp.concatenate([ref[...] for ref in kinds_refs], 0)
-    place = lax.broadcasted_iota(jnp.int32, (chunk, LANES), 0)
-    order = jnp.concatenate([place + start for start in starts], 0)
-    earlier = (order_row.astype(F32) < order[:, :1].astype(F32)).astype(BF16)
+    order = jnp.concatenate([within_ref[...] + start for start in starts], 0)
+    earlier = (order_row < order[:, :1]).astype(BF16)
     decode_before = jnp.dot(earlier, kinds, preferred_element_type=F32)
-    target = jnp.where(kinds.astype(F32) > 0.5, PREFILL + decode_before, order.astype(F32) - decode_before)
+    target = jnp.where(kinds.astype(F32) > 0.5, PREFILL + decode_before, order - decode_before)
     place_ref[...] = (target[:, :1] == slot_ref[...]).astype(BF16)
 
 
 def placement(chunks, half, x, own_tokens):
     chunk = chunks[0].shape[0]
     count = X * chunk
-    slot = np.arange(count).reshape(X, ZO, ZI, own_tokens).transpose(0, 2, 1, 3).reshape(1, count)
+    slot = np.arange(count, dtype=np.float32).reshape(X, ZO, ZI, own_tokens).transpose(0, 2, 1, 3)
+    within = slot[0].reshape(chunk)
     kinds = pl.BlockSpec((chunk, LANES), lambda i: (0, half // LANES))
+    row = pl.BlockSpec((1, count), lambda i: (0, 0))
     return pl.pallas_call(
         place_kernel,
         grid=(1,),
         in_specs=[pl.BlockSpec(memory_space=pltpu.SMEM)]
         + [kinds] * X
-        + [pl.BlockSpec((1, count), lambda i: (0, 0))],
+        + [pl.BlockSpec((chunk, LANES), lambda i: (0, 0)), row, row],
         out_specs=pl.BlockSpec((count, count), lambda i: (0, 0)),
         out_shape=jax.ShapeDtypeStruct((count, count), BF16),
         name="placement",
-    )(x, *chunks, slot.astype(np.float32))
+    )(
+        x,
+        *chunks,
+        np.broadcast_to(within[:, None], (chunk, LANES)).copy(),
+        np.tile(within, X).reshape(1, count),
+        slot.reshape(1, count),
+    )
 
 
 def values_kernel(*refs):
@@ -209,20 +216,22 @@
 def block(tokens, segment_ids, gate_weight, up_weight, down_weight):
     x, gy = lax.axis_index("x"), lax.axis_index("gy")
     own_tokens, half = tokens.shape
-    down = exchanged(cut_by_x(down_weight[0].T), "x")
-
     kinds = jnp.broadcast_to(segment_ids.astype(tokens.dtype)[:, None], (own_tokens, LANES))
     wide = jnp.concatenate([tokens, kinds], 1)
-    column = lax.all_gather(wide, ("zo", "zi"), axis=0, tiled=True)
-    gate, up = gate_weight[:, 0].T, up_weight[:, 0].T
+    copies = jnp.broadcast_to(wide, (ZO, *wide.shape))
+    strided = exchanged(copies, "zo").reshape(ZO * own_tokens, -1)
+
+    down = cut_by_x(down_weight[0].T)
+    down = exchanged(down, "x")
+    own_rows, other_rows = split_rows(gate_weight[:, 0].T, up_weight[:, 0].T, gy.reshape(1))
+    other_rows = shifted(other_rows, "gy", 1)
+
+    column = lax.all_gather(strided, "zi", axis=0, tiled=True)
     chunks = [column]
     for by in STEPS[1:]:
         chunks.append(shifted(column, "x", by))
     group = cut_by_zi(down, gy.reshape(1))
     group = exchanged(group, "zi")
-
-    own_rows, other_rows = split_rows(gate, up, gy.reshape(1))
-    other_rows = shifted(other_rows, "gy", 1)
 
     own_value, other_value = values(chunks, own_rows, other_rows)
     other_value = shifted(other_value, "gy", 1)

time: 323 us -> 337 us (1.043)
  waiting for transfers between devices: 31.6 us -> 70.3 us
  blocking collectives: 178 us -> 144 us
  starting transfers between devices: 82.9 us -> 94.1 us
    all_to_all x2 -> x3, starting transfers between devices: 21.4 us -> 69.8 us  [exchanged(): return lax.all_to_all(blocks, axes, split_axis=0, concat_axis=0, tiled=True)]
    ppermute x6, starting transfers between devices: 61.5 us -> 24.3 us  [shifted(): lax.ppermute(value, axis, [(i, (i + by) % count) for i in range(count)])]
    all_gather x1, blocking collectives: 84.1 us -> 49.5 us  [block(): column = lax.all_gather(strided, 'zi', axis=0, tiled=True)]
    all_to_all x2 -> x3, waiting for transfers between devices: 13.3 us -> 38.2 us  [exchanged(): return lax.all_to_all(blocks, axes, split_axis=0, concat_axis=0, tiled=True)]
    ppermute x6, waiting for transfers between devices: 18.4 us -> 32.1 us  [shifted(): lax.ppermute(value, axis, [(i, (i + by) % count) for i in range(count)])]
  transfers between devices with their start and end apart: 8 -> 9, of which waited for: 5 -> 6; matrix products, arithmetic and copies ran while one was open for 0% -> 0% of each run, Pallas kernels for 4% -> 5%
where the time goes in v6:
time: 337 us; the launch traced here: 335 us
  blocking collectives  144 us (43%)
  starting transfers between devices  94.1 us (28%)
  waiting for transfers between devices  70.3 us (21%)
  Pallas kernels  20.2 us (6%)
  local copies, waits for them, and re-layouts  3.8 us (1%)
    all_to_all x3, starting transfers between devices, exchanged(): return lax.all_to_all(blocks, axes, split_axis=0, concat_axis=0, tiled=True)  69.8 us
    all_to_all x2, blocking collectives, exchanged(): return lax.all_to_all(blocks, axes, split_axis=0, concat_axis=0, tiled=True)  52.3 us
    all_gather x1, blocking collectives, block(): column = lax.all_gather(strided, 'zi', axis=0, tiled=True)  49.5 us
    all_gather x1, blocking collectives, block(): gathered = lax.all_gather(placed, 'zo', axis=0, tiled=True)  41.6 us
    all_to_all x3, waiting for transfers between devices, exchanged(): return lax.all_to_all(blocks, axes, split_axis=0, concat_axis=0, tiled=True)  38.2 us
    ppermute x6, waiting for transfers between devices, shifted(): lax.ppermute(value, axis, [(i, (i + by) % count) for i in range(count)])  32.1 us
    ppermute x6, starting transfers between devices, shifted(): lax.ppermute(value, axis, [(i, (i + by) % count) for i in range(count)])  24.3 us
  transfers between devices with their start and end apart: 9, of which 6 were waited for; matrix products, arithmetic and copies ran while one was open for 0% of the time, Pallas kernels for 5%

profile of v6, /device:TPU:33, one launch (start us, length us, event | category | flops | bytes accessed | tf_op | source)
XLA Modules:
  0.0 334.9 jit_solution(1905399865621145326)
XLA Ops:
  0.0 2.3 cut_by_x.1
  2.3 0.0 copy-start.7
  2.3 0.0 copy-start.6
  2.3 5.1 %all-to-all-start.1 = ((bf16[4,64,3328]{2,1,0:T(8,128)(2,1)}), bf16[4,64,3328]{2,1,0:T(8,128)(2,1)S(1)}, u32[]{:S(2)}, u32[]{:S(2)}) async-start(bf16[4,64,3328]{2,1,0:T(8,128)(2,1)} %cut_by_x.1), calls=%async_computation.1 | async-start | bytes 3407872 | tf_op jit(solution)/shard_map/all_to_all | solution.py:29
  7.4 0.0 copy-done.7
  7.5 0.1 broadcast_in_dim.4
  7.5 0.0 copy-done.6
  7.6 13.1 %all-to-all-done.1.rows_ref = bf16[4,64,3328]{2,1,0:T(8,128)(2,1)S(1)} async-done(((bf16[4,64,3328]{2,1,0:T(8,128)(2,1)}), bf16[4,64,3328]{2,1,0:T(8,128)(2,1)S(1)}, u32[]{:S(2)}, u32[]{:S(2)}) %all-to-all-start.1) | async-done | bytes 1703968 | tf_op jit(solution)/shard_map/all_to_all | solution.py:29
  20.7 0.9 broadcast_in_dim.10
  21.6 51.2 %all-to-all-start = ((bf16[8,3,4224]{2,1,0:T(4,128)(2,1)}), bf16[8,3,4224]{2,1,0:T(4,128)(2,1)S(1)}, u32[]{:S(2)}, u32[]{:S(2)}) async-start(bf16[8,3,4224]{2,1,0:T(4,128)(2,1)} %broadcast_in_dim.10), calls=%async_computation | async-start | bytes 540672 | tf_op jit(solution)/shard_map/all_to_all | solution.py:29
  72.8 0.0 copy-done.1
  72.8 4.2 %cut_by_zi.1 = bf16[4,4,64,832]{3,2,1,0:T(8,128)(2,1)} custom-call(s32[1]{0:T(128)} %bitcast.gy_ref, bf16[4,64,3328]{2,1,0:T(8,128)(2,1)} %copy-done.1), custom_call_target="tpu_custom_call" | custom-call | tf_op jit(solution)/shard_map/cut_by_zi/pallas_call | solution.py:112
  77.0 25.0 %all-to-all-done = bf16[8,3,4224]{2,1,0:T(4,128)(2,1)S(1)} async-done(((bf16[8,3,4224]{2,1,0:T(4,128)(2,1)}), bf16[8,3,4224]{2,1,0:T(4,128)(2,1)S(1)}, u32[]{:S(2)}, u32[]{:S(2)}) %all-to-all-start) | async-done | bytes 202784 | tf_op jit(solution)/shard_map/all_to_all | solution.py:29
  102.1 13.5 %all-to-all-start.2 = ((bf16[4,4,64,832]{3,2,1,0:T(8,128)(2,1)}), bf16[4,4,64,832]{3,2,1,0:T(8,128)(2,1)}, u32[]{:S(2)}, u32[]{:S(2)}) async-start(bf16[4,4,64,832]{3,2,1,0:T(8,128)(2,1)} %cut_by_zi.1), calls=%async_computation.2 | async-start | bytes 3670016 | tf_op jit(solution)/shard_map/all_to_all | solution.py:29
  115.5 3.0 split_rows.1
  118.6 3.8 %collective-permute-start.3 = (bf16[208,4096]{1,0:T(8,128)(2,1)}, bf16[208,4096]{1,0:T(8,128)(2,1)}, u32[]{:S(2)}, u32[]{:S(2)}) collective-permute-start(bf16[208,4096]{1,0:T(8,128)(2,1)} %bitcast.26), channel_id=1, source_target_pairs={{0,1},{1,0},{2,3},{3,2},{4,5},{5,4},{6,7},{7,6},{8,9},{9,8},{10,11... | collective-permute-start | bytes 5111816 | tf_op jit(solution)/shard_map/ppermute | solution.py:25
  122.3 0.2 reshape.32
  122.5 49.5 %all_gather.6.refs_0_ = bf16[96,4224]{1,0:T(8,128)(2,1)S(1)} all-gather(bf16[24,4224]{1,0:T(8,128)(2,1)S(1)} %reshape.32), channel_id=1, replica_groups=mesh['rep'=2,'x'=4,'zo'=8,'zi'=4,'gy'=2] {'zi'}, dimensions={0}, use_global_device_ids=true | all-gather | bytes 1013760 | tf_op jit(solution)/shard_map/all_gather | solution.py:229
  172.1 2.2 collective-permute-start
  174.3 4.3 %collective-permute-start.1 = (bf16[96,4224]{1,0:T(8,128)(2,1)S(1)}, bf16[96,4224]{1,0:T(8,128)(2,1)S(1)}, u32[]{:S(2)}, u32[]{:S(2)}) collective-permute-start(bf16[96,4224]{1,0:T(8,128)(2,1)S(1)} %all_gather.6.refs_0_), channel_id=1, source_target_pairs={{0,192},{64,0},{128,64},{192,128},{1,193},{65,1},{129,65},{193,129... | collective-permute-start | bytes 2433032 | tf_op jit(solution)/shard_map/ppermute | solution.py:25
  178.6 2.0 collective-permute-start.2
  180.6 0.0 collective-permute-done.3.refs_5_
  180.6 14.0 %collective-permute-done.refs_1_ = bf16[96,4224]{1,0:T(8,128)(2,1)S(1)} collective-permute-done((bf16[96,4224]{1,0:T(8,128)(2,1)S(1)}, bf16[96,4224]{1,0:T(8,128)(2,1)S(1)}, u32[]{:S(2)}, u32[]{:S(2)}) %collective-permute-start) | collective-permute-done | bytes 811040 | tf_op jit(solution)/shard_map/ppermute | solution.py:25
  194.6 1.0 collective-permute-done.1.refs_2_
  195.6 15.2 %collective-permute-done.2.refs_3_ = bf16[96,4224]{1,0:T(8,128)(2,1)S(1)} collective-permute-done((bf16[96,4224]{1,0:T(8,128)(2,1)S(1)}, bf16[96,4224]{1,0:T(8,128)(2,1)S(1)}, u32[]{:S(2)}, u32[]{:S(2)}) %collective-permute-start.2) | collective-permute-done | bytes 811040 | tf_op jit(solution)/shard_map/ppermute | solution.py:25
  210.8 0.0 copy-done
  210.8 0.0 copy-done.2
  210.8 0.0 copy-done.3
  210.8 0.9 copy-done.4
  211.7 6.7 %values.1 = (f32[208,384]{1,0:T(8,128)}, f32[208,384]{1,0:T(8,128)}) custom-call(bf16[96,4224]{1,0:T(8,128)(2,1)} %copy-done, bf16[96,4224]{1,0:T(8,128)(2,1)} %copy-done.2, bf16[96,4224]{1,0:T(8,128)(2,1)} %copy-done.3, bf16[96,4224]{1,0:T(8,128)(2,1)} %copy-done.4, bf16[208,4096]{1,0:T(8,128)(2,1)} %bitcast.23, ...), custom_call_target="tpu_custom_call" | custom-call | tf_op jit(solution)/shard_map/values/pallas_call | solution.py:190
  218.5 5.6 %collective-permute-start.4 = (f32[208,384]{1,0:T(8,128)}, f32[208,384]{1,0:T(8,128)S(1)}, u32[]{:S(2)}, u32[]{:S(2)}) collective-permute-start(f32[208,384]{1,0:T(8,128)} %get-tuple-element.12), channel_id=1, source_target_pairs={{0,1},{1,0},{2,3},{3,2},{4,5},{5,4},{6,7},{7,6},{8,9},{9,8},{10,11... | collective-permute-start | bytes 958472 | tf_op jit(solution)/shard_map/ppermute | solution.py:25
  224.1 2.0 placement.1.place_ref
  226.1 0.0 collective-permute-done.4.other_ref
  226.1 0.7 copy-done.5
  226.8 2.0 placed_hidden.1
  228.9 41.6 %all_gather.7 = bf16[832,384]{1,0:T(8,128)(2,1)S(1)} all-gather(bf16[104,384]{1,0:T(8,128)(2,1)} %placed_hidden.1), channel_id=1, replica_groups=mesh['rep'=2,'x'=4,'zo'=8,'zi'=4,'gy'=2] {'zo'}, dimensions={0}, use_global_device_ids=true | all-gather | bytes 718848 | tf_op jit(solution)/shard_map/all_gather | solution.py:241
  270.5 0.0 all-to-all-done.2
  270.5 2.5 fusion.2
  273.0 0.1 fusion.1
  273.1 0.1 pad_maximum_fusion
  273.2 6.4 %collective-permute-start.5 = (f32[384,512]{1,0:T(8,128)S(1)}, f32[384,512]{1,0:T(8,128)S(1)}, u32[]{:S(2)}, u32[]{:S(2)}) collective-permute-start(f32[384,512]{1,0:T(8,128)S(1)} %pad_maximum_fusion), channel_id=1, source_target_pairs={{0,1},{1,0},{2,3},{3,2},{4,5},{5,4},{6,7},{7,6},{8,9},{9,8},{10,11... | collective-permute-start | bytes 2359304 | tf_op jit(solution)/shard_map/ppermute | solution.py:25
  279.6 1.9 collective-permute-done.5
  281.5 0.1 fusion
  281.6 17.5 %all_to_all.25 = bf16[16,24,512]{2,1,0:T(8,128)(2,1)S(1)} all-to-all(bf16[16,24,512]{2,1,0:T(8,128)(2,1)S(1)} %bitcast.24), channel_id=1, replica_groups=mesh['rep'=2,'x'=4,'zo'=8,'zi'=4,'gy'=2] {'x','zi'}, dimensions={0} | all-to-all | bytes 786432 | tf_op jit(solution)/shard_map/all_to_all | solution.py:29
  299.1 0.1 reduce_sum.12
  299.2 34.9 %all_to_all.26 = bf16[8,3,512]{2,1,0:T(4,128)(2,1)S(1)} all-to-all(bf16[8,3,512]{2,1,0:T(4,128)(2,1)S(1)} %reshape.39), channel_id=1, replica_groups=mesh['rep'=2,'x'=4,'zo'=8,'zi'=4,'gy'=2] {'zo'}, dimensions={0} | all-to-all | bytes 49152 | tf_op jit(solution)/shard_map/all_to_all | solution.py:29
  334.1 0.1 reshape.40
  334.2 0.7 reshape.41
  (11 shorter events, 0.1 us)
Async XLA Ops:
  2.3 5.2 %copy-start.7 = (s32[3]{0:T(128)S(1)}, s32[3]{0:T(128)}, u32[]{:S(2)}) copy-start(s32[3]{0:T(128)} %param.9) | copy-start | bytes 40
  2.3 5.2 %copy-start.6 = (bf16[3,4096]{1,0:T(4,128)(2,1)S(1)}, bf16[3,4096]{1,0:T(4,128)(2,1)}, u32[]{:S(2)}) copy-start(bf16[3,4096]{1,0:T(4,128)(2,1)} %param.8) | copy-start | bytes 73732
  2.3 18.4 %all-to-all-start.1 = ((bf16[4,64,3328]{2,1,0:T(8,128)(2,1)}), bf16[4,64,3328]{2,1,0:T(8,128)(2,1)S(1)}, u32[]{:S(2)}, u32[]{:S(2)}) async-start(bf16[4,64,3328]{2,1,0:T(8,128)(2,1)} %cut_by_x.1), calls=%async_computation.1 | async-start | bytes 3407872 | tf_op jit(solution)/shard_map/all_to_all | solution.py:29
  20.7 52.1 %copy-start.1 = (bf16[4,64,3328]{2,1,0:T(8,128)(2,1)}, bf16[4,64,3328]{2,1,0:T(8,128)(2,1)S(1)}, u32[]{:S(2)}) copy-start(bf16[4,64,3328]{2,1,0:T(8,128)(2,1)S(1)} %all-to-all-done.1.rows_ref) | copy-start | bytes 5111812
  21.6 80.5 %all-to-all-start = ((bf16[8,3,4224]{2,1,0:T(4,128)(2,1)}), bf16[8,3,4224]{2,1,0:T(4,128)(2,1)S(1)}, u32[]{:S(2)}, u32[]{:S(2)}) async-start(bf16[8,3,4224]{2,1,0:T(4,128)(2,1)} %broadcast_in_dim.10), calls=%async_computation | async-start | bytes 540672 | tf_op jit(solution)/shard_map/all_to_all | solution.py:29
  102.1 168.4 %all-to-all-start.2 = ((bf16[4,4,64,832]{3,2,1,0:T(8,128)(2,1)}), bf16[4,4,64,832]{3,2,1,0:T(8,128)(2,1)}, u32[]{:S(2)}, u32[]{:S(2)}) async-start(bf16[4,4,64,832]{3,2,1,0:T(8,128)(2,1)} %cut_by_zi.1), calls=%async_computation.2 | async-start | bytes 3670016 | tf_op jit(solution)/shard_map/all_to_all | solution.py:29
  118.6 62.0 %collective-permute-start.3 = (bf16[208,4096]{1,0:T(8,128)(2,1)}, bf16[208,4096]{1,0:T(8,128)(2,1)}, u32[]{:S(2)}, u32[]{:S(2)}) collective-permute-start(bf16[208,4096]{1,0:T(8,128)(2,1)} %bitcast.26), channel_id=1, source_target_pairs={{0,1},{1,0},{2,3},{3,2},{4,5},{5,4},{6,7},{7,6},{8,9},{9,8},{10,11... | collective-permute-start | bytes 5111816 | tf_op jit(solution)/shard_map/ppermute | solution.py:25
  172.1 38.8 %copy-start = (bf16[96,4224]{1,0:T(8,128)(2,1)}, bf16[96,4224]{1,0:T(8,128)(2,1)S(1)}, u32[]{:S(2)}) copy-start(bf16[96,4224]{1,0:T(8,128)(2,1)S(1)} %all_gather.6.refs_0_) | copy-start | bytes 2433028
  172.1 22.5 %collective-permute-start = (bf16[96,4224]{1,0:T(8,128)(2,1)S(1)}, bf16[96,4224]{1,0:T(8,128)(2,1)S(1)}, u32[]{:S(2)}, u32[]{:S(2)}) collective-permute-start(bf16[96,4224]{1,0:T(8,128)(2,1)S(1)} %all_gather.6.refs_0_), channel_id=1, source_target_pairs={{0,64},{64,128},{128,192},{192,0},{1,65},{65,129},{129,193},{193,1... | collective-permute-start | bytes 2433032 | tf_op jit(solution)/shard_map/ppermute | solution.py:25
  174.3 21.4 %collective-permute-start.1 = (bf16[96,4224]{1,0:T(8,128)(2,1)S(1)}, bf16[96,4224]{1,0:T(8,128)(2,1)S(1)}, u32[]{:S(2)}, u32[]{:S(2)}) collective-permute-start(bf16[96,4224]{1,0:T(8,128)(2,1)S(1)} %all_gather.6.refs_0_), channel_id=1, source_target_pairs={{0,192},{64,0},{128,64},{192,128},{1,193},{65,1},{129,65},{193,129... | collective-permute-start | bytes 2433032 | tf_op jit(solution)/shard_map/ppermute | solution.py:25
  178.6 32.2 %collective-permute-start.2 = (bf16[96,4224]{1,0:T(8,128)(2,1)S(1)}, bf16[96,4224]{1,0:T(8,128)(2,1)S(1)}, u32[]{:S(2)}, u32[]{:S(2)}) collective-permute-start(bf16[96,4224]{1,0:T(8,128)(2,1)S(1)} %all_gather.6.refs_0_), channel_id=1, source_target_pairs={{0,128},{64,192},{128,0},{192,64},{1,129},{65,193},{129,1},{193,65... | collective-permute-start | bytes 2433032 | tf_op jit(solution)/shard_map/ppermute | solution.py:25
  194.6 16.2 %copy-start.2 = (bf16[96,4224]{1,0:T(8,128)(2,1)}, bf16[96,4224]{1,0:T(8,128)(2,1)S(1)}, u32[]{:S(2)}) copy-start(bf16[96,4224]{1,0:T(8,128)(2,1)S(1)} %collective-permute-done.refs_1_) | copy-start | bytes 2433028
  195.6 15.2 %copy-start.3 = (bf16[96,4224]{1,0:T(8,128)(2,1)}, bf16[96,4224]{1,0:T(8,128)(2,1)S(1)}, u32[]{:S(2)}) copy-start(bf16[96,4224]{1,0:T(8,128)(2,1)S(1)} %collective-permute-done.1.refs_2_) | copy-start | bytes 2433028
  210.8 0.9 copy-start.4
  218.5 7.6 %collective-permute-start.4 = (f32[208,384]{1,0:T(8,128)}, f32[208,384]{1,0:T(8,128)S(1)}, u32[]{:S(2)}, u32[]{:S(2)}) collective-permute-start(f32[208,384]{1,0:T(8,128)} %get-tuple-element.12), channel_id=1, source_target_pairs={{0,1},{1,0},{2,3},{3,2},{4,5},{5,4},{6,7},{7,6},{8,9},{9,8},{10,11... | collective-permute-start | bytes 958472 | tf_op jit(solution)/shard_map/ppermute | solution.py:25
  226.1 0.7 copy-start.5
  273.2 8.3 %collective-permute-start.5 = (f32[384,512]{1,0:T(8,128)S(1)}, f32[384,512]{1,0:T(8,128)S(1)}, u32[]{:S(2)}, u32[]{:S(2)}) collective-permute-start(f32[384,512]{1,0:T(8,128)S(1)} %pad_maximum_fusion), channel_id=1, source_target_pairs={{0,1},{1,0},{2,3},{3,2},{4,5},{5,4},{6,7},{7,6},{8,9},{9,8},{10,11... | collective-permute-start | bytes 2359304 | tf_op jit(solution)/shard_map/ppermute | solution.py:25

commit v7 on v6

--- a/solution.py
+++ b/solution.py
@@ -42,31 +42,35 @@
         copy.wait()
 
 
-def cut_by_x_kernel(rows_ref, out_ref, held, in_sems, out_sems):
-    rows = out_ref.shape[2]
-    ins = [
-        pltpu.make_async_copy(rows_ref.at[:, pl.ds(k * rows, rows)], held.at[k], in_sems.at[k])
-        for k in range(X)
-    ]
-    outs = [pltpu.make_async_copy(held.at[k], out_ref.at[k], out_sems.at[k]) for k in range(X)]
-    pass_on(ins, outs)
-
-
-def cut_by_x(down):
+def cut_by_x_kernel(x_ref, rows_ref, *refs):
+    *outs, held, in_sems, out_sems = refs
+    rows = held.shape[2]
+    at = [pl.multiple_of(lax.rem(x_ref[0] + by, X) * rows, LANES) for by in STEPS]
+    pass_on(
+        [
+            pltpu.make_async_copy(rows_ref.at[:, pl.ds(at[k], rows)], held.at[k], in_sems.at[k])
+            for k in range(X)
+        ],
+        [pltpu.make_async_copy(held.at[k], outs[k], out_sems.at[k]) for k in range(X)],
+    )
+
+
+def cut_by_x(down, x):
     features, rows = down.shape
-    shape = (X, features, rows // X)
-    return pl.pallas_call(
+    out = jax.ShapeDtypeStruct((features, rows // X), down.dtype)
+    return list(
+        pl.pallas_call(
         cut_by_x_kernel,
-        in_specs=[HBM],
-        out_specs=HBM,
-        out_shape=jax.ShapeDtypeStruct(shape, down.dtype),
+        in_specs=[pl.BlockSpec(memory_space=pltpu.SMEM), HBM],
+        out_specs=[HBM] * X,
+        out_shape=[out] * X,
         scratch_shapes=[
-            pltpu.VMEM(shape, down.dtype),
+            pltpu.VMEM((X, *out.shape), down.dtype),
             pltpu.SemaphoreType.DMA((X,)),
             pltpu.SemaphoreType.DMA((X,)),
         ],
         name="cut_by_x",
-    )(down)
+    )(x, down))
 
 
 def split_kernel(gy_ref, gate_ref, up_ref, own_ref, other_ref, held, in_sems, out_sems):
@@ -100,28 +104,27 @@
     return own.reshape(2 * columns, -1), other.reshape(2 * columns, -1)
 
 
-def cut_kernel(depth, gy_ref, rows_ref, out_ref):
-    for zi in range(ZI):
-        pieces = [rows_ref[0, :, (zo * ZI + zi) * depth : (zo * ZI + zi + 1) * depth] for zo in range(ZO)]
-        out_ref[zi, 0] = jnp.concatenate(pieces, axis=1)
-
-
-def cut_by_zi(blocks, gy):
-    count, features, rows = blocks.shape
+def cut_by_zi_kernel(depth, x_ref, gy_ref, *refs):
+    *rows_refs, out_ref = refs
+    for by, rows_ref in zip(STEPS, rows_refs, strict=True):
+        position = lax.rem(x_ref[0] + 2 * X - by - gy_ref[0] * (X // 2), X)
+        for zi in range(ZI):
+            pieces = [rows_ref[:, (zo * ZI + zi) * depth : (zo * ZI + zi + 1) * depth] for zo in range(ZO)]
+            out_ref[zi, position] = jnp.concatenate(pieces, axis=1)
+
+
+def cut_by_zi(blocks, x, gy):
+    features, rows = blocks[0].shape
     depth = rows // (ZO * ZI)
-    return pl.pallas_call(
-        functools.partial(cut_kernel, depth),
-        grid_spec=pltpu.PrefetchScalarGridSpec(
-            num_scalar_prefetch=1,
-            grid=(count,),
-            in_specs=[
-                pl.BlockSpec((1, features, rows), lambda i, gy: (lax.rem(i + gy[0] * (X // 2), X), 0, 0))
-            ],
-            out_specs=pl.BlockSpec((ZI, 1, features, ZO * depth), lambda i, gy: (0, i, 0, 0)),
-        ),
-        out_shape=jax.ShapeDtypeStruct((ZI, count, features, ZO * depth), blocks.dtype),
+    scalar = pl.BlockSpec(memory_space=pltpu.SMEM)
+    whole = pl.BlockSpec(memory_space=pltpu.VMEM)
+    return pl.pallas_call(
+        functools.partial(cut_by_zi_kernel, depth),
+        in_specs=[scalar, scalar] + [whole] * X,
+        out_specs=whole,
+        out_shape=jax.ShapeDtypeStruct((ZI, X, features, ZO * depth), blocks[0].dtype),
         name="cut_by_zi",
-    )(gy, blocks)
+    )(x, gy, *blocks)
 
 
 def place_kernel(x_ref, *refs):
@@ -221,21 +224,24 @@
     copies = jnp.broadcast_to(wide, (ZO, *wide.shape))
     strided = exchanged(copies, "zo").reshape(ZO * own_tokens, -1)
 
-    down = cut_by_x(down_weight[0].T)
-    down = exchanged(down, "x")
-    own_rows, other_rows = split_rows(gate_weight[:, 0].T, up_weight[:, 0].T, gy.reshape(1))
+    x_at, gy_at = x.reshape(1), gy.reshape(1)
+    blocks = cut_by_x(down_weight[0].T, x_at)
+    for k in range(1, X):
+        blocks[k] = shifted(blocks[k], "x", STEPS[k])
+    own_rows, other_rows = split_rows(gate_weight[:, 0].T, up_weight[:, 0].T, gy_at)
     other_rows = shifted(other_rows, "gy", 1)
+    other_rows, *blocks = lax.optimization_barrier((other_rows, *blocks))
+    group = cut_by_zi(blocks, x_at, gy_at)
 
     column = lax.all_gather(strided, "zi", axis=0, tiled=True)
     chunks = [column]
     for by in STEPS[1:]:
         chunks.append(shifted(column, "x", by))
-    group = cut_by_zi(down, gy.reshape(1))
     group = exchanged(group, "zi")
 
     own_value, other_value = values(chunks, own_rows, other_rows)
     other_value = shifted(other_value, "gy", 1)
-    place = placement(chunks, half, x.reshape(1), own_tokens)
+    place = placement(chunks, half, x_at, own_tokens)
     placed = placed_hidden(own_value, other_value, place)
 
     gathered = lax.all_gather(placed, "zo", axis=0, tiled=True)
@@ -267,4 +273,6 @@
         ("rep", "x", "zo", "zi", "gy"),
     )
     placed = (P(REP_GX, "gy"), P(REP_GX), P(None, "gy", GX), P(None, "gy", GX), P("gy", None, GX))
-    return jax.shard_map(block, mesh=torus, in_specs=placed, out_specs=P(REP_GX, "gy"), check_vma=False)
+    return jax.shard_map(
+        block, mesh=torus, in_specs=placed, out_specs=P(REP_GX, "gy"), check_vma=False
+    )

time: 337 us -> 317 us (0.941)
  waiting for transfers between devices: 70.3 us -> 47.7 us
  blocking collectives: 144 us -> 149 us
    all_to_all x3 -> x2, starting transfers between devices: 69.8 us -> 14.8 us  [exchanged(): return lax.all_to_all(blocks, axes, split_axis=0, concat_axis=0, tiled=True)]
    ppermute x6 -> x9, starting transfers between devices: 24.3 us -> 77.1 us  [shifted(): lax.ppermute(value, axis, [(i, (i + by) % count) for i in range(count)])]
    all_to_all x3 -> x2, waiting for transfers between devices: 38.2 us -> 0.77 us  [exchanged(): return lax.all_to_all(blocks, axes, split_axis=0, concat_axis=0, tiled=True)]
    ppermute x6 -> x9, waiting for transfers between devices: 32.1 us -> 46.9 us  [shifted(): lax.ppermute(value, axis, [(i, (i + by) % count) for i in range(count)])]
    all_gather x1, blocking collectives: 49.5 us -> 56.3 us  [block(): column = lax.all_gather(strided, 'zi', axis=0, tiled=True)]
  transfers between devices with their start and end apart: 9 -> 11, of which waited for: 6 -> 8; matrix products, arithmetic and copies ran while one was open for 0% -> 0% of each run, Pallas kernels for 5% -> 5%
where the time goes in v7:
time: 317 us; the launch traced here: 315 us
  blocking collectives  149 us (47%)
  starting transfers between devices  91.9 us (29%)
  waiting for transfers between devices  47.7 us (15%)
  Pallas kernels  19.6 us (6%)
  local copies, waits for them, and re-layouts  4.36 us (1%)
    ppermute x9, starting transfers between devices, shifted(): lax.ppermute(value, axis, [(i, (i + by) % count) for i in range(count)])  77.1 us
    all_gather x1, blocking collectives, block(): column = lax.all_gather(strided, 'zi', axis=0, tiled=True)  56.3 us
    all_to_all x2, blocking collectives, exchanged(): return lax.all_to_all(blocks, axes, split_axis=0, concat_axis=0, tiled=True)  53.5 us
    ppermute x9, waiting for transfers between devices, shifted(): lax.ppermute(value, axis, [(i, (i + by) % count) for i in range(count)])  46.9 us
    all_gather x1, blocking collectives, block(): gathered = lax.all_gather(placed, 'zo', axis=0, tiled=True)  38.9 us
    all_to_all x2, starting transfers between devices, exchanged(): return lax.all_to_all(blocks, axes, split_axis=0, concat_axis=0, tiled=True)  14.8 us
    pallas_call x1, Pallas kernels, values(): pl.pallas_call(values_kernel, grid=(steps,), in_specs=[pl.BlockSpec((coun...  6.72 us
  transfers between devices with their start and end apart: 11, of which 8 were waited for; matrix products, arithmetic and copies ran while one was open for 0% of the time, Pallas kernels for 5%

profile of v7, /device:TPU:33, one launch (start us, length us, event | category | flops | bytes accessed | tf_op | source)
XLA Modules:
  0.0 315.2 jit_solution(487921030153005568)
XLA Ops:
  0.0 3.0 split_rows.1
  3.0 43.4 %collective-permute-start.3 = (bf16[208,4096]{1,0:T(8,128)(2,1)}, bf16[208,4096]{1,0:T(8,128)(2,1)S(1)}, u32[]{:S(2)}, u32[]{:S(2)}) collective-permute-start(bf16[208,4096]{1,0:T(8,128)(2,1)} %bitcast.26), channel_id=1, source_target_pairs={{0,1},{1,0},{2,3},{3,2},{4,5},{5,4},{6,7},{7,6},{8,9},{9,8},{10,11... | collective-permute-start | bytes 5111816 | tf_op jit(solution)/shard_map/ppermute | solution.py:25
  46.4 0.0 copy-done.10
  46.4 0.1 broadcast_in_dim.4
  46.5 0.8 broadcast_in_dim.10
  47.3 3.6 %all-to-all-start = ((bf16[8,3,4224]{2,1,0:T(4,128)(2,1)}), bf16[8,3,4224]{2,1,0:T(4,128)(2,1)S(1)}, u32[]{:S(2)}, u32[]{:S(2)}) async-start(bf16[8,3,4224]{2,1,0:T(4,128)(2,1)} %broadcast_in_dim.10), calls=%async_computation | async-start | bytes 540672 | tf_op jit(solution)/shard_map/all_to_all | solution.py:29
  50.9 2.3 cut_by_x.1
  53.2 2.8 collective-permute-start.4
  56.0 3.7 %collective-permute-start.5 = (bf16[64,3328]{1,0:T(8,128)(2,1)}, bf16[64,3328]{1,0:T(8,128)(2,1)S(1)}, u32[]{:S(2)}, u32[]{:S(2)}) collective-permute-start(bf16[64,3328]{1,0:T(8,128)(2,1)} %get-tuple-element.22), channel_id=1, source_target_pairs={{0,192},{64,0},{128,64},{192,128},{1,193},{65,1},{129,65},{193,129... | collective-permute-start | bytes 1277960 | tf_op jit(solution)/shard_map/ppermute | solution.py:25
  59.7 3.3 %collective-permute-start.6 = (bf16[64,3328]{1,0:T(8,128)(2,1)}, bf16[64,3328]{1,0:T(8,128)(2,1)S(1)}, u32[]{:S(2)}, u32[]{:S(2)}) collective-permute-start(bf16[64,3328]{1,0:T(8,128)(2,1)} %get-tuple-element.23), channel_id=1, source_target_pairs={{0,128},{64,192},{128,0},{192,64},{1,129},{65,193},{129,1},{193,65... | collective-permute-start | bytes 1277960 | tf_op jit(solution)/shard_map/ppermute | solution.py:25
  63.0 4.9 %collective-permute-done.4.refs_1_ = bf16[64,3328]{1,0:T(8,128)(2,1)S(1)} collective-permute-done((bf16[64,3328]{1,0:T(8,128)(2,1)}, bf16[64,3328]{1,0:T(8,128)(2,1)S(1)}, u32[]{:S(2)}, u32[]{:S(2)}) %collective-permute-start.4) | collective-permute-done | bytes 426016 | tf_op jit(solution)/shard_map/ppermute | solution.py:25
  67.9 1.4 collective-permute-done.5.refs_2_
  69.3 8.3 %collective-permute-done.6.refs_3_ = bf16[64,3328]{1,0:T(8,128)(2,1)S(1)} collective-permute-done((bf16[64,3328]{1,0:T(8,128)(2,1)}, bf16[64,3328]{1,0:T(8,128)(2,1)S(1)}, u32[]{:S(2)}, u32[]{:S(2)}) %collective-permute-start.6) | collective-permute-done | bytes 426016 | tf_op jit(solution)/shard_map/ppermute | solution.py:25
  77.6 0.0 collective-permute-done.3.refs_5_
  77.7 0.7 copy-done.7
  78.4 3.6 %cut_by_zi.1 = bf16[4,4,64,832]{3,2,1,0:T(8,128)(2,1)} custom-call(s32[1]{0:T(128)} %bitcast.7.x_ref, s32[1]{0:T(128)} %bitcast.gy_ref, bf16[64,3328]{1,0:T(8,128)(2,1)} %get-tuple-element.27.refs_0_, bf16[64,3328]{1,0:T(8,128)(2,1)} %copy-done.5, bf16[64,3328]{1,0:T(8,128)(2,1)} %copy-done.6, bf16[64,3328]{1,0:T(8,128)(2,1)} %copy-done.7), custom_call_target="tpu_custom_call" | custom-call | tf_op jit(solution)/shard_map/cut_by_zi/pallas_call | solution.py:121
  82.0 0.8 all-to-all-done
  82.8 11.2 %all-to-all-start.1 = ((bf16[4,4,64,832]{3,2,1,0:T(8,128)(2,1)}), bf16[4,4,64,832]{3,2,1,0:T(8,128)(2,1)}, u32[]{:S(2)}, u32[]{:S(2)}) async-start(bf16[4,4,64,832]{3,2,1,0:T(8,128)(2,1)} %cut_by_zi.1), calls=%async_computation.1 | async-start | bytes 3670016 | tf_op jit(solution)/shard_map/all_to_all | solution.py:29
  94.0 0.2 reshape.31
  94.2 56.3 %all_gather.6.refs_0_ = bf16[96,4224]{1,0:T(8,128)(2,1)S(1)} all-gather(bf16[24,4224]{1,0:T(8,128)(2,1)S(1)} %reshape.31), channel_id=1, replica_groups=mesh['rep'=2,'x'=4,'zo'=8,'zi'=4,'gy'=2] {'zi'}, dimensions={0}, use_global_device_ids=true | all-gather | bytes 1013760 | tf_op jit(solution)/shard_map/all_gather | solution.py:236
  150.5 2.9 collective-permute-start
  153.4 3.7 %collective-permute-start.1 = (bf16[96,4224]{1,0:T(8,128)(2,1)S(1)}, bf16[96,4224]{1,0:T(8,128)(2,1)S(1)}, u32[]{:S(2)}, u32[]{:S(2)}) collective-permute-start(bf16[96,4224]{1,0:T(8,128)(2,1)S(1)} %all_gather.6.refs_0_), channel_id=1, source_target_pairs={{0,192},{64,0},{128,64},{192,128},{1,193},{65,1},{129,65},{193,129... | collective-permute-start | bytes 2433032 | tf_op jit(solution)/shard_map/ppermute | solution.py:25
  157.0 3.4 %collective-permute-start.2 = (bf16[96,4224]{1,0:T(8,128)(2,1)S(1)}, bf16[96,4224]{1,0:T(8,128)(2,1)S(1)}, u32[]{:S(2)}, u32[]{:S(2)}) collective-permute-start(bf16[96,4224]{1,0:T(8,128)(2,1)S(1)} %all_gather.6.refs_0_), channel_id=1, source_target_pairs={{0,128},{64,192},{128,0},{192,64},{1,129},{65,193},{129,1},{193,65... | collective-permute-start | bytes 2433032 | tf_op jit(solution)/shard_map/ppermute | solution.py:25
  160.4 12.0 %collective-permute-done.refs_1_ = bf16[96,4224]{1,0:T(8,128)(2,1)S(1)} collective-permute-done((bf16[96,4224]{1,0:T(8,128)(2,1)S(1)}, bf16[96,4224]{1,0:T(8,128)(2,1)S(1)}, u32[]{:S(2)}, u32[]{:S(2)}) %collective-permute-start) | collective-permute-done | bytes 811040 | tf_op jit(solution)/shard_map/ppermute | solution.py:25
  172.4 1.4 collective-permute-done.1.refs_2_
  173.8 17.0 %collective-permute-done.2.refs_3_ = bf16[96,4224]{1,0:T(8,128)(2,1)S(1)} collective-permute-done((bf16[96,4224]{1,0:T(8,128)(2,1)S(1)}, bf16[96,4224]{1,0:T(8,128)(2,1)S(1)}, u32[]{:S(2)}, u32[]{:S(2)}) %collective-permute-start.2) | collective-permute-done | bytes 811040 | tf_op jit(solution)/shard_map/ppermute | solution.py:25
  190.8 0.0 copy-done
  190.8 0.0 copy-done.2
  190.8 0.9 copy-done.3
  191.7 6.7 %values.1 = (f32[208,384]{1,0:T(8,128)}, f32[208,384]{1,0:T(8,128)}) custom-call(bf16[96,4224]{1,0:T(8,128)(2,1)} %copy-done, bf16[96,4224]{1,0:T(8,128)(2,1)} %copy-done.1, bf16[96,4224]{1,0:T(8,128)(2,1)} %copy-done.2, bf16[96,4224]{1,0:T(8,128)(2,1)} %copy-done.3, bf16[208,4096]{1,0:T(8,128)(2,1)} %bitcast.23, bf16[208,4096]{1,0:T(8,128)(2,1)} %copy-done.4), custom_call_target="tpu_custom_call" | custom-call | tf_op jit(solution)/shard_map/values/pallas_call | solution.py:193
  198.4 4.1 %collective-permute-start.7 = (f32[208,384]{1,0:T(8,128)}, f32[208,384]{1,0:T(8,128)S(1)}, u32[]{:S(2)}, u32[]{:S(2)}) collective-permute-start(f32[208,384]{1,0:T(8,128)} %get-tuple-element.26), channel_id=1, source_target_pairs={{0,1},{1,0},{2,3},{3,2},{4,5},{5,4},{6,7},{7,6},{8,9},{9,8},{10,11... | collective-permute-start | bytes 958472 | tf_op jit(solution)/shard_map/ppermute | solution.py:25
  202.5 2.0 placement.1.place_ref
  204.5 0.0 collective-permute-done.7.other_ref
  204.5 0.7 copy-done.8
  205.2 2.0 placed_hidden.1
  207.2 38.9 %all_gather.7 = bf16[832,384]{1,0:T(8,128)(2,1)S(1)} all-gather(bf16[104,384]{1,0:T(8,128)(2,1)} %placed_hidden.1), channel_id=1, replica_groups=mesh['rep'=2,'x'=4,'zo'=8,'zi'=4,'gy'=2] {'zo'}, dimensions={0}, use_global_device_ids=true | all-gather | bytes 718848 | tf_op jit(solution)/shard_map/all_gather | solution.py:247
  246.1 0.0 all-to-all-done.1
  246.1 2.5 fusion.2
  248.6 0.1 fusion.1
  248.7 0.1 pad_maximum_fusion
  248.8 9.9 %collective-permute-start.8 = (f32[384,512]{1,0:T(8,128)S(1)}, f32[384,512]{1,0:T(8,128)S(1)}, u32[]{:S(2)}, u32[]{:S(2)}) collective-permute-start(f32[384,512]{1,0:T(8,128)S(1)} %pad_maximum_fusion), channel_id=1, source_target_pairs={{0,1},{1,0},{2,3},{3,2},{4,5},{5,4},{6,7},{7,6},{8,9},{9,8},{10,11... | collective-permute-start | bytes 2359304 | tf_op jit(solution)/shard_map/ppermute | solution.py:25
  258.7 1.9 collective-permute-done.8
  260.6 0.1 fusion
  260.7 21.0 %all_to_all.20 = bf16[16,24,512]{2,1,0:T(8,128)(2,1)S(1)} all-to-all(bf16[16,24,512]{2,1,0:T(8,128)(2,1)S(1)} %bitcast.24), channel_id=1, replica_groups=mesh['rep'=2,'x'=4,'zo'=8,'zi'=4,'gy'=2] {'x','zi'}, dimensions={0} | all-to-all | bytes 786432 | tf_op jit(solution)/shard_map/all_to_all | solution.py:29
  281.7 0.1 reduce_sum.12
  281.8 32.5 %all_to_all.21 = bf16[8,3,512]{2,1,0:T(4,128)(2,1)S(1)} all-to-all(bf16[8,3,512]{2,1,0:T(4,128)(2,1)S(1)} %reshape.38), channel_id=1, replica_groups=mesh['rep'=2,'x'=4,'zo'=8,'zi'=4,'gy'=2] {'zo'}, dimensions={0} | all-to-all | bytes 49152 | tf_op jit(solution)/shard_map/all_to_all | solution.py:29
  314.3 0.1 reshape.39
  314.5 0.7 reshape.40
  (21 shorter events, 0.1 us)
Async XLA Ops:
  0.0 46.4 %copy-start.10 = (s32[3]{0:T(128)S(1)}, s32[3]{0:T(128)}, u32[]{:S(2)}) copy-start(s32[3]{0:T(128)} %param.9) | copy-start | bytes 40
  0.0 46.5 %copy-start.9 = (bf16[3,4096]{1,0:T(4,128)(2,1)S(1)}, bf16[3,4096]{1,0:T(4,128)(2,1)}, u32[]{:S(2)}) copy-start(bf16[3,4096]{1,0:T(4,128)(2,1)} %param.8) | copy-start | bytes 73732
  3.0 74.6 %collective-permute-start.3 = (bf16[208,4096]{1,0:T(8,128)(2,1)}, bf16[208,4096]{1,0:T(8,128)(2,1)S(1)}, u32[]{:S(2)}, u32[]{:S(2)}) collective-permute-start(bf16[208,4096]{1,0:T(8,128)(2,1)} %bitcast.26), channel_id=1, source_target_pairs={{0,1},{1,0},{2,3},{3,2},{4,5},{5,4},{6,7},{7,6},{8,9},{9,8},{10,11... | collective-permute-start | bytes 5111816 | tf_op jit(solution)/shard_map/ppermute | solution.py:25
  47.3 35.5 %all-to-all-start = ((bf16[8,3,4224]{2,1,0:T(4,128)(2,1)}), bf16[8,3,4224]{2,1,0:T(4,128)(2,1)S(1)}, u32[]{:S(2)}, u32[]{:S(2)}) async-start(bf16[8,3,4224]{2,1,0:T(4,128)(2,1)} %broadcast_in_dim.10), calls=%async_computation | async-start | bytes 540672 | tf_op jit(solution)/shard_map/all_to_all | solution.py:29
  53.2 14.7 %collective-permute-start.4 = (bf16[64,3328]{1,0:T(8,128)(2,1)}, bf16[64,3328]{1,0:T(8,128)(2,1)S(1)}, u32[]{:S(2)}, u32[]{:S(2)}) collective-permute-start(bf16[64,3328]{1,0:T(8,128)(2,1)} %get-tuple-element.21), channel_id=1, source_target_pairs={{0,64},{64,128},{128,192},{192,0},{1,65},{65,129},{129,193},{193,1... | collective-permute-start | bytes 1277960 | tf_op jit(solution)/shard_map/ppermute | solution.py:25
  56.0 13.3 %collective-permute-start.5 = (bf16[64,3328]{1,0:T(8,128)(2,1)}, bf16[64,3328]{1,0:T(8,128)(2,1)S(1)}, u32[]{:S(2)}, u32[]{:S(2)}) collective-permute-start(bf16[64,3328]{1,0:T(8,128)(2,1)} %get-tuple-element.22), channel_id=1, source_target_pairs={{0,192},{64,0},{128,64},{192,128},{1,193},{65,1},{129,65},{193,129... | collective-permute-start | bytes 1277960 | tf_op jit(solution)/shard_map/ppermute | solution.py:25
  59.7 17.9 %collective-permute-start.6 = (bf16[64,3328]{1,0:T(8,128)(2,1)}, bf16[64,3328]{1,0:T(8,128)(2,1)S(1)}, u32[]{:S(2)}, u32[]{:S(2)}) collective-permute-start(bf16[64,3328]{1,0:T(8,128)(2,1)} %get-tuple-element.23), channel_id=1, source_target_pairs={{0,128},{64,192},{128,0},{192,64},{1,129},{65,193},{129,1},{193,65... | collective-permute-start | bytes 1277960 | tf_op jit(solution)/shard_map/ppermute | solution.py:25
  67.9 9.8 %copy-start.5 = (bf16[64,3328]{1,0:T(8,128)(2,1)}, bf16[64,3328]{1,0:T(8,128)(2,1)S(1)}, u32[]{:S(2)}) copy-start(bf16[64,3328]{1,0:T(8,128)(2,1)S(1)} %collective-permute-done.4.refs_1_) | copy-start | bytes 1277956
  69.3 8.3 %copy-start.6 = (bf16[64,3328]{1,0:T(8,128)(2,1)}, bf16[64,3328]{1,0:T(8,128)(2,1)S(1)}, u32[]{:S(2)}) copy-start(bf16[64,3328]{1,0:T(8,128)(2,1)S(1)} %collective-permute-done.5.refs_2_) | copy-start | bytes 1277956
  77.6 0.7 copy-start.7
  77.6 4.4 %copy-start.4 = (bf16[208,4096]{1,0:T(8,128)(2,1)}, bf16[208,4096]{1,0:T(8,128)(2,1)S(1)}, u32[]{:S(2)}) copy-start(bf16[208,4096]{1,0:T(8,128)(2,1)S(1)} %collective-permute-done.3.refs_5_) | copy-start | bytes 5111812
  82.8 163.3 %all-to-all-start.1 = ((bf16[4,4,64,832]{3,2,1,0:T(8,128)(2,1)}), bf16[4,4,64,832]{3,2,1,0:T(8,128)(2,1)}, u32[]{:S(2)}, u32[]{:S(2)}) async-start(bf16[4,4,64,832]{3,2,1,0:T(8,128)(2,1)} %cut_by_zi.1), calls=%async_computation.1 | async-start | bytes 3670016 | tf_op jit(solution)/shard_map/all_to_all | solution.py:29
  150.5 40.3 %copy-start = (bf16[96,4224]{1,0:T(8,128)(2,1)}, bf16[96,4224]{1,0:T(8,128)(2,1)S(1)}, u32[]{:S(2)}) copy-start(bf16[96,4224]{1,0:T(8,128)(2,1)S(1)} %all_gather.6.refs_0_) | copy-start | bytes 2433028
  150.5 21.9 %collective-permute-start = (bf16[96,4224]{1,0:T(8,128)(2,1)S(1)}, bf16[96,4224]{1,0:T(8,128)(2,1)S(1)}, u32[]{:S(2)}, u32[]{:S(2)}) collective-permute-start(bf16[96,4224]{1,0:T(8,128)(2,1)S(1)} %all_gather.6.refs_0_), channel_id=1, source_target_pairs={{0,64},{64,128},{128,192},{192,0},{1,65},{65,129},{129,193},{193,1... | collective-permute-start | bytes 2433032 | tf_op jit(solution)/shard_map/ppermute | solution.py:25
  153.4 20.4 %collective-permute-start.1 = (bf16[96,4224]{1,0:T(8,128)(2,1)S(1)}, bf16[96,4224]{1,0:T(8,128)(2,1)S(1)}, u32[]{:S(2)}, u32[]{:S(2)}) collective-permute-start(bf16[96,4224]{1,0:T(8,128)(2,1)S(1)} %all_gather.6.refs_0_), channel_id=1, source_target_pairs={{0,192},{64,0},{128,64},{192,128},{1,193},{65,1},{129,65},{193,129... | collective-permute-start | bytes 2433032 | tf_op jit(solution)/shard_map/ppermute | solution.py:25
  157.0 33.8 %collective-permute-start.2 = (bf16[96,4224]{1,0:T(8,128)(2,1)S(1)}, bf16[96,4224]{1,0:T(8,128)(2,1)S(1)}, u32[]{:S(2)}, u32[]{:S(2)}) collective-permute-start(bf16[96,4224]{1,0:T(8,128)(2,1)S(1)} %all_gather.6.refs_0_), channel_id=1, source_target_pairs={{0,128},{64,192},{128,0},{192,64},{1,129},{65,193},{129,1},{193,65... | collective-permute-start | bytes 2433032 | tf_op jit(solution)/shard_map/ppermute | solution.py:25
  172.4 18.4 %copy-start.1 = (bf16[96,4224]{1,0:T(8,128)(2,1)}, bf16[96,4224]{1,0:T(8,128)(2,1)S(1)}, u32[]{:S(2)}) copy-start(bf16[96,4224]{1,0:T(8,128)(2,1)S(1)} %collective-permute-done.refs_1_) | copy-start | bytes 2433028
  173.8 17.0 %copy-start.2 = (bf16[96,4224]{1,0:T(8,128)(2,1)}, bf16[96,4224]{1,0:T(8,128)(2,1)S(1)}, u32[]{:S(2)}) copy-start(bf16[96,4224]{1,0:T(8,128)(2,1)S(1)} %collective-permute-done.1.refs_2_) | copy-start | bytes 2433028
  190.8 0.9 copy-start.3
  198.4 6.1 %collective-permute-start.7 = (f32[208,384]{1,0:T(8,128)}, f32[208,384]{1,0:T(8,128)S(1)}, u32[]{:S(2)}, u32[]{:S(2)}) collective-permute-start(f32[208,384]{1,0:T(8,128)} %get-tuple-element.26), channel_id=1, source_target_pairs={{0,1},{1,0},{2,3},{3,2},{4,5},{5,4},{6,7},{7,6},{8,9},{9,8},{10,11... | collective-permute-start | bytes 958472 | tf_op jit(solution)/shard_map/ppermute | solution.py:25
  204.5 0.7 copy-start.8
  248.8 11.8 %collective-permute-start.8 = (f32[384,512]{1,0:T(8,128)S(1)}, f32[384,512]{1,0:T(8,128)S(1)}, u32[]{:S(2)}, u32[]{:S(2)}) collective-permute-start(f32[384,512]{1,0:T(8,128)S(1)} %pad_maximum_fusion), channel_id=1, source_target_pairs={{0,1},{1,0},{2,3},{3,2},{4,5},{5,4},{6,7},{7,6},{8,9},{9,8},{10,11... | collective-permute-start | bytes 2359304 | tf_op jit(solution)/shard_map/ppermute | solution.py:25

commit v8 on v7

--- a/solution.py
+++ b/solution.py
@@ -40,6 +40,28 @@
         leave.start()
     for copy in outs:
         copy.wait()
+
+
+def copies_kernel(kinds_ref, tokens_ref, out_ref):
+    count, half = tokens_ref.shape
+    row = lax.broadcasted_iota(jnp.int32, (count, LANES), 0)
+    kinds = jnp.zeros((count, LANES), F32)
+    for k in range(count):
+        kinds = jnp.where(row == k, kinds_ref[k].astype(F32), kinds)
+    for k in range(ZO):
+        out_ref[k, :, :half] = tokens_ref[...]
+        out_ref[k, :, half:] = kinds.astype(BF16)
+
+
+def token_copies(tokens, segment_ids):
+    count, half = tokens.shape
+    return pl.pallas_call(
+        copies_kernel,
+        in_specs=[pl.BlockSpec(memory_space=pltpu.SMEM), pl.BlockSpec(memory_space=pltpu.VMEM)],
+        out_specs=pl.BlockSpec(memory_space=pltpu.VMEM),
+        out_shape=jax.ShapeDtypeStruct((ZO, count, half + LANES), tokens.dtype),
+        name="token_copies",
+    )(segment_ids, tokens)
 
 
 def cut_by_x_kernel(x_ref, rows_ref, *refs):
@@ -58,8 +80,7 @@
 def cut_by_x(down, x):
     features, rows = down.shape
     out = jax.ShapeDtypeStruct((features, rows // X), down.dtype)
-    return list(
-        pl.pallas_call(
+    blocks = pl.pallas_call(
         cut_by_x_kernel,
         in_specs=[pl.BlockSpec(memory_space=pltpu.SMEM), HBM],
         out_specs=[HBM] * X,
@@ -70,7 +91,8 @@
             pltpu.SemaphoreType.DMA((X,)),
         ],
         name="cut_by_x",
-    )(x, down))
+    )(x, down)
+    return list(blocks)
 
 
 def split_kernel(gy_ref, gate_ref, up_ref, own_ref, other_ref, held, in_sems, out_sems):
@@ -171,29 +193,33 @@
 def values_kernel(*refs):
     *chunk_refs, own_rows_ref, other_rows_ref, own_ref, other_ref = refs
     step = pl.program_id(0)
+    columns = own_rows_ref.shape[0]
     chunks = jnp.concatenate([ref[...] for ref in chunk_refs], 0)
-    for rows, out in ((other_rows_ref, other_ref), (own_rows_ref, own_ref)):
-        term = lax.dot_general(rows[...], chunks, (((1,), (1,)), ((), ())), preferred_element_type=F32)
-
-        @pl.when(step == 0)
-        def _():
-            out[...] = term
-
-        @pl.when(step > 0)
-        def _():
-            out[...] += term
-
-
-def values(chunks, own_rows, other_rows, steps=4):
-    count, (columns, half) = chunks[0].shape[0], own_rows.shape
+    rows = jnp.concatenate([own_rows_ref[...], other_rows_ref[...]], 0)
+    term = lax.dot_general(rows, chunks, (((1,), (1,)), ((), ())), preferred_element_type=F32)
+
+    @pl.when(step == 0)
+    def _():
+        own_ref[...] = term[:columns]
+        other_ref[...] = term[columns:]
+
+    @pl.when(step > 0)
+    def _():
+        own_ref[...] += term[:columns]
+        other_ref[...] += term[columns:]
+
+
+def values(chunks, own_rows, other_rows, steps=2):
+    columns, half = own_rows.shape
+    count = sum(chunk.shape[0] for chunk in chunks)
     depth = half // steps
-    out = jax.ShapeDtypeStruct((columns, X * count), F32)
+    out = jax.ShapeDtypeStruct((columns, count), F32)
     rows = pl.BlockSpec((columns, depth), lambda i: (0, i))
     out_spec = pl.BlockSpec(out.shape, lambda i: (0, 0))
     return pl.pallas_call(
         values_kernel,
         grid=(steps,),
-        in_specs=[pl.BlockSpec((count, depth), lambda i: (0, i))] * X + [rows, rows],
+        in_specs=[pl.BlockSpec((chunk.shape[0], depth), lambda i: (0, i)) for chunk in chunks] + [rows, rows],
         out_specs=[out_spec, out_spec],
         out_shape=[out, out],
         name="values",
@@ -219,9 +245,7 @@
 def block(tokens, segment_ids, gate_weight, up_weight, down_weight):
     x, gy = lax.axis_index("x"), lax.axis_index("gy")
     own_tokens, half = tokens.shape
-    kinds = jnp.broadcast_to(segment_ids.astype(tokens.dtype)[:, None], (own_tokens, LANES))
-    wide = jnp.concatenate([tokens, kinds], 1)
-    copies = jnp.broadcast_to(wide, (ZO, *wide.shape))
+    copies = token_copies(tokens, segment_ids)
     strided = exchanged(copies, "zo").reshape(ZO * own_tokens, -1)
 
     x_at, gy_at = x.reshape(1), gy.reshape(1)

time: 317 us -> 316 us (level)
    pallas_call x1 -> x2, Pallas kernels: 6.72 us -> 6.48 us  [the longest x1 4.98 us: values(): pl.pallas_call(values_kernel, grid=(steps,), in_specs=[pl.BlockSpec((chun...]
where the time goes in v8:
time: 316 us; the launch traced here: 314 us
  blocking collectives  149 us (47%)
  starting transfers between devices  91.7 us (29%)
  waiting for transfers between devices  47.6 us (15%)
  Pallas kernels  19.4 us (6%)
  local copies, waits for them, and re-layouts  3.51 us (1%)
    ppermute x9, starting transfers between devices, shifted(): lax.ppermute(value, axis, [(i, (i + by) % count) for i in range(count)])  76.8 us
    all_gather x1, blocking collectives, block(): column = lax.all_gather(strided, 'zi', axis=0, tiled=True)  56.3 us
    all_to_all x2, blocking collectives, exchanged(): return lax.all_to_all(blocks, axes, split_axis=0, concat_axis=0, tiled=True)  53.9 us
    ppermute x9, waiting for transfers between devices, shifted(): lax.ppermute(value, axis, [(i, (i + by) % count) for i in range(count)])  46.9 us
    all_gather x1, blocking collectives, block(): gathered = lax.all_gather(placed, 'zo', axis=0, tiled=True)  39 us
    all_to_all x2, starting transfers between devices, exchanged(): return lax.all_to_all(blocks, axes, split_axis=0, concat_axis=0, tiled=True)  14.8 us
  transfers between devices with their start and end apart: 11, of which 8 were waited for; matrix products, arithmetic and copies ran while one was open for 0% of the time, Pallas kernels for 5%

profile of v8, /device:TPU:33, one launch (start us, length us, event | category | flops | bytes accessed | tf_op | source)
XLA Modules:
  0.0 314.3 jit_solution(5690437183859533905)
XLA Ops:
  0.0 3.0 split_rows.1
  3.0 43.4 %collective-permute-start.3 = (bf16[208,4096]{1,0:T(8,128)(2,1)}, bf16[208,4096]{1,0:T(8,128)(2,1)S(1)}, u32[]{:S(2)}, u32[]{:S(2)}) collective-permute-start(bf16[208,4096]{1,0:T(8,128)(2,1)} %bitcast.26), channel_id=1, source_target_pairs={{0,1},{1,0},{2,3},{3,2},{4,5},{5,4},{6,7},{7,6},{8,9},{9,8},{10,11... | collective-permute-start | bytes 5111816 | tf_op jit(solution)/shard_map/ppermute | solution.py:25
  46.4 1.5 token_copies.1
  47.8 3.6 %all-to-all-start = ((bf16[8,3,4224]{2,1,0:T(4,128)(2,1)}), bf16[8,3,4224]{2,1,0:T(4,128)(2,1)S(1)}, u32[]{:S(2)}, u32[]{:S(2)}) async-start(bf16[8,3,4224]{2,1,0:T(4,128)(2,1)} %token_copies.1), calls=%async_computation | async-start | bytes 540672 | tf_op jit(solution)/shard_map/all_to_all | solution.py:29
  51.5 2.3 cut_by_x.1
  53.8 2.8 collective-permute-start.4
  56.6 3.7 %collective-permute-start.5 = (bf16[64,3328]{1,0:T(8,128)(2,1)}, bf16[64,3328]{1,0:T(8,128)(2,1)S(1)}, u32[]{:S(2)}, u32[]{:S(2)}) collective-permute-start(bf16[64,3328]{1,0:T(8,128)(2,1)} %get-tuple-element.22), channel_id=1, source_target_pairs={{0,192},{64,0},{128,64},{192,128},{1,193},{65,1},{129,65},{193,129... | collective-permute-start | bytes 1277960 | tf_op jit(solution)/shard_map/ppermute | solution.py:25
  60.3 3.3 %collective-permute-start.6 = (bf16[64,3328]{1,0:T(8,128)(2,1)}, bf16[64,3328]{1,0:T(8,128)(2,1)S(1)}, u32[]{:S(2)}, u32[]{:S(2)}) collective-permute-start(bf16[64,3328]{1,0:T(8,128)(2,1)} %get-tuple-element.23), channel_id=1, source_target_pairs={{0,128},{64,192},{128,0},{192,64},{1,129},{65,193},{129,1},{193,65... | collective-permute-start | bytes 1277960 | tf_op jit(solution)/shard_map/ppermute | solution.py:25
  63.6 4.9 %collective-permute-done.4.refs_1_ = bf16[64,3328]{1,0:T(8,128)(2,1)S(1)} collective-permute-done((bf16[64,3328]{1,0:T(8,128)(2,1)}, bf16[64,3328]{1,0:T(8,128)(2,1)S(1)}, u32[]{:S(2)}, u32[]{:S(2)}) %collective-permute-start.4) | collective-permute-done | bytes 426016 | tf_op jit(solution)/shard_map/ppermute | solution.py:25
  68.5 1.4 collective-permute-done.5.refs_2_
  69.9 8.3 %collective-permute-done.6.refs_3_ = bf16[64,3328]{1,0:T(8,128)(2,1)S(1)} collective-permute-done((bf16[64,3328]{1,0:T(8,128)(2,1)}, bf16[64,3328]{1,0:T(8,128)(2,1)S(1)}, u32[]{:S(2)}, u32[]{:S(2)}) %collective-permute-start.6) | collective-permute-done | bytes 426016 | tf_op jit(solution)/shard_map/ppermute | solution.py:25
  78.2 0.0 collective-permute-done.3.refs_5_
  78.2 0.0 copy-done.5
  78.3 0.0 copy-done.6
  78.3 0.7 copy-done.7
  79.0 3.6 %cut_by_zi.1 = bf16[4,4,64,832]{3,2,1,0:T(8,128)(2,1)} custom-call(s32[1]{0:T(128)} %bitcast.7.x_ref, s32[1]{0:T(128)} %bitcast.gy_ref, bf16[64,3328]{1,0:T(8,128)(2,1)} %get-tuple-element.27.refs_0_, bf16[64,3328]{1,0:T(8,128)(2,1)} %copy-done.5, bf16[64,3328]{1,0:T(8,128)(2,1)} %copy-done.6, bf16[64,3328]{1,0:T(8,128)(2,1)} %copy-done.7), custom_call_target="tpu_custom_call" | custom-call | tf_op jit(solution)/shard_map/cut_by_zi/pallas_call | solution.py:143
  82.6 0.0 copy-done.4
  82.6 0.7 all-to-all-done
  83.4 11.2 %all-to-all-start.1 = ((bf16[4,4,64,832]{3,2,1,0:T(8,128)(2,1)}), bf16[4,4,64,832]{3,2,1,0:T(8,128)(2,1)}, u32[]{:S(2)}, u32[]{:S(2)}) async-start(bf16[4,4,64,832]{3,2,1,0:T(8,128)(2,1)} %cut_by_zi.1), calls=%async_computation.1 | async-start | bytes 3670016 | tf_op jit(solution)/shard_map/all_to_all | solution.py:29
  94.6 0.2 reshape.30
  94.8 56.3 %all_gather.6.refs_0_ = bf16[96,4224]{1,0:T(8,128)(2,1)S(1)} all-gather(bf16[24,4224]{1,0:T(8,128)(2,1)S(1)} %reshape.30), channel_id=1, replica_groups=mesh['rep'=2,'x'=4,'zo'=8,'zi'=4,'gy'=2] {'zi'}, dimensions={0}, use_global_device_ids=true | all-gather | bytes 1013760 | tf_op jit(solution)/shard_map/all_gather | solution.py:260
  151.1 2.9 collective-permute-start
  154.0 3.7 %collective-permute-start.1 = (bf16[96,4224]{1,0:T(8,128)(2,1)S(1)}, bf16[96,4224]{1,0:T(8,128)(2,1)S(1)}, u32[]{:S(2)}, u32[]{:S(2)}) collective-permute-start(bf16[96,4224]{1,0:T(8,128)(2,1)S(1)} %all_gather.6.refs_0_), channel_id=1, source_target_pairs={{0,192},{64,0},{128,64},{192,128},{1,193},{65,1},{129,65},{193,129... | collective-permute-start | bytes 2433032 | tf_op jit(solution)/shard_map/ppermute | solution.py:25
  157.6 3.4 %collective-permute-start.2 = (bf16[96,4224]{1,0:T(8,128)(2,1)S(1)}, bf16[96,4224]{1,0:T(8,128)(2,1)S(1)}, u32[]{:S(2)}, u32[]{:S(2)}) collective-permute-start(bf16[96,4224]{1,0:T(8,128)(2,1)S(1)} %all_gather.6.refs_0_), channel_id=1, source_target_pairs={{0,128},{64,192},{128,0},{192,64},{1,129},{65,193},{129,1},{193,65... | collective-permute-start | bytes 2433032 | tf_op jit(solution)/shard_map/ppermute | solution.py:25
  161.0 12.0 %collective-permute-done.refs_1_ = bf16[96,4224]{1,0:T(8,128)(2,1)S(1)} collective-permute-done((bf16[96,4224]{1,0:T(8,128)(2,1)S(1)}, bf16[96,4224]{1,0:T(8,128)(2,1)S(1)}, u32[]{:S(2)}, u32[]{:S(2)}) %collective-permute-start) | collective-permute-done | bytes 811040 | tf_op jit(solution)/shard_map/ppermute | solution.py:25
  173.0 1.4 collective-permute-done.1.refs_2_
  174.4 17.0 %collective-permute-done.2.refs_3_ = bf16[96,4224]{1,0:T(8,128)(2,1)S(1)} collective-permute-done((bf16[96,4224]{1,0:T(8,128)(2,1)S(1)}, bf16[96,4224]{1,0:T(8,128)(2,1)S(1)}, u32[]{:S(2)}, u32[]{:S(2)}) %collective-permute-start.2) | collective-permute-done | bytes 811040 | tf_op jit(solution)/shard_map/ppermute | solution.py:25
  191.4 0.0 copy-done.1
  191.4 0.9 copy-done.3
  192.3 5.0 %values.1 = (f32[208,384]{1,0:T(8,128)}, f32[208,384]{1,0:T(8,128)}) custom-call(bf16[96,4224]{1,0:T(8,128)(2,1)} %copy-done, bf16[96,4224]{1,0:T(8,128)(2,1)} %copy-done.1, bf16[96,4224]{1,0:T(8,128)(2,1)} %copy-done.2, bf16[96,4224]{1,0:T(8,128)(2,1)} %copy-done.3, bf16[208,4096]{1,0:T(8,128)(2,1)} %bitcast.23, bf16[208,4096]{1,0:T(8,128)(2,1)} %copy-done.4), custom_call_target="tpu_custom_call" | custom-call | tf_op jit(solution)/shard_map/values/pallas_call | solution.py:219
  197.2 4.1 %collective-permute-start.7 = (f32[208,384]{1,0:T(8,128)}, f32[208,384]{1,0:T(8,128)S(1)}, u32[]{:S(2)}, u32[]{:S(2)}) collective-permute-start(f32[208,384]{1,0:T(8,128)} %get-tuple-element.26), channel_id=1, source_target_pairs={{0,1},{1,0},{2,3},{3,2},{4,5},{5,4},{6,7},{7,6},{8,9},{9,8},{10,11... | collective-permute-start | bytes 958472 | tf_op jit(solution)/shard_map/ppermute | solution.py:25
  201.4 2.0 placement.1.place_ref
  203.4 0.0 collective-permute-done.7.other_ref
  203.4 0.7 copy-done.8
  204.1 2.0 placed_hidden.1
  206.1 39.0 %all_gather.7 = bf16[832,384]{1,0:T(8,128)(2,1)S(1)} all-gather(bf16[104,384]{1,0:T(8,128)(2,1)} %placed_hidden.1), channel_id=1, replica_groups=mesh['rep'=2,'x'=4,'zo'=8,'zi'=4,'gy'=2] {'zo'}, dimensions={0}, use_global_device_ids=true | all-gather | bytes 718848 | tf_op jit(solution)/shard_map/all_gather | solution.py:271
  245.1 0.0 all-to-all-done.1
  245.2 2.5 fusion.2
  247.7 0.1 fusion.1
  247.8 0.1 pad_maximum_fusion
  247.9 9.6 %collective-permute-start.8 = (f32[384,512]{1,0:T(8,128)S(1)}, f32[384,512]{1,0:T(8,128)S(1)}, u32[]{:S(2)}, u32[]{:S(2)}) collective-permute-start(f32[384,512]{1,0:T(8,128)S(1)} %pad_maximum_fusion), channel_id=1, source_target_pairs={{0,1},{1,0},{2,3},{3,2},{4,5},{5,4},{6,7},{7,6},{8,9},{9,8},{10,11... | collective-permute-start | bytes 2359304 | tf_op jit(solution)/shard_map/ppermute | solution.py:25
  257.5 1.9 collective-permute-done.8
  259.4 0.1 fusion
  259.5 20.7 %all_to_all.20 = bf16[16,24,512]{2,1,0:T(8,128)(2,1)S(1)} all-to-all(bf16[16,24,512]{2,1,0:T(8,128)(2,1)S(1)} %bitcast.24), channel_id=1, replica_groups=mesh['rep'=2,'x'=4,'zo'=8,'zi'=4,'gy'=2] {'x','zi'}, dimensions={0} | all-to-all | bytes 786432 | tf_op jit(solution)/shard_map/all_to_all | solution.py:29
  280.2 0.1 reduce_sum.12
  280.2 33.2 %all_to_all.21 = bf16[8,3,512]{2,1,0:T(4,128)(2,1)S(1)} all-to-all(bf16[8,3,512]{2,1,0:T(4,128)(2,1)S(1)} %reshape.37), channel_id=1, replica_groups=mesh['rep'=2,'x'=4,'zo'=8,'zi'=4,'gy'=2] {'zo'}, dimensions={0} | all-to-all | bytes 49152 | tf_op jit(solution)/shard_map/all_to_all | solution.py:29
  313.5 0.1 reshape.38
  313.6 0.7 reshape.39
  (14 shorter events, 0.1 us)
Async XLA Ops:
  3.0 75.3 %collective-permute-start.3 = (bf16[208,4096]{1,0:T(8,128)(2,1)}, bf16[208,4096]{1,0:T(8,128)(2,1)S(1)}, u32[]{:S(2)}, u32[]{:S(2)}) collective-permute-start(bf16[208,4096]{1,0:T(8,128)(2,1)} %bitcast.26), channel_id=1, source_target_pairs={{0,1},{1,0},{2,3},{3,2},{4,5},{5,4},{6,7},{7,6},{8,9},{9,8},{10,11... | collective-permute-start | bytes 5111816 | tf_op jit(solution)/shard_map/ppermute | solution.py:25
  47.8 35.5 %all-to-all-start = ((bf16[8,3,4224]{2,1,0:T(4,128)(2,1)}), bf16[8,3,4224]{2,1,0:T(4,128)(2,1)S(1)}, u32[]{:S(2)}, u32[]{:S(2)}) async-start(bf16[8,3,4224]{2,1,0:T(4,128)(2,1)} %token_copies.1), calls=%async_computation | async-start | bytes 540672 | tf_op jit(solution)/shard_map/all_to_all | solution.py:29
  53.8 14.7 %collective-permute-start.4 = (bf16[64,3328]{1,0:T(8,128)(2,1)}, bf16[64,3328]{1,0:T(8,128)(2,1)S(1)}, u32[]{:S(2)}, u32[]{:S(2)}) collective-permute-start(bf16[64,3328]{1,0:T(8,128)(2,1)} %get-tuple-element.21), channel_id=1, source_target_pairs={{0,64},{64,128},{128,192},{192,0},{1,65},{65,129},{129,193},{193,1... | collective-permute-start | bytes 1277960 | tf_op jit(solution)/shard_map/ppermute | solution.py:25
  56.6 13.3 %collective-permute-start.5 = (bf16[64,3328]{1,0:T(8,128)(2,1)}, bf16[64,3328]{1,0:T(8,128)(2,1)S(1)}, u32[]{:S(2)}, u32[]{:S(2)}) collective-permute-start(bf16[64,3328]{1,0:T(8,128)(2,1)} %get-tuple-element.22), channel_id=1, source_target_pairs={{0,192},{64,0},{128,64},{192,128},{1,193},{65,1},{129,65},{193,129... | collective-permute-start | bytes 1277960 | tf_op jit(solution)/shard_map/ppermute | solution.py:25
  60.3 17.9 %collective-permute-start.6 = (bf16[64,3328]{1,0:T(8,128)(2,1)}, bf16[64,3328]{1,0:T(8,128)(2,1)S(1)}, u32[]{:S(2)}, u32[]{:S(2)}) collective-permute-start(bf16[64,3328]{1,0:T(8,128)(2,1)} %get-tuple-element.23), channel_id=1, source_target_pairs={{0,128},{64,192},{128,0},{192,64},{1,129},{65,193},{129,1},{193,65... | collective-permute-start | bytes 1277960 | tf_op jit(solution)/shard_map/ppermute | solution.py:25
  68.5 9.8 %copy-start.5 = (bf16[64,3328]{1,0:T(8,128)(2,1)}, bf16[64,3328]{1,0:T(8,128)(2,1)S(1)}, u32[]{:S(2)}) copy-start(bf16[64,3328]{1,0:T(8,128)(2,1)S(1)} %collective-permute-done.4.refs_1_) | copy-start | bytes 1277956
  69.9 8.3 %copy-start.6 = (bf16[64,3328]{1,0:T(8,128)(2,1)}, bf16[64,3328]{1,0:T(8,128)(2,1)S(1)}, u32[]{:S(2)}) copy-start(bf16[64,3328]{1,0:T(8,128)(2,1)S(1)} %collective-permute-done.5.refs_2_) | copy-start | bytes 1277956
  78.2 0.8 copy-start.7
  78.2 4.4 %copy-start.4 = (bf16[208,4096]{1,0:T(8,128)(2,1)}, bf16[208,4096]{1,0:T(8,128)(2,1)S(1)}, u32[]{:S(2)}) copy-start(bf16[208,4096]{1,0:T(8,128)(2,1)S(1)} %collective-permute-done.3.refs_5_) | copy-start | bytes 5111812
  83.4 161.8 %all-to-all-start.1 = ((bf16[4,4,64,832]{3,2,1,0:T(8,128)(2,1)}), bf16[4,4,64,832]{3,2,1,0:T(8,128)(2,1)}, u32[]{:S(2)}, u32[]{:S(2)}) async-start(bf16[4,4,64,832]{3,2,1,0:T(8,128)(2,1)} %cut_by_zi.1), calls=%async_computation.1 | async-start | bytes 3670016 | tf_op jit(solution)/shard_map/all_to_all | solution.py:29
  151.1 40.3 %copy-start = (bf16[96,4224]{1,0:T(8,128)(2,1)}, bf16[96,4224]{1,0:T(8,128)(2,1)S(1)}, u32[]{:S(2)}) copy-start(bf16[96,4224]{1,0:T(8,128)(2,1)S(1)} %all_gather.6.refs_0_) | copy-start | bytes 2433028
  151.1 21.9 %collective-permute-start = (bf16[96,4224]{1,0:T(8,128)(2,1)S(1)}, bf16[96,4224]{1,0:T(8,128)(2,1)S(1)}, u32[]{:S(2)}, u32[]{:S(2)}) collective-permute-start(bf16[96,4224]{1,0:T(8,128)(2,1)S(1)} %all_gather.6.refs_0_), channel_id=1, source_target_pairs={{0,64},{64,128},{128,192},{192,0},{1,65},{65,129},{129,193},{193,1... | collective-permute-start | bytes 2433032 | tf_op jit(solution)/shard_map/ppermute | solution.py:25
  154.0 20.4 %collective-permute-start.1 = (bf16[96,4224]{1,0:T(8,128)(2,1)S(1)}, bf16[96,4224]{1,0:T(8,128)(2,1)S(1)}, u32[]{:S(2)}, u32[]{:S(2)}) collective-permute-start(bf16[96,4224]{1,0:T(8,128)(2,1)S(1)} %all_gather.6.refs_0_), channel_id=1, source_target_pairs={{0,192},{64,0},{128,64},{192,128},{1,193},{65,1},{129,65},{193,129... | collective-permute-start | bytes 2433032 | tf_op jit(solution)/shard_map/ppermute | solution.py:25
  157.6 33.8 %collective-permute-start.2 = (bf16[96,4224]{1,0:T(8,128)(2,1)S(1)}, bf16[96,4224]{1,0:T(8,128)(2,1)S(1)}, u32[]{:S(2)}, u32[]{:S(2)}) collective-permute-start(bf16[96,4224]{1,0:T(8,128)(2,1)S(1)} %all_gather.6.refs_0_), channel_id=1, source_target_pairs={{0,128},{64,192},{128,0},{192,64},{1,129},{65,193},{129,1},{193,65... | collective-permute-start | bytes 2433032 | tf_op jit(solution)/shard_map/ppermute | solution.py:25
  173.0 18.4 %copy-start.1 = (bf16[96,4224]{1,0:T(8,128)(2,1)}, bf16[96,4224]{1,0:T(8,128)(2,1)S(1)}, u32[]{:S(2)}) copy-start(bf16[96,4224]{1,0:T(8,128)(2,1)S(1)} %collective-permute-done.refs_1_) | copy-start | bytes 2433028
  174.4 17.0 %copy-start.2 = (bf16[96,4224]{1,0:T(8,128)(2,1)}, bf16[96,4224]{1,0:T(8,128)(2,1)S(1)}, u32[]{:S(2)}) copy-start(bf16[96,4224]{1,0:T(8,128)(2,1)S(1)} %collective-permute-done.1.refs_2_) | copy-start | bytes 2433028
  191.4 0.9 copy-start.3
  197.2 6.1 %collective-permute-start.7 = (f32[208,384]{1,0:T(8,128)}, f32[208,384]{1,0:T(8,128)S(1)}, u32[]{:S(2)}, u32[]{:S(2)}) collective-permute-start(f32[208,384]{1,0:T(8,128)} %get-tuple-element.26), channel_id=1, source_target_pairs={{0,1},{1,0},{2,3},{3,2},{4,5},{5,4},{6,7},{7,6},{8,9},{9,8},{10,11... | collective-permute-start | bytes 958472 | tf_op jit(solution)/shard_map/ppermute | solution.py:25
  203.4 0.7 copy-start.8
  247.9 11.5 %collective-permute-start.8 = (f32[384,512]{1,0:T(8,128)S(1)}, f32[384,512]{1,0:T(8,128)S(1)}, u32[]{:S(2)}, u32[]{:S(2)}) collective-permute-start(f32[384,512]{1,0:T(8,128)S(1)} %pad_maximum_fusion), channel_id=1, source_target_pairs={{0,1},{1,0},{2,3},{3,2},{4,5},{5,4},{6,7},{7,6},{8,9},{9,8},{10,11... | collective-permute-start | bytes 2359304 | tf_op jit(solution)/shard_map/ppermute | solution.py:25

commit v9 on v8

--- a/solution.py
+++ b/solution.py
@@ -14,7 +14,7 @@
 X, ZO, ZI = 4, 8, 4
 GX = ("x", "zo", "zi")
 REP_GX = ("rep", "x", "zo", "zi")
-LANES = 128
+SUBLANES, LANES = 8, 128
 STEPS = (0, 1, 3, 2)
 F32 = jnp.float32
 BF16 = jnp.bfloat16
@@ -42,26 +42,55 @@
         copy.wait()
 
 
-def copies_kernel(kinds_ref, tokens_ref, out_ref):
+def pack_kernel(kinds_ref, tokens_ref, out_ref):
     count, half = tokens_ref.shape
-    row = lax.broadcasted_iota(jnp.int32, (count, LANES), 0)
-    kinds = jnp.zeros((count, LANES), F32)
+    piece = half // SUBLANES
+    tokens = tokens_ref[...].astype(F32)
+    rows = [
+        jnp.concatenate([tokens[k : k + 1, e * piece : (e + 1) * piece] for k in range(count)], 1)
+        for e in range(SUBLANES)
+    ]
+    packed = jnp.concatenate(rows, 0).astype(BF16)
+    row = lax.broadcasted_iota(jnp.int32, (SUBLANES, LANES), 0)
+    kinds = jnp.zeros((SUBLANES, LANES), F32)
     for k in range(count):
         kinds = jnp.where(row == k, kinds_ref[k].astype(F32), kinds)
     for k in range(ZO):
-        out_ref[k, :, :half] = tokens_ref[...]
-        out_ref[k, :, half:] = kinds.astype(BF16)
-
-
-def token_copies(tokens, segment_ids):
+        out_ref[k, :, : count * piece] = packed
+        out_ref[k, :, count * piece :] = kinds.astype(BF16)
+
+
+def packed_tokens(tokens, segment_ids):
     count, half = tokens.shape
     return pl.pallas_call(
-        copies_kernel,
+        pack_kernel,
         in_specs=[pl.BlockSpec(memory_space=pltpu.SMEM), pl.BlockSpec(memory_space=pltpu.VMEM)],
         out_specs=pl.BlockSpec(memory_space=pltpu.VMEM),
-        out_shape=jax.ShapeDtypeStruct((ZO, count, half + LANES), tokens.dtype),
-        name="token_copies",
+        out_shape=jax.ShapeDtypeStruct((ZO, SUBLANES, count * half // SUBLANES + LANES), tokens.dtype),
+        name="packed_tokens",
     )(segment_ids, tokens)
+
+
+def unpack_kernel(count, packed_ref, out_ref):
+    piece = (packed_ref.shape[2] - LANES) // count
+    rows = []
+    for zo in range(ZO):
+        packed = packed_ref[zo].astype(F32)
+        for k in range(count):
+            parts = [packed[e : e + 1, k * piece : (k + 1) * piece] for e in range(SUBLANES)]
+            rows.append(jnp.concatenate(parts + [packed[k : k + 1, count * piece :]], 1))
+    out_ref[...] = jnp.concatenate(rows, 0).astype(BF16)
+
+
+def unpacked_tokens(packed, count):
+    columns = (packed.shape[2] - LANES) // count * SUBLANES + LANES
+    return pl.pallas_call(
+        functools.partial(unpack_kernel, count),
+        in_specs=[pl.BlockSpec(memory_space=pltpu.VMEM)],
+        out_specs=pl.BlockSpec(memory_space=pltpu.VMEM),
+        out_shape=jax.ShapeDtypeStruct((ZO * count, columns), packed.dtype),
+        name="unpacked_tokens",
+    )(packed)
 
 
 def cut_by_x_kernel(x_ref, rows_ref, *refs):
@@ -245,8 +274,8 @@
 def block(tokens, segment_ids, gate_weight, up_weight, down_weight):
     x, gy = lax.axis_index("x"), lax.axis_index("gy")
     own_tokens, half = tokens.shape
-    copies = token_copies(tokens, segment_ids)
-    strided = exchanged(copies, "zo").reshape(ZO * own_tokens, -1)
+    packed = exchanged(packed_tokens(tokens, segment_ids), "zo")
+    strided = unpacked_tokens(packed, own_tokens)
 
     x_at, gy_at = x.reshape(1), gy.reshape(1)
     blocks = cut_by_x(down_weight[0].T, x_at)
@@ -297,6 +326,4 @@
         ("rep", "x", "zo", "zi", "gy"),
     )
     placed = (P(REP_GX, "gy"), P(REP_GX), P(None, "gy", GX), P(None, "gy", GX), P("gy", None, GX))
-    return jax.shard_map(
-        block, mesh=torus, in_specs=placed, out_specs=P(REP_GX, "gy"), check_vma=False
-    )
+    return jax.shard_map(block, mesh=torus, in_specs=placed, out_specs=P(REP_GX, "gy"), check_vma=False)

time: 316 us -> 319 us (level)
  starting transfers between devices: 91.7 us -> 86.4 us
  blocking collectives: 149 us -> 153 us
    all_gather x1, blocking collectives: 39 us -> 45.4 us  [block(): gathered = lax.all_gather(placed, 'zo', axis=0, tiled=True)]
    all_to_all x2, starting transfers between devices: 14.8 us -> 10.1 us  [exchanged(): return lax.all_to_all(blocks, axes, split_axis=0, concat_axis=0, tiled=True)]
  transfers between devices with their start and end apart: 11 -> 11, of which waited for: 8 -> 8; matrix products, arithmetic and copies ran while one was open for 0% -> 0% of each run, Pallas kernels for 5% -> 6%
where the time goes in v9:
time: 319 us; the launch traced here: 316 us
  blocking collectives  153 us (48%)
  starting transfers between devices  86.4 us (27%)
  waiting for transfers between devices  47.5 us (15%)
  Pallas kernels  21.2 us (7%)
  local copies, waits for them, and re-layouts  4.04 us (1%)
    ppermute x9, starting transfers between devices, shifted(): lax.ppermute(value, axis, [(i, (i + by) % count) for i in range(count)])  76.2 us
    all_gather x1, blocking collectives, block(): column = lax.all_gather(strided, 'zi', axis=0, tiled=True)  54.6 us
    all_to_all x2, blocking collectives, exchanged(): return lax.all_to_all(blocks, axes, split_axis=0, concat_axis=0, tiled=True)  53.4 us
    ppermute x9, waiting for transfers between devices, shifted(): lax.ppermute(value, axis, [(i, (i + by) % count) for i in range(count)])  46.9 us
    all_gather x1, blocking collectives, block(): gathered = lax.all_gather(placed, 'zo', axis=0, tiled=True)  45.4 us
    all_to_all x2, starting transfers between devices, exchanged(): return lax.all_to_all(blocks, axes, split_axis=0, concat_axis=0, tiled=True)  10.1 us
  transfers between devices with their start and end apart: 11, of which 8 were waited for; matrix products, arithmetic and copies ran while one was open for 0% of the time, Pallas kernels for 6%

profile of v9, /device:TPU:33, one launch (start us, length us, event | category | flops | bytes accessed | tf_op | source)
XLA Modules:
  0.0 315.6 jit_solution(12917878058726077788)
XLA Ops:
  0.0 3.0 split_rows.1
  3.0 43.4 %collective-permute-start.3 = (bf16[208,4096]{1,0:T(8,128)(2,1)}, bf16[208,4096]{1,0:T(8,128)(2,1)S(1)}, u32[]{:S(2)}, u32[]{:S(2)}) collective-permute-start(bf16[208,4096]{1,0:T(8,128)(2,1)} %bitcast.26), channel_id=1, source_target_pairs={{0,1},{1,0},{2,3},{3,2},{4,5},{5,4},{6,7},{7,6},{8,9},{9,8},{10,11... | collective-permute-start | bytes 5111816 | tf_op jit(solution)/shard_map/ppermute | solution.py:25
  46.4 1.5 packed_tokens.1
  47.9 3.6 %all-to-all-start = ((bf16[8,8,1664]{2,1,0:T(8,128)(2,1)}), bf16[8,8,1664]{2,1,0:T(8,128)(2,1)S(1)}, u32[]{:S(2)}, u32[]{:S(2)}) async-start(bf16[8,8,1664]{2,1,0:T(8,128)(2,1)} %packed_tokens.1), calls=%async_computation | async-start | bytes 425984 | tf_op jit(solution)/shard_map/all_to_all | solution.py:29
  51.5 2.3 cut_by_x.1
  53.8 2.8 collective-permute-start.4
  56.6 3.7 %collective-permute-start.5 = (bf16[64,3328]{1,0:T(8,128)(2,1)}, bf16[64,3328]{1,0:T(8,128)(2,1)S(1)}, u32[]{:S(2)}, u32[]{:S(2)}) collective-permute-start(bf16[64,3328]{1,0:T(8,128)(2,1)} %get-tuple-element.22), channel_id=1, source_target_pairs={{0,192},{64,0},{128,64},{192,128},{1,193},{65,1},{129,65},{193,129... | collective-permute-start | bytes 1277960 | tf_op jit(solution)/shard_map/ppermute | solution.py:25
  60.3 3.3 %collective-permute-start.6 = (bf16[64,3328]{1,0:T(8,128)(2,1)}, bf16[64,3328]{1,0:T(8,128)(2,1)S(1)}, u32[]{:S(2)}, u32[]{:S(2)}) collective-permute-start(bf16[64,3328]{1,0:T(8,128)(2,1)} %get-tuple-element.23), channel_id=1, source_target_pairs={{0,128},{64,192},{128,0},{192,64},{1,129},{65,193},{129,1},{193,65... | collective-permute-start | bytes 1277960 | tf_op jit(solution)/shard_map/ppermute | solution.py:25
  63.6 4.8 %collective-permute-done.4.refs_1_ = bf16[64,3328]{1,0:T(8,128)(2,1)S(1)} collective-permute-done((bf16[64,3328]{1,0:T(8,128)(2,1)}, bf16[64,3328]{1,0:T(8,128)(2,1)S(1)}, u32[]{:S(2)}, u32[]{:S(2)}) %collective-permute-start.4) | collective-permute-done | bytes 426016 | tf_op jit(solution)/shard_map/ppermute | solution.py:25
  68.5 1.4 collective-permute-done.5.refs_2_
  69.9 8.3 %collective-permute-done.6.refs_3_ = bf16[64,3328]{1,0:T(8,128)(2,1)S(1)} collective-permute-done((bf16[64,3328]{1,0:T(8,128)(2,1)}, bf16[64,3328]{1,0:T(8,128)(2,1)S(1)}, u32[]{:S(2)}, u32[]{:S(2)}) %collective-permute-start.6) | collective-permute-done | bytes 426016 | tf_op jit(solution)/shard_map/ppermute | solution.py:25
  78.3 0.0 collective-permute-done.3.refs_5_
  78.3 0.0 copy-done.6
  78.3 0.0 copy-done.7
  78.3 0.7 copy-done.8
  79.0 3.6 %cut_by_zi.1 = bf16[4,4,64,832]{3,2,1,0:T(8,128)(2,1)} custom-call(s32[1]{0:T(128)} %bitcast.7.x_ref, s32[1]{0:T(128)} %bitcast.gy_ref, bf16[64,3328]{1,0:T(8,128)(2,1)} %get-tuple-element.27.refs_0_, bf16[64,3328]{1,0:T(8,128)(2,1)} %copy-done.6, bf16[64,3328]{1,0:T(8,128)(2,1)} %copy-done.7, bf16[64,3328]{1,0:T(8,128)(2,1)} %copy-done.8), custom_call_target="tpu_custom_call" | custom-call | tf_op jit(solution)/shard_map/cut_by_zi/pallas_call | solution.py:172
  82.7 0.6 all-to-all-done.packed_ref
  83.3 0.7 copy-done.5
  83.9 6.5 %all-to-all-start.1 = ((bf16[4,4,64,832]{3,2,1,0:T(8,128)(2,1)}), bf16[4,4,64,832]{3,2,1,0:T(8,128)(2,1)}, u32[]{:S(2)}, u32[]{:S(2)}) async-start(bf16[4,4,64,832]{3,2,1,0:T(8,128)(2,1)} %cut_by_zi.1), calls=%async_computation.1 | async-start | bytes 3670016 | tf_op jit(solution)/shard_map/all_to_all | solution.py:29
  90.5 1.8 unpacked_tokens.1
  92.3 54.6 %all_gather.6.refs_0_ = bf16[96,4224]{1,0:T(8,128)(2,1)S(1)} all-gather(bf16[24,4224]{1,0:T(8,128)(2,1)} %unpacked_tokens.1), channel_id=1, replica_groups=mesh['rep'=2,'x'=4,'zo'=8,'zi'=4,'gy'=2] {'zi'}, dimensions={0}, use_global_device_ids=true | all-gather | bytes 1013760 | tf_op jit(solution)/shard_map/all_gather | solution.py:289
  146.9 3.0 collective-permute-start
  149.9 3.6 %collective-permute-start.1 = (bf16[96,4224]{1,0:T(8,128)(2,1)S(1)}, bf16[96,4224]{1,0:T(8,128)(2,1)S(1)}, u32[]{:S(2)}, u32[]{:S(2)}) collective-permute-start(bf16[96,4224]{1,0:T(8,128)(2,1)S(1)} %all_gather.6.refs_0_), channel_id=1, source_target_pairs={{0,192},{64,0},{128,64},{192,128},{1,193},{65,1},{129,65},{193,129... | collective-permute-start | bytes 2433032 | tf_op jit(solution)/shard_map/ppermute | solution.py:25
  153.5 3.4 %collective-permute-start.2 = (bf16[96,4224]{1,0:T(8,128)(2,1)S(1)}, bf16[96,4224]{1,0:T(8,128)(2,1)S(1)}, u32[]{:S(2)}, u32[]{:S(2)}) collective-permute-start(bf16[96,4224]{1,0:T(8,128)(2,1)S(1)} %all_gather.6.refs_0_), channel_id=1, source_target_pairs={{0,128},{64,192},{128,0},{192,64},{1,129},{65,193},{129,1},{193,65... | collective-permute-start | bytes 2433032 | tf_op jit(solution)/shard_map/ppermute | solution.py:25
  157.0 11.9 %collective-permute-done.refs_1_ = bf16[96,4224]{1,0:T(8,128)(2,1)S(1)} collective-permute-done((bf16[96,4224]{1,0:T(8,128)(2,1)S(1)}, bf16[96,4224]{1,0:T(8,128)(2,1)S(1)}, u32[]{:S(2)}, u32[]{:S(2)}) %collective-permute-start) | collective-permute-done | bytes 811040 | tf_op jit(solution)/shard_map/ppermute | solution.py:25
  168.9 1.5 collective-permute-done.1.refs_2_
  170.4 17.0 %collective-permute-done.2.refs_3_ = bf16[96,4224]{1,0:T(8,128)(2,1)S(1)} collective-permute-done((bf16[96,4224]{1,0:T(8,128)(2,1)S(1)}, bf16[96,4224]{1,0:T(8,128)(2,1)S(1)}, u32[]{:S(2)}, u32[]{:S(2)}) %collective-permute-start.2) | collective-permute-done | bytes 811040 | tf_op jit(solution)/shard_map/ppermute | solution.py:25
  187.3 0.0 copy-done
  187.4 0.9 copy-done.3
  188.3 5.0 %values.1 = (f32[208,384]{1,0:T(8,128)}, f32[208,384]{1,0:T(8,128)}) custom-call(bf16[96,4224]{1,0:T(8,128)(2,1)} %copy-done, bf16[96,4224]{1,0:T(8,128)(2,1)} %copy-done.1, bf16[96,4224]{1,0:T(8,128)(2,1)} %copy-done.2, bf16[96,4224]{1,0:T(8,128)(2,1)} %copy-done.3, bf16[208,4096]{1,0:T(8,128)(2,1)} %bitcast.23, bf16[208,4096]{1,0:T(8,128)(2,1)} %copy-done.4), custom_call_target="tpu_custom_call" | custom-call | tf_op jit(solution)/shard_map/values/pallas_call | solution.py:248
  193.2 4.0 %collective-permute-start.7 = (f32[208,384]{1,0:T(8,128)}, f32[208,384]{1,0:T(8,128)S(1)}, u32[]{:S(2)}, u32[]{:S(2)}) collective-permute-start(f32[208,384]{1,0:T(8,128)} %get-tuple-element.26), channel_id=1, source_target_pairs={{0,1},{1,0},{2,3},{3,2},{4,5},{5,4},{6,7},{7,6},{8,9},{9,8},{10,11... | collective-permute-start | bytes 958472 | tf_op jit(solution)/shard_map/ppermute | solution.py:25
  197.3 2.0 placement.1.place_ref
  199.3 0.0 collective-permute-done.7.other_ref
  199.3 0.7 copy-done.9
  200.0 2.0 placed_hidden.1
  202.0 45.4 %all_gather.7 = bf16[832,384]{1,0:T(8,128)(2,1)S(1)} all-gather(bf16[104,384]{1,0:T(8,128)(2,1)} %placed_hidden.1), channel_id=1, replica_groups=mesh['rep'=2,'x'=4,'zo'=8,'zi'=4,'gy'=2] {'zo'}, dimensions={0}, use_global_device_ids=true | all-gather | bytes 718848 | tf_op jit(solution)/shard_map/all_gather | solution.py:300
  247.4 0.0 all-to-all-done.1
  247.4 2.5 fusion.2
  250.0 0.1 fusion.1
  250.1 0.1 pad_maximum_fusion
  250.2 9.0 %collective-permute-start.8 = (f32[384,512]{1,0:T(8,128)S(1)}, f32[384,512]{1,0:T(8,128)S(1)}, u32[]{:S(2)}, u32[]{:S(2)}) collective-permute-start(f32[384,512]{1,0:T(8,128)S(1)} %pad_maximum_fusion), channel_id=1, source_target_pairs={{0,1},{1,0},{2,3},{3,2},{4,5},{5,4},{6,7},{7,6},{8,9},{9,8},{10,11... | collective-permute-start | bytes 2359304 | tf_op jit(solution)/shard_map/ppermute | solution.py:25
  259.2 1.9 collective-permute-done.8
  261.1 0.1 fusion
  261.2 19.2 %all_to_all.20 = bf16[16,24,512]{2,1,0:T(8,128)(2,1)S(1)} all-to-all(bf16[16,24,512]{2,1,0:T(8,128)(2,1)S(1)} %bitcast.24), channel_id=1, replica_groups=mesh['rep'=2,'x'=4,'zo'=8,'zi'=4,'gy'=2] {'x','zi'}, dimensions={0} | all-to-all | bytes 786432 | tf_op jit(solution)/shard_map/all_to_all | solution.py:29
  280.3 0.1 reduce_sum.12
  280.4 34.3 %all_to_all.21 = bf16[8,3,512]{2,1,0:T(4,128)(2,1)S(1)} all-to-all(bf16[8,3,512]{2,1,0:T(4,128)(2,1)S(1)} %reshape.33), channel_id=1, replica_groups=mesh['rep'=2,'x'=4,'zo'=8,'zi'=4,'gy'=2] {'zo'}, dimensions={0} | all-to-all | bytes 49152 | tf_op jit(solution)/shard_map/all_to_all | solution.py:29
  314.7 0.1 reshape.34
  314.8 0.7 reshape.35
  (16 shorter events, 0.1 us)
Async XLA Ops:
  3.0 75.3 %collective-permute-start.3 = (bf16[208,4096]{1,0:T(8,128)(2,1)}, bf16[208,4096]{1,0:T(8,128)(2,1)S(1)}, u32[]{:S(2)}, u32[]{:S(2)}) collective-permute-start(bf16[208,4096]{1,0:T(8,128)(2,1)} %bitcast.26), channel_id=1, source_target_pairs={{0,1},{1,0},{2,3},{3,2},{4,5},{5,4},{6,7},{7,6},{8,9},{9,8},{10,11... | collective-permute-start | bytes 5111816 | tf_op jit(solution)/shard_map/ppermute | solution.py:25
  47.9 35.4 %all-to-all-start = ((bf16[8,8,1664]{2,1,0:T(8,128)(2,1)}), bf16[8,8,1664]{2,1,0:T(8,128)(2,1)S(1)}, u32[]{:S(2)}, u32[]{:S(2)}) async-start(bf16[8,8,1664]{2,1,0:T(8,128)(2,1)} %packed_tokens.1), calls=%async_computation | async-start | bytes 425984 | tf_op jit(solution)/shard_map/all_to_all | solution.py:29
  53.8 14.7 %collective-permute-start.4 = (bf16[64,3328]{1,0:T(8,128)(2,1)}, bf16[64,3328]{1,0:T(8,128)(2,1)S(1)}, u32[]{:S(2)}, u32[]{:S(2)}) collective-permute-start(bf16[64,3328]{1,0:T(8,128)(2,1)} %get-tuple-element.21), channel_id=1, source_target_pairs={{0,64},{64,128},{128,192},{192,0},{1,65},{65,129},{129,193},{193,1... | collective-permute-start | bytes 1277960 | tf_op jit(solution)/shard_map/ppermute | solution.py:25
  56.6 13.3 %collective-permute-start.5 = (bf16[64,3328]{1,0:T(8,128)(2,1)}, bf16[64,3328]{1,0:T(8,128)(2,1)S(1)}, u32[]{:S(2)}, u32[]{:S(2)}) collective-permute-start(bf16[64,3328]{1,0:T(8,128)(2,1)} %get-tuple-element.22), channel_id=1, source_target_pairs={{0,192},{64,0},{128,64},{192,128},{1,193},{65,1},{129,65},{193,129... | collective-permute-start | bytes 1277960 | tf_op jit(solution)/shard_map/ppermute | solution.py:25
  60.3 17.9 %collective-permute-start.6 = (bf16[64,3328]{1,0:T(8,128)(2,1)}, bf16[64,3328]{1,0:T(8,128)(2,1)S(1)}, u32[]{:S(2)}, u32[]{:S(2)}) collective-permute-start(bf16[64,3328]{1,0:T(8,128)(2,1)} %get-tuple-element.23), channel_id=1, source_target_pairs={{0,128},{64,192},{128,0},{192,64},{1,129},{65,193},{129,1},{193,65... | collective-permute-start | bytes 1277960 | tf_op jit(solution)/shard_map/ppermute | solution.py:25
  68.5 9.8 %copy-start.6 = (bf16[64,3328]{1,0:T(8,128)(2,1)}, bf16[64,3328]{1,0:T(8,128)(2,1)S(1)}, u32[]{:S(2)}) copy-start(bf16[64,3328]{1,0:T(8,128)(2,1)S(1)} %collective-permute-done.4.refs_1_) | copy-start | bytes 1277956
  69.9 8.4 %copy-start.7 = (bf16[64,3328]{1,0:T(8,128)(2,1)}, bf16[64,3328]{1,0:T(8,128)(2,1)S(1)}, u32[]{:S(2)}) copy-start(bf16[64,3328]{1,0:T(8,128)(2,1)S(1)} %collective-permute-done.5.refs_2_) | copy-start | bytes 1277956
  78.3 0.8 copy-start.8
  78.3 4.4 %copy-start.4 = (bf16[208,4096]{1,0:T(8,128)(2,1)}, bf16[208,4096]{1,0:T(8,128)(2,1)S(1)}, u32[]{:S(2)}) copy-start(bf16[208,4096]{1,0:T(8,128)(2,1)S(1)} %collective-permute-done.3.refs_5_) | copy-start | bytes 5111812
  83.3 0.7 copy-start.5
  83.9 163.5 %all-to-all-start.1 = ((bf16[4,4,64,832]{3,2,1,0:T(8,128)(2,1)}), bf16[4,4,64,832]{3,2,1,0:T(8,128)(2,1)}, u32[]{:S(2)}, u32[]{:S(2)}) async-start(bf16[4,4,64,832]{3,2,1,0:T(8,128)(2,1)} %cut_by_zi.1), calls=%async_computation.1 | async-start | bytes 3670016 | tf_op jit(solution)/shard_map/all_to_all | solution.py:29
  146.9 40.4 %copy-start = (bf16[96,4224]{1,0:T(8,128)(2,1)}, bf16[96,4224]{1,0:T(8,128)(2,1)S(1)}, u32[]{:S(2)}) copy-start(bf16[96,4224]{1,0:T(8,128)(2,1)S(1)} %all_gather.6.refs_0_) | copy-start | bytes 2433028
  146.9 21.9 %collective-permute-start = (bf16[96,4224]{1,0:T(8,128)(2,1)S(1)}, bf16[96,4224]{1,0:T(8,128)(2,1)S(1)}, u32[]{:S(2)}, u32[]{:S(2)}) collective-permute-start(bf16[96,4224]{1,0:T(8,128)(2,1)S(1)} %all_gather.6.refs_0_), channel_id=1, source_target_pairs={{0,64},{64,128},{128,192},{192,0},{1,65},{65,129},{129,193},{193,1... | collective-permute-start | bytes 2433032 | tf_op jit(solution)/shard_map/ppermute | solution.py:25
  149.9 20.4 %collective-permute-start.1 = (bf16[96,4224]{1,0:T(8,128)(2,1)S(1)}, bf16[96,4224]{1,0:T(8,128)(2,1)S(1)}, u32[]{:S(2)}, u32[]{:S(2)}) collective-permute-start(bf16[96,4224]{1,0:T(8,128)(2,1)S(1)} %all_gather.6.refs_0_), channel_id=1, source_target_pairs={{0,192},{64,0},{128,64},{192,128},{1,193},{65,1},{129,65},{193,129... | collective-permute-start | bytes 2433032 | tf_op jit(solution)/shard_map/ppermute | solution.py:25
  153.5 33.8 %collective-permute-start.2 = (bf16[96,4224]{1,0:T(8,128)(2,1)S(1)}, bf16[96,4224]{1,0:T(8,128)(2,1)S(1)}, u32[]{:S(2)}, u32[]{:S(2)}) collective-permute-start(bf16[96,4224]{1,0:T(8,128)(2,1)S(1)} %all_gather.6.refs_0_), channel_id=1, source_target_pairs={{0,128},{64,192},{128,0},{192,64},{1,129},{65,193},{129,1},{193,65... | collective-permute-start | bytes 2433032 | tf_op jit(solution)/shard_map/ppermute | solution.py:25
  168.9 18.5 %copy-start.1 = (bf16[96,4224]{1,0:T(8,128)(2,1)}, bf16[96,4224]{1,0:T(8,128)(2,1)S(1)}, u32[]{:S(2)}) copy-start(bf16[96,4224]{1,0:T(8,128)(2,1)S(1)} %collective-permute-done.refs_1_) | copy-start | bytes 2433028
  170.4 17.0 %copy-start.2 = (bf16[96,4224]{1,0:T(8,128)(2,1)}, bf16[96,4224]{1,0:T(8,128)(2,1)S(1)}, u32[]{:S(2)}) copy-start(bf16[96,4224]{1,0:T(8,128)(2,1)S(1)} %collective-permute-done.1.refs_2_) | copy-start | bytes 2433028
  187.3 0.9 copy-start.3
  193.2 6.0 %collective-permute-start.7 = (f32[208,384]{1,0:T(8,128)}, f32[208,384]{1,0:T(8,128)S(1)}, u32[]{:S(2)}, u32[]{:S(2)}) collective-permute-start(f32[208,384]{1,0:T(8,128)} %get-tuple-element.26), channel_id=1, source_target_pairs={{0,1},{1,0},{2,3},{3,2},{4,5},{5,4},{6,7},{7,6},{8,9},{9,8},{10,11... | collective-permute-start | bytes 958472 | tf_op jit(solution)/shard_map/ppermute | solution.py:25
  199.3 0.7 copy-start.9
  250.2 10.9 %collective-permute-start.8 = (f32[384,512]{1,0:T(8,128)S(1)}, f32[384,512]{1,0:T(8,128)S(1)}, u32[]{:S(2)}, u32[]{:S(2)}) collective-permute-start(f32[384,512]{1,0:T(8,128)S(1)} %pad_maximum_fusion), channel_id=1, source_target_pairs={{0,1},{1,0},{2,3},{3,2},{4,5},{5,4},{6,7},{7,6},{8,9},{9,8},{10,11... | collective-permute-start | bytes 2359304 | tf_op jit(solution)/shard_map/ppermute | solution.py:25

commit v10 on v8

--- a/solution.py
+++ b/solution.py
@@ -151,7 +151,7 @@
 
 def place_kernel(x_ref, *refs):
     *kinds_refs, within_ref, within_row_ref, slot_ref, place_ref = refs
-    chunk, count = kinds_refs[0].shape[0], slot_ref.shape[1]
+    chunk, count = within_ref.shape[0], slot_ref.shape[1]
     starts = [(lax.rem(x_ref[0] + X - by, X) * chunk).astype(F32) for by in STEPS]
     lane = lax.broadcasted_iota(jnp.int32, (1, count), 1)
     order_row = within_row_ref[...] + starts[0]
@@ -166,17 +166,17 @@
 
 
 def placement(chunks, half, x, own_tokens):
-    chunk = chunks[0].shape[0]
-    count = X * chunk
+    count = sum(chunk.shape[0] for chunk in chunks)
+    chunk = count // X
     slot = np.arange(count, dtype=np.float32).reshape(X, ZO, ZI, own_tokens).transpose(0, 2, 1, 3)
     within = slot[0].reshape(chunk)
-    kinds = pl.BlockSpec((chunk, LANES), lambda i: (0, half // LANES))
+    kinds = [pl.BlockSpec((piece.shape[0], LANES), lambda i: (0, half // LANES)) for piece in chunks]
     row = pl.BlockSpec((1, count), lambda i: (0, 0))
     return pl.pallas_call(
         place_kernel,
         grid=(1,),
         in_specs=[pl.BlockSpec(memory_space=pltpu.SMEM)]
-        + [kinds] * X
+        + kinds
         + [pl.BlockSpec((chunk, LANES), lambda i: (0, 0)), row, row],
         out_specs=pl.BlockSpec((count, count), lambda i: (0, 0)),
         out_shape=jax.ShapeDtypeStruct((count, count), BF16),
@@ -258,9 +258,16 @@
     group = cut_by_zi(blocks, x_at, gy_at)
 
     column = lax.all_gather(strided, "zi", axis=0, tiled=True)
-    chunks = [column]
-    for by in STEPS[1:]:
-        chunks.append(shifted(column, "x", by))
+    upper, lower = jnp.split(column, 2, axis=0)
+
+    def passed(piece, by):
+        return shifted(piece, "x", by)
+
+    before_upper, after_lower = passed(upper, 1), passed(lower, 3)
+    before_lower, after_upper = passed(lower, 1), passed(upper, 3)
+    across_upper, across_lower = passed(before_upper, 1), passed(after_lower, 3)
+    chunks = [column, before_upper, before_lower, after_upper, after_lower, across_upper, across_lower]
+
     group = exchanged(group, "zi")
 
     own_value, other_value = values(chunks, own_rows, other_rows)
@@ -281,7 +288,7 @@
             [partial[:, (2 * k + which) * width : (2 * k + which + 1) * width] for k in range(ZI)], 1
         )
 
-    other_half = shifted(half_of(1), "gy", 1)
+    other_half = shifted(half_of(1).astype(BF16), "gy", 1)
     summed = (half_of(0) + other_half).astype(BF16)
     slots = summed.shape[0]
     arrived = exchanged(summed.reshape(X * ZI, slots // (X * ZI), -1), ("x", "zi"))
@@ -297,6 +304,4 @@
         ("rep", "x", "zo", "zi", "gy"),
     )
     placed = (P(REP_GX, "gy"), P(REP_GX), P(None, "gy", GX), P(None, "gy", GX), P("gy", None, GX))
-    return jax.shard_map(
-        block, mesh=torus, in_specs=placed, out_specs=P(REP_GX, "gy"), check_vma=False
-    )
+    return jax.shard_map(block, mesh=torus, in_specs=placed, out_specs=P(REP_GX, "gy"), check_vma=False)

time: 316 us -> 306 us (0.968)
  waiting for transfers between devices: 47.6 us -> 27.7 us
  starting transfers between devices: 91.7 us -> 105 us
    ppermute x9 -> x12, waiting for transfers between devices: 46.9 us -> 26.9 us  [shifted(): lax.ppermute(value, axis, [(i, (i + by) % count) for i in range(count)])]
    ppermute x9 -> x12, starting transfers between devices: 76.8 us -> 90.1 us  [shifted(): lax.ppermute(value, axis, [(i, (i + by) % count) for i in range(count)])]
    all_gather x1, blocking collectives: 39 us -> 43 us  [block(): gathered = lax.all_gather(placed, 'zo', axis=0, tiled=True)]
  transfers between devices with their start and end apart: 11 -> 14, of which waited for: 8 -> 9; matrix products, arithmetic and copies ran while one was open for 0% -> 0% of each run, Pallas kernels for 5% -> 5%
where the time goes in v10:
time: 306 us; the launch traced here: 304 us
  blocking collectives  147 us (48%)
  starting transfers between devices  105 us (34%)
  waiting for transfers between devices  27.7 us (9%)
  Pallas kernels  19.4 us (6%)
  local copies, waits for them, and re-layouts  3.48 us (1%)
    ppermute x12, starting transfers between devices, shifted(): lax.ppermute(value, axis, [(i, (i + by) % count) for i in range(count)])  90.1 us
    all_gather x1, blocking collectives, block(): column = lax.all_gather(strided, 'zi', axis=0, tiled=True)  53.6 us
    all_to_all x2, blocking collectives, exchanged(): return lax.all_to_all(blocks, axes, split_axis=0, concat_axis=0, tiled=True)  50.8 us
    all_gather x1, blocking collectives, block(): gathered = lax.all_gather(placed, 'zo', axis=0, tiled=True)  43 us
    ppermute x12, waiting for transfers between devices, shifted(): lax.ppermute(value, axis, [(i, (i + by) % count) for i in range(count)])  26.9 us
    all_to_all x2, starting transfers between devices, exchanged(): return lax.all_to_all(blocks, axes, split_axis=0, concat_axis=0, tiled=True)  14.8 us
  transfers between devices with their start and end apart: 14, of which 9 were waited for; matrix products, arithmetic and copies ran while one was open for 0% of the time, Pallas kernels for 5%

profile of v10, /device:TPU:33, one launch (start us, length us, event | category | flops | bytes accessed | tf_op | source)
XLA Modules:
  0.0 304.4 jit_solution(8521211354075152285)
XLA Ops:
  0.0 2.9 split_rows.1
  2.9 43.4 %collective-permute-start.6 = (bf16[208,4096]{1,0:T(8,128)(2,1)}, bf16[208,4096]{1,0:T(8,128)(2,1)S(1)}, u32[]{:S(2)}, u32[]{:S(2)}) collective-permute-start(bf16[208,4096]{1,0:T(8,128)(2,1)} %bitcast.27), channel_id=1, source_target_pairs={{0,1},{1,0},{2,3},{3,2},{4,5},{5,4},{6,7},{7,6},{8,9},{9,8},{10,11... | collective-permute-start | bytes 5111816 | tf_op jit(solution)/shard_map/ppermute | solution.py:25
  46.3 1.5 token_copies.1
  47.8 3.6 %all-to-all-start = ((bf16[8,3,4224]{2,1,0:T(4,128)(2,1)}), bf16[8,3,4224]{2,1,0:T(4,128)(2,1)S(1)}, u32[]{:S(2)}, u32[]{:S(2)}) async-start(bf16[8,3,4224]{2,1,0:T(4,128)(2,1)} %token_copies.1), calls=%async_computation | async-start | bytes 540672 | tf_op jit(solution)/shard_map/all_to_all | solution.py:29
  51.4 2.3 cut_by_x.1
  53.7 2.8 collective-permute-start.7
  56.5 3.7 %collective-permute-start.8 = (bf16[64,3328]{1,0:T(8,128)(2,1)}, bf16[64,3328]{1,0:T(8,128)(2,1)S(1)}, u32[]{:S(2)}, u32[]{:S(2)}) collective-permute-start(bf16[64,3328]{1,0:T(8,128)(2,1)} %get-tuple-element.22), channel_id=1, source_target_pairs={{0,192},{64,0},{128,64},{192,128},{1,193},{65,1},{129,65},{193,129... | collective-permute-start | bytes 1277960 | tf_op jit(solution)/shard_map/ppermute | solution.py:25
  60.3 3.3 %collective-permute-start.9 = (bf16[64,3328]{1,0:T(8,128)(2,1)}, bf16[64,3328]{1,0:T(8,128)(2,1)S(1)}, u32[]{:S(2)}, u32[]{:S(2)}) collective-permute-start(bf16[64,3328]{1,0:T(8,128)(2,1)} %get-tuple-element.23), channel_id=1, source_target_pairs={{0,128},{64,192},{128,0},{192,64},{1,129},{65,193},{129,1},{193,65... | collective-permute-start | bytes 1277960 | tf_op jit(solution)/shard_map/ppermute | solution.py:25
  63.6 4.9 %collective-permute-done.7.refs_1_ = bf16[64,3328]{1,0:T(8,128)(2,1)S(1)} collective-permute-done((bf16[64,3328]{1,0:T(8,128)(2,1)}, bf16[64,3328]{1,0:T(8,128)(2,1)S(1)}, u32[]{:S(2)}, u32[]{:S(2)}) %collective-permute-start.7) | collective-permute-done | bytes 426016 | tf_op jit(solution)/shard_map/ppermute | solution.py:25
  68.4 1.4 collective-permute-done.8.refs_2_
  69.9 8.3 %collective-permute-done.9.refs_3_ = bf16[64,3328]{1,0:T(8,128)(2,1)S(1)} collective-permute-done((bf16[64,3328]{1,0:T(8,128)(2,1)}, bf16[64,3328]{1,0:T(8,128)(2,1)S(1)}, u32[]{:S(2)}, u32[]{:S(2)}) %collective-permute-start.9) | collective-permute-done | bytes 426016 | tf_op jit(solution)/shard_map/ppermute | solution.py:25
  78.2 0.0 collective-permute-done.6.refs_8_
  78.2 0.8 copy-done.10
  79.0 3.6 %cut_by_zi.1 = bf16[4,4,64,832]{3,2,1,0:T(8,128)(2,1)} custom-call(s32[1]{0:T(128)} %bitcast.7.x_ref, s32[1]{0:T(128)} %bitcast.gy_ref, bf16[64,3328]{1,0:T(8,128)(2,1)} %get-tuple-element.27.refs_0_, bf16[64,3328]{1,0:T(8,128)(2,1)} %copy-done.8, bf16[64,3328]{1,0:T(8,128)(2,1)} %copy-done.9, bf16[64,3328]{1,0:T(8,128)(2,1)} %copy-done.10), custom_call_target="tpu_custom_call" | custom-call | tf_op jit(solution)/shard_map/cut_by_zi/pallas_call | solution.py:143
  82.6 0.7 all-to-all-done
  83.3 11.2 %all-to-all-start.1 = ((bf16[4,4,64,832]{3,2,1,0:T(8,128)(2,1)}), bf16[4,4,64,832]{3,2,1,0:T(8,128)(2,1)S(1)}, u32[]{:S(2)}, u32[]{:S(2)}) async-start(bf16[4,4,64,832]{3,2,1,0:T(8,128)(2,1)} %cut_by_zi.1), calls=%async_computation.1 | async-start | bytes 3670016 | tf_op jit(solution)/shard_map/all_to_all | solution.py:29
  94.6 0.2 reshape.30
  94.7 53.6 %all_gather.6.refs_0_ = bf16[96,4224]{1,0:T(8,128)(2,1)S(1)} all-gather(bf16[24,4224]{1,0:T(8,128)(2,1)S(1)} %reshape.30), channel_id=1, replica_groups=mesh['rep'=2,'x'=4,'zo'=8,'zi'=4,'gy'=2] {'zi'}, dimensions={0}, use_global_device_ids=true | all-gather | bytes 1013760 | tf_op jit(solution)/shard_map/all_gather | solution.py:260
  148.4 0.1 fusion.2
  148.4 2.9 collective-permute-start
  151.4 3.7 %collective-permute-start.3 = (bf16[48,4224]{1,0:T(8,128)(2,1)S(1)}, bf16[48,4224]{1,0:T(8,128)(2,1)S(1)}, u32[]{:S(2)}, u32[]{:S(2)}) collective-permute-start(bf16[48,4224]{1,0:T(8,128)(2,1)S(1)} %get-tuple-element.35), channel_id=1, source_target_pairs={{0,192},{64,0},{128,64},{192,128},{1,193},{65,1},{129,65},{193,129... | collective-permute-start | bytes 1216520 | tf_op jit(solution)/shard_map/ppermute | solution.py:25
  155.0 2.0 collective-permute-start.1
  157.0 4.6 %collective-permute-start.2 = (bf16[48,4224]{1,0:T(8,128)(2,1)S(1)}, bf16[48,4224]{1,0:T(8,128)(2,1)S(1)}, u32[]{:S(2)}, u32[]{:S(2)}) collective-permute-start(bf16[48,4224]{1,0:T(8,128)(2,1)S(1)} %get-tuple-element.36), channel_id=1, source_target_pairs={{0,192},{64,0},{128,64},{192,128},{1,193},{65,1},{129,65},{193,129... | collective-permute-start | bytes 1216520 | tf_op jit(solution)/shard_map/ppermute | solution.py:25
  161.6 0.0 collective-permute-done.refs_1_
  161.6 2.0 collective-permute-start.4
  163.6 4.6 %collective-permute-start.5 = (bf16[48,4224]{1,0:T(8,128)(2,1)S(1)}, bf16[48,4224]{1,0:T(8,128)(2,1)S(1)}, u32[]{:S(2)}, u32[]{:S(2)}) collective-permute-start(bf16[48,4224]{1,0:T(8,128)(2,1)S(1)} %collective-permute-done.3.refs_4_), channel_id=1, source_target_pairs={{0,192},{64,0},{128,64},{192,128},{1,193},{65,1},{129,65},{193,129... | collective-permute-start | bytes 1216520 | tf_op jit(solution)/shard_map/ppermute | solution.py:25
  168.2 1.3 collective-permute-done.1.refs_2_
  169.5 1.0 collective-permute-done.2.refs_3_
  170.6 7.7 %collective-permute-done.4.refs_5_ = bf16[48,4224]{1,0:T(8,128)(2,1)S(1)} collective-permute-done((bf16[48,4224]{1,0:T(8,128)(2,1)S(1)}, bf16[48,4224]{1,0:T(8,128)(2,1)S(1)}, u32[]{:S(2)}, u32[]{:S(2)}) %collective-permute-start.4) | collective-permute-done | bytes 405536 | tf_op jit(solution)/shard_map/ppermute | solution.py:25
  178.2 1.0 collective-permute-done.5.refs_6_
  179.3 0.8 copy-done.7
  180.0 5.1 %values.1 = (f32[208,384]{1,0:T(8,128)}, f32[208,384]{1,0:T(8,128)}) custom-call(bf16[96,4224]{1,0:T(8,128)(2,1)} %copy-done, bf16[48,4224]{1,0:T(8,128)(2,1)} %copy-done.2, bf16[48,4224]{1,0:T(8,128)(2,1)} %copy-done.4, bf16[48,4224]{1,0:T(8,128)(2,1)} %copy-done.5, bf16[48,4224]{1,0:T(8,128)(2,1)} %copy-done.3, bf16[48,4224]{1,0:T(8,128)(2,1)} %copy-done.6, ...), custom_call_target="tpu_custom_call" | custom-call | tf_op jit(solution)/shard_map/values/pallas_call | solution.py:219
  185.1 5.1 %collective-permute-start.10 = (f32[208,384]{1,0:T(8,128)}, f32[208,384]{1,0:T(8,128)S(1)}, u32[]{:S(2)}, u32[]{:S(2)}) collective-permute-start(f32[208,384]{1,0:T(8,128)} %get-tuple-element.26), channel_id=1, source_target_pairs={{0,1},{1,0},{2,3},{3,2},{4,5},{5,4},{6,7},{7,6},{8,9},{9,8},{10,11... | collective-permute-start | bytes 958472 | tf_op jit(solution)/shard_map/ppermute | solution.py:25
  190.3 1.9 placement.1.place_ref
  192.2 0.7 copy-done.11
  192.9 2.0 placed_hidden.1
  194.9 43.0 %all_gather.7 = bf16[832,384]{1,0:T(8,128)(2,1)S(1)} all-gather(bf16[104,384]{1,0:T(8,128)(2,1)} %placed_hidden.1), channel_id=1, replica_groups=mesh['rep'=2,'x'=4,'zo'=8,'zi'=4,'gy'=2] {'zo'}, dimensions={0}, use_global_device_ids=true | all-gather | bytes 718848 | tf_op jit(solution)/shard_map/all_gather | solution.py:278
  237.9 1.0 fusion.4
  239.0 0.1 fusion.3
  239.1 12.2 %collective-permute-start.11 = (bf16[384,512]{1,0:T(8,128)(2,1)S(1)}, bf16[384,512]{1,0:T(8,128)(2,1)S(1)}, u32[]{:S(2)}, u32[]{:S(2)}) collective-permute-start(bf16[384,512]{1,0:T(8,128)(2,1)S(1)} %pad_maximum_fusion), channel_id=1, source_target_pairs={{0,1},{1,0},{2,3},{3,2},{4,5},{5,4},{6,7},{7,6},{8,9},{9,8},{10,11... | collective-permute-start | bytes 1179656 | tf_op jit(solution)/shard_map/ppermute | solution.py:25
  251.3 0.1 fusion.1
  251.3 1.3 collective-permute-done.11
  252.6 0.1 fusion
  252.7 17.4 %all_to_all.20 = bf16[16,24,512]{2,1,0:T(8,128)(2,1)S(1)} all-to-all(bf16[16,24,512]{2,1,0:T(8,128)(2,1)S(1)} %bitcast.25), channel_id=1, replica_groups=mesh['rep'=2,'x'=4,'zo'=8,'zi'=4,'gy'=2] {'x','zi'}, dimensions={0} | all-to-all | bytes 786432 | tf_op jit(solution)/shard_map/all_to_all | solution.py:29
  270.1 0.1 reduce_sum.12
  270.2 33.4 %all_to_all.21 = bf16[8,3,512]{2,1,0:T(4,128)(2,1)S(1)} all-to-all(bf16[8,3,512]{2,1,0:T(4,128)(2,1)S(1)} %reshape.37), channel_id=1, replica_groups=mesh['rep'=2,'x'=4,'zo'=8,'zi'=4,'gy'=2] {'zo'}, dimensions={0} | all-to-all | bytes 49152 | tf_op jit(solution)/shard_map/all_to_all | solution.py:29
  303.6 0.1 reshape.38
  303.7 0.7 reshape.39
  (28 shorter events, 0.1 us)
Async XLA Ops:
  2.9 75.3 %collective-permute-start.6 = (bf16[208,4096]{1,0:T(8,128)(2,1)}, bf16[208,4096]{1,0:T(8,128)(2,1)S(1)}, u32[]{:S(2)}, u32[]{:S(2)}) collective-permute-start(bf16[208,4096]{1,0:T(8,128)(2,1)} %bitcast.27), channel_id=1, source_target_pairs={{0,1},{1,0},{2,3},{3,2},{4,5},{5,4},{6,7},{7,6},{8,9},{9,8},{10,11... | collective-permute-start | bytes 5111816 | tf_op jit(solution)/shard_map/ppermute | solution.py:25
  47.8 35.5 %all-to-all-start = ((bf16[8,3,4224]{2,1,0:T(4,128)(2,1)}), bf16[8,3,4224]{2,1,0:T(4,128)(2,1)S(1)}, u32[]{:S(2)}, u32[]{:S(2)}) async-start(bf16[8,3,4224]{2,1,0:T(4,128)(2,1)} %token_copies.1), calls=%async_computation | async-start | bytes 540672 | tf_op jit(solution)/shard_map/all_to_all | solution.py:29
  53.7 14.7 %collective-permute-start.7 = (bf16[64,3328]{1,0:T(8,128)(2,1)}, bf16[64,3328]{1,0:T(8,128)(2,1)S(1)}, u32[]{:S(2)}, u32[]{:S(2)}) collective-permute-start(bf16[64,3328]{1,0:T(8,128)(2,1)} %get-tuple-element.21), channel_id=1, source_target_pairs={{0,64},{64,128},{128,192},{192,0},{1,65},{65,129},{129,193},{193,1... | collective-permute-start | bytes 1277960 | tf_op jit(solution)/shard_map/ppermute | solution.py:25
  56.5 13.3 %collective-permute-start.8 = (bf16[64,3328]{1,0:T(8,128)(2,1)}, bf16[64,3328]{1,0:T(8,128)(2,1)S(1)}, u32[]{:S(2)}, u32[]{:S(2)}) collective-permute-start(bf16[64,3328]{1,0:T(8,128)(2,1)} %get-tuple-element.22), channel_id=1, source_target_pairs={{0,192},{64,0},{128,64},{192,128},{1,193},{65,1},{129,65},{193,129... | collective-permute-start | bytes 1277960 | tf_op jit(solution)/shard_map/ppermute | solution.py:25
  60.3 17.9 %collective-permute-start.9 = (bf16[64,3328]{1,0:T(8,128)(2,1)}, bf16[64,3328]{1,0:T(8,128)(2,1)S(1)}, u32[]{:S(2)}, u32[]{:S(2)}) collective-permute-start(bf16[64,3328]{1,0:T(8,128)(2,1)} %get-tuple-element.23), channel_id=1, source_target_pairs={{0,128},{64,192},{128,0},{192,64},{1,129},{65,193},{129,1},{193,65... | collective-permute-start | bytes 1277960 | tf_op jit(solution)/shard_map/ppermute | solution.py:25
  68.4 9.8 %copy-start.8 = (bf16[64,3328]{1,0:T(8,128)(2,1)}, bf16[64,3328]{1,0:T(8,128)(2,1)S(1)}, u32[]{:S(2)}) copy-start(bf16[64,3328]{1,0:T(8,128)(2,1)S(1)} %collective-permute-done.7.refs_1_) | copy-start | bytes 1277956
  69.9 8.3 %copy-start.9 = (bf16[64,3328]{1,0:T(8,128)(2,1)}, bf16[64,3328]{1,0:T(8,128)(2,1)S(1)}, u32[]{:S(2)}) copy-start(bf16[64,3328]{1,0:T(8,128)(2,1)S(1)} %collective-permute-done.8.refs_2_) | copy-start | bytes 1277956
  78.2 0.8 copy-start.10
  78.2 4.4 %copy-start.1 = (bf16[208,4096]{1,0:T(8,128)(2,1)}, bf16[208,4096]{1,0:T(8,128)(2,1)S(1)}, u32[]{:S(2)}) copy-start(bf16[208,4096]{1,0:T(8,128)(2,1)S(1)} %collective-permute-done.6.refs_8_) | copy-start | bytes 5111812
  83.3 154.6 %all-to-all-start.1 = ((bf16[4,4,64,832]{3,2,1,0:T(8,128)(2,1)}), bf16[4,4,64,832]{3,2,1,0:T(8,128)(2,1)S(1)}, u32[]{:S(2)}, u32[]{:S(2)}) async-start(bf16[4,4,64,832]{3,2,1,0:T(8,128)(2,1)} %cut_by_zi.1), calls=%async_computation.1 | async-start | bytes 3670016 | tf_op jit(solution)/shard_map/all_to_all | solution.py:29
  148.4 31.6 %copy-start = (bf16[96,4224]{1,0:T(8,128)(2,1)}, bf16[96,4224]{1,0:T(8,128)(2,1)S(1)}, u32[]{:S(2)}) copy-start(bf16[96,4224]{1,0:T(8,128)(2,1)S(1)} %all_gather.6.refs_0_) | copy-start | bytes 2433028
  148.4 13.1 %collective-permute-start = (bf16[48,4224]{1,0:T(8,128)(2,1)S(1)}, bf16[48,4224]{1,0:T(8,128)(2,1)S(1)}, u32[]{:S(2)}, u32[]{:S(2)}) collective-permute-start(bf16[48,4224]{1,0:T(8,128)(2,1)S(1)} %get-tuple-element.36), channel_id=1, source_target_pairs={{0,64},{64,128},{128,192},{192,0},{1,65},{65,129},{129,193},{193,1... | collective-permute-start | bytes 1216520 | tf_op jit(solution)/shard_map/ppermute | solution.py:25
  151.4 12.2 %collective-permute-start.3 = (bf16[48,4224]{1,0:T(8,128)(2,1)S(1)}, bf16[48,4224]{1,0:T(8,128)(2,1)S(1)}, u32[]{:S(2)}, u32[]{:S(2)}) collective-permute-start(bf16[48,4224]{1,0:T(8,128)(2,1)S(1)} %get-tuple-element.35), channel_id=1, source_target_pairs={{0,192},{64,0},{128,64},{192,128},{1,193},{65,1},{129,65},{193,129... | collective-permute-start | bytes 1216520 | tf_op jit(solution)/shard_map/ppermute | solution.py:25
  155.0 14.5 %collective-permute-start.1 = (bf16[48,4224]{1,0:T(8,128)(2,1)S(1)}, bf16[48,4224]{1,0:T(8,128)(2,1)S(1)}, u32[]{:S(2)}, u32[]{:S(2)}) collective-permute-start(bf16[48,4224]{1,0:T(8,128)(2,1)S(1)} %get-tuple-element.35), channel_id=1, source_target_pairs={{0,64},{64,128},{128,192},{192,0},{1,65},{65,129},{129,193},{193,1... | collective-permute-start | bytes 1216520 | tf_op jit(solution)/shard_map/ppermute | solution.py:25
  157.0 13.6 %collective-permute-start.2 = (bf16[48,4224]{1,0:T(8,128)(2,1)S(1)}, bf16[48,4224]{1,0:T(8,128)(2,1)S(1)}, u32[]{:S(2)}, u32[]{:S(2)}) collective-permute-start(bf16[48,4224]{1,0:T(8,128)(2,1)S(1)} %get-tuple-element.36), channel_id=1, source_target_pairs={{0,192},{64,0},{128,64},{192,128},{1,193},{65,1},{129,65},{193,129... | collective-permute-start | bytes 1216520 | tf_op jit(solution)/shard_map/ppermute | solution.py:25
  161.6 18.4 %copy-start.2 = (bf16[48,4224]{1,0:T(8,128)(2,1)}, bf16[48,4224]{1,0:T(8,128)(2,1)S(1)}, u32[]{:S(2)}) copy-start(bf16[48,4224]{1,0:T(8,128)(2,1)S(1)} %collective-permute-done.refs_1_) | copy-start | bytes 1216516
  161.6 16.6 %collective-permute-start.4 = (bf16[48,4224]{1,0:T(8,128)(2,1)S(1)}, bf16[48,4224]{1,0:T(8,128)(2,1)S(1)}, u32[]{:S(2)}, u32[]{:S(2)}) collective-permute-start(bf16[48,4224]{1,0:T(8,128)(2,1)S(1)} %collective-permute-done.refs_1_), channel_id=1, source_target_pairs={{0,64},{64,128},{128,192},{192,0},{1,65},{65,129},{129,193},{193,1... | collective-permute-start | bytes 1216520 | tf_op jit(solution)/shard_map/ppermute | solution.py:25
  163.6 16.5 %copy-start.3 = (bf16[48,4224]{1,0:T(8,128)(2,1)}, bf16[48,4224]{1,0:T(8,128)(2,1)S(1)}, u32[]{:S(2)}) copy-start(bf16[48,4224]{1,0:T(8,128)(2,1)S(1)} %collective-permute-done.3.refs_4_) | copy-start | bytes 1216516
  163.6 15.7 %collective-permute-start.5 = (bf16[48,4224]{1,0:T(8,128)(2,1)S(1)}, bf16[48,4224]{1,0:T(8,128)(2,1)S(1)}, u32[]{:S(2)}, u32[]{:S(2)}) collective-permute-start(bf16[48,4224]{1,0:T(8,128)(2,1)S(1)} %collective-permute-done.3.refs_4_), channel_id=1, source_target_pairs={{0,192},{64,0},{128,64},{192,128},{1,193},{65,1},{129,65},{193,129... | collective-permute-start | bytes 1216520 | tf_op jit(solution)/shard_map/ppermute | solution.py:25
  169.5 9.7 %copy-start.4 = (bf16[48,4224]{1,0:T(8,128)(2,1)}, bf16[48,4224]{1,0:T(8,128)(2,1)S(1)}, u32[]{:S(2)}) copy-start(bf16[48,4224]{1,0:T(8,128)(2,1)S(1)} %collective-permute-done.1.refs_2_) | copy-start | bytes 1216516
  170.6 8.7 %copy-start.5 = (bf16[48,4224]{1,0:T(8,128)(2,1)}, bf16[48,4224]{1,0:T(8,128)(2,1)S(1)}, u32[]{:S(2)}) copy-start(bf16[48,4224]{1,0:T(8,128)(2,1)S(1)} %collective-permute-done.2.refs_3_) | copy-start | bytes 1216516
  178.2 1.0 copy-start.6
  179.3 0.8 copy-start.7
  185.1 7.1 %collective-permute-start.10 = (f32[208,384]{1,0:T(8,128)}, f32[208,384]{1,0:T(8,128)S(1)}, u32[]{:S(2)}, u32[]{:S(2)}) collective-permute-start(f32[208,384]{1,0:T(8,128)} %get-tuple-element.26), channel_id=1, source_target_pairs={{0,1},{1,0},{2,3},{3,2},{4,5},{5,4},{6,7},{7,6},{8,9},{9,8},{10,11... | collective-permute-start | bytes 958472 | tf_op jit(solution)/shard_map/ppermute | solution.py:25
  192.2 0.7 copy-start.11
  239.1 13.5 %collective-permute-start.11 = (bf16[384,512]{1,0:T(8,128)(2,1)S(1)}, bf16[384,512]{1,0:T(8,128)(2,1)S(1)}, u32[]{:S(2)}, u32[]{:S(2)}) collective-permute-start(bf16[384,512]{1,0:T(8,128)(2,1)S(1)} %pad_maximum_fusion), channel_id=1, source_target_pairs={{0,1},{1,0},{2,3},{3,2},{4,5},{5,4},{6,7},{7,6},{8,9},{9,8},{10,11... | collective-permute-start | bytes 1179656 | tf_op jit(solution)/shard_map/ppermute | solution.py:25

commit v11 on v10

--- a/solution.py
+++ b/solution.py
@@ -226,20 +226,11 @@
     )(*chunks, own_rows, other_rows)
 
 
-def hidden_kernel(own_ref, other_ref, place_ref, out_ref):
-    value = own_ref[...] + other_ref[...]
-    width = value.shape[0] // 2
-    gate_value, up_value = value[:width], value[width:]
+def placed_hidden(own_value, other_value, place):
+    value = own_value + other_value
+    gate_value, up_value = jnp.split(value, 2, axis=0)
     hidden = (gate_value / (1 + jnp.exp(-gate_value)) * up_value).astype(BF16)
-    out_ref[...] = jnp.dot(hidden, place_ref[...], preferred_element_type=F32).astype(BF16)
-
-
-def placed_hidden(own_value, other_value, place):
-    return pl.pallas_call(
-        hidden_kernel,
-        out_shape=jax.ShapeDtypeStruct((own_value.shape[0] // 2, place.shape[1]), BF16),
-        name="placed_hidden",
-    )(own_value, other_value, place)
+    return jnp.dot(hidden, place, preferred_element_type=F32).astype(BF16)
 
 
 def block(tokens, segment_ids, gate_weight, up_weight, down_weight):

time: 306 us -> 304 us (level)
  no operation moved by 1% of the time
where the time goes in v11:
time: 304 us; the launch traced here: 303 us
  blocking collectives  148 us (49%)
  starting transfers between devices  104 us (34%)
  waiting for transfers between devices  27.7 us (9%)
  Pallas kernels  17.4 us (6%)
    ppermute x12, starting transfers between devices, shifted(): lax.ppermute(value, axis, [(i, (i + by) % count) for i in range(count)])  89.5 us
    all_gather x1, blocking collectives, block(): column = lax.all_gather(strided, 'zi', axis=0, tiled=True)  53.6 us
    all_to_all x2, blocking collectives, exchanged(): return lax.all_to_all(blocks, axes, split_axis=0, concat_axis=0, tiled=True)  52 us
    all_gather x1, blocking collectives, block(): gathered = lax.all_gather(placed, 'zo', axis=0, tiled=True)  42.5 us
    ppermute x12, waiting for transfers between devices, shifted(): lax.ppermute(value, axis, [(i, (i + by) % count) for i in range(count)])  26.9 us
    all_to_all x2, starting transfers between devices, exchanged(): return lax.all_to_all(blocks, axes, split_axis=0, concat_axis=0, tiled=True)  14.8 us
  transfers between devices with their start and end apart: 14, of which 9 were waited for; matrix products, arithmetic and copies ran while one was open for 0% of the time, Pallas kernels for 5%

profile of v11, /device:TPU:33, one launch (start us, length us, event | category | flops | bytes accessed | tf_op | source)
XLA Modules:
  0.0 303.1 jit_solution(11114513980007934244)
XLA Ops:
  0.0 2.9 split_rows.1
  2.9 43.4 %collective-permute-start.6 = (bf16[208,4096]{1,0:T(8,128)(2,1)}, bf16[208,4096]{1,0:T(8,128)(2,1)S(1)}, u32[]{:S(2)}, u32[]{:S(2)}) collective-permute-start(bf16[208,4096]{1,0:T(8,128)(2,1)} %bitcast.28), channel_id=1, source_target_pairs={{0,1},{1,0},{2,3},{3,2},{4,5},{5,4},{6,7},{7,6},{8,9},{9,8},{10,11... | collective-permute-start | bytes 5111816 | tf_op jit(solution)/shard_map/ppermute | solution.py:25
  46.3 1.5 token_copies.1
  47.8 3.6 %all-to-all-start = ((bf16[8,3,4224]{2,1,0:T(4,128)(2,1)}), bf16[8,3,4224]{2,1,0:T(4,128)(2,1)S(1)}, u32[]{:S(2)}, u32[]{:S(2)}) async-start(bf16[8,3,4224]{2,1,0:T(4,128)(2,1)} %token_copies.1), calls=%async_computation | async-start | bytes 540672 | tf_op jit(solution)/shard_map/all_to_all | solution.py:29
  51.4 2.3 cut_by_x.1
  53.7 2.8 collective-permute-start.7
  56.5 3.7 %collective-permute-start.8 = (bf16[64,3328]{1,0:T(8,128)(2,1)}, bf16[64,3328]{1,0:T(8,128)(2,1)S(1)}, u32[]{:S(2)}, u32[]{:S(2)}) collective-permute-start(bf16[64,3328]{1,0:T(8,128)(2,1)} %get-tuple-element.22), channel_id=1, source_target_pairs={{0,192},{64,0},{128,64},{192,128},{1,193},{65,1},{129,65},{193,129... | collective-permute-start | bytes 1277960 | tf_op jit(solution)/shard_map/ppermute | solution.py:25
  60.3 3.3 %collective-permute-start.9 = (bf16[64,3328]{1,0:T(8,128)(2,1)}, bf16[64,3328]{1,0:T(8,128)(2,1)S(1)}, u32[]{:S(2)}, u32[]{:S(2)}) collective-permute-start(bf16[64,3328]{1,0:T(8,128)(2,1)} %get-tuple-element.23), channel_id=1, source_target_pairs={{0,128},{64,192},{128,0},{192,64},{1,129},{65,193},{129,1},{193,65... | collective-permute-start | bytes 1277960 | tf_op jit(solution)/shard_map/ppermute | solution.py:25
  63.6 4.9 %collective-permute-done.7.refs_1_ = bf16[64,3328]{1,0:T(8,128)(2,1)S(1)} collective-permute-done((bf16[64,3328]{1,0:T(8,128)(2,1)}, bf16[64,3328]{1,0:T(8,128)(2,1)S(1)}, u32[]{:S(2)}, u32[]{:S(2)}) %collective-permute-start.7) | collective-permute-done | bytes 426016 | tf_op jit(solution)/shard_map/ppermute | solution.py:25
  68.4 1.4 collective-permute-done.8.refs_2_
  69.9 8.3 %collective-permute-done.9.refs_3_ = bf16[64,3328]{1,0:T(8,128)(2,1)S(1)} collective-permute-done((bf16[64,3328]{1,0:T(8,128)(2,1)}, bf16[64,3328]{1,0:T(8,128)(2,1)S(1)}, u32[]{:S(2)}, u32[]{:S(2)}) %collective-permute-start.9) | collective-permute-done | bytes 426016 | tf_op jit(solution)/shard_map/ppermute | solution.py:25
  78.2 0.0 collective-permute-done.6.refs_8_
  78.2 0.8 copy-done.10
  79.0 3.6 %cut_by_zi.1 = bf16[4,4,64,832]{3,2,1,0:T(8,128)(2,1)} custom-call(s32[1]{0:T(128)} %bitcast.7.x_ref, s32[1]{0:T(128)} %bitcast.gy_ref, bf16[64,3328]{1,0:T(8,128)(2,1)} %get-tuple-element.27.refs_0_, bf16[64,3328]{1,0:T(8,128)(2,1)} %copy-done.8, bf16[64,3328]{1,0:T(8,128)(2,1)} %copy-done.9, bf16[64,3328]{1,0:T(8,128)(2,1)} %copy-done.10), custom_call_target="tpu_custom_call" | custom-call | tf_op jit(solution)/shard_map/cut_by_zi/pallas_call | solution.py:143
  82.6 0.7 all-to-all-done
  83.3 11.2 %all-to-all-start.1 = ((bf16[4,4,64,832]{3,2,1,0:T(8,128)(2,1)}), bf16[4,4,64,832]{3,2,1,0:T(8,128)(2,1)S(1)}, u32[]{:S(2)}, u32[]{:S(2)}) async-start(bf16[4,4,64,832]{3,2,1,0:T(8,128)(2,1)} %cut_by_zi.1), calls=%async_computation.1 | async-start | bytes 3670016 | tf_op jit(solution)/shard_map/all_to_all | solution.py:29
  94.6 0.2 reshape.30
  94.7 53.6 %all_gather.6.refs_0_ = bf16[96,4224]{1,0:T(8,128)(2,1)S(1)} all-gather(bf16[24,4224]{1,0:T(8,128)(2,1)S(1)} %reshape.30), channel_id=1, replica_groups=mesh['rep'=2,'x'=4,'zo'=8,'zi'=4,'gy'=2] {'zi'}, dimensions={0}, use_global_device_ids=true | all-gather | bytes 1013760 | tf_op jit(solution)/shard_map/all_gather | solution.py:251
  148.4 0.1 fusion.6
  148.4 2.9 collective-permute-start
  151.4 3.7 %collective-permute-start.3 = (bf16[48,4224]{1,0:T(8,128)(2,1)S(1)}, bf16[48,4224]{1,0:T(8,128)(2,1)S(1)}, u32[]{:S(2)}, u32[]{:S(2)}) collective-permute-start(bf16[48,4224]{1,0:T(8,128)(2,1)S(1)} %get-tuple-element.35), channel_id=1, source_target_pairs={{0,192},{64,0},{128,64},{192,128},{1,193},{65,1},{129,65},{193,129... | collective-permute-start | bytes 1216520 | tf_op jit(solution)/shard_map/ppermute | solution.py:25
  155.0 2.0 collective-permute-start.1
  157.0 4.6 %collective-permute-start.2 = (bf16[48,4224]{1,0:T(8,128)(2,1)S(1)}, bf16[48,4224]{1,0:T(8,128)(2,1)S(1)}, u32[]{:S(2)}, u32[]{:S(2)}) collective-permute-start(bf16[48,4224]{1,0:T(8,128)(2,1)S(1)} %get-tuple-element.36), channel_id=1, source_target_pairs={{0,192},{64,0},{128,64},{192,128},{1,193},{65,1},{129,65},{193,129... | collective-permute-start | bytes 1216520 | tf_op jit(solution)/shard_map/ppermute | solution.py:25
  161.6 0.0 collective-permute-done.refs_1_
  161.6 2.0 collective-permute-start.4
  163.6 0.0 collective-permute-done.3.refs_4_
  163.6 4.6 %collective-permute-start.5 = (bf16[48,4224]{1,0:T(8,128)(2,1)S(1)}, bf16[48,4224]{1,0:T(8,128)(2,1)S(1)}, u32[]{:S(2)}, u32[]{:S(2)}) collective-permute-start(bf16[48,4224]{1,0:T(8,128)(2,1)S(1)} %collective-permute-done.3.refs_4_), channel_id=1, source_target_pairs={{0,192},{64,0},{128,64},{192,128},{1,193},{65,1},{129,65},{193,129... | collective-permute-start | bytes 1216520 | tf_op jit(solution)/shard_map/ppermute | solution.py:25
  168.2 1.3 collective-permute-done.1.refs_2_
  169.5 1.0 collective-permute-done.2.refs_3_
  170.6 7.7 %collective-permute-done.4.refs_5_ = bf16[48,4224]{1,0:T(8,128)(2,1)S(1)} collective-permute-done((bf16[48,4224]{1,0:T(8,128)(2,1)S(1)}, bf16[48,4224]{1,0:T(8,128)(2,1)S(1)}, u32[]{:S(2)}, u32[]{:S(2)}) %collective-permute-start.4) | collective-permute-done | bytes 405536 | tf_op jit(solution)/shard_map/ppermute | solution.py:25
  178.2 1.0 collective-permute-done.5.refs_6_
  179.3 0.8 copy-done.7
  180.0 5.1 %values.1 = (f32[208,384]{1,0:T(8,128)}, f32[208,384]{1,0:T(8,128)}) custom-call(bf16[96,4224]{1,0:T(8,128)(2,1)} %copy-done, bf16[48,4224]{1,0:T(8,128)(2,1)} %copy-done.2, bf16[48,4224]{1,0:T(8,128)(2,1)} %copy-done.4, bf16[48,4224]{1,0:T(8,128)(2,1)} %copy-done.5, bf16[48,4224]{1,0:T(8,128)(2,1)} %copy-done.3, bf16[48,4224]{1,0:T(8,128)(2,1)} %copy-done.6, ...), custom_call_target="tpu_custom_call" | custom-call | tf_op jit(solution)/shard_map/values/pallas_call | solution.py:219
  185.1 5.3 %collective-permute-start.10 = (f32[208,384]{1,0:T(8,128)}, f32[208,384]{1,0:T(8,128)S(1)}, u32[]{:S(2)}, u32[]{:S(2)}) collective-permute-start(f32[208,384]{1,0:T(8,128)} %get-tuple-element.26), channel_id=1, source_target_pairs={{0,1},{1,0},{2,3},{3,2},{4,5},{5,4},{6,7},{7,6},{8,9},{9,8},{10,11... | collective-permute-start | bytes 958472 | tf_op jit(solution)/shard_map/ppermute | solution.py:25
  190.4 1.9 placement.1
  192.4 1.2 convolution_convert_fusion
  193.6 42.5 %all_gather.7 = bf16[832,384]{1,0:T(8,128)(2,1)S(1)} all-gather(bf16[104,384]{1,0:T(8,128)(2,1)S(1)} %convolution_convert_fusion), channel_id=1, replica_groups=mesh['rep'=2,'x'=4,'zo'=8,'zi'=4,'gy'=2] {'zo'}, dimensions={0}, use_global_device_ids=true | all-gather | bytes 718848 | tf_op jit(solution)/shard_map/all_gather | solution.py:269
  236.1 1.0 fusion.8
  237.1 0.1 fusion.7
  237.3 11.4 %collective-permute-start.11 = (bf16[384,512]{1,0:T(8,128)(2,1)S(1)}, bf16[384,512]{1,0:T(8,128)(2,1)S(1)}, u32[]{:S(2)}, u32[]{:S(2)}) collective-permute-start(bf16[384,512]{1,0:T(8,128)(2,1)S(1)} %pad_maximum_fusion), channel_id=1, source_target_pairs={{0,1},{1,0},{2,3},{3,2},{4,5},{5,4},{6,7},{7,6},{8,9},{9,8},{10,11... | collective-permute-start | bytes 1179656 | tf_op jit(solution)/shard_map/ppermute | solution.py:25
  248.7 0.1 fusion.5
  248.7 1.3 collective-permute-done.11
  250.0 0.1 fusion
  250.1 18.9 %all_to_all.20 = bf16[16,24,512]{2,1,0:T(8,128)(2,1)S(1)} all-to-all(bf16[16,24,512]{2,1,0:T(8,128)(2,1)S(1)} %bitcast.26), channel_id=1, replica_groups=mesh['rep'=2,'x'=4,'zo'=8,'zi'=4,'gy'=2] {'x','zi'}, dimensions={0} | all-to-all | bytes 786432 | tf_op jit(solution)/shard_map/all_to_all | solution.py:29
  269.0 0.1 reduce_sum.12
  269.1 33.1 %all_to_all.21 = bf16[8,3,512]{2,1,0:T(4,128)(2,1)S(1)} all-to-all(bf16[8,3,512]{2,1,0:T(4,128)(2,1)S(1)} %reshape.37), channel_id=1, replica_groups=mesh['rep'=2,'x'=4,'zo'=8,'zi'=4,'gy'=2] {'zo'}, dimensions={0} | all-to-all | bytes 49152 | tf_op jit(solution)/shard_map/all_to_all | solution.py:29
  302.2 0.1 reshape.38
  302.3 0.7 reshape.39
  (29 shorter events, 0.2 us)
Async XLA Ops:
  2.9 75.3 %collective-permute-start.6 = (bf16[208,4096]{1,0:T(8,128)(2,1)}, bf16[208,4096]{1,0:T(8,128)(2,1)S(1)}, u32[]{:S(2)}, u32[]{:S(2)}) collective-permute-start(bf16[208,4096]{1,0:T(8,128)(2,1)} %bitcast.28), channel_id=1, source_target_pairs={{0,1},{1,0},{2,3},{3,2},{4,5},{5,4},{6,7},{7,6},{8,9},{9,8},{10,11... | collective-permute-start | bytes 5111816 | tf_op jit(solution)/shard_map/ppermute | solution.py:25
  47.8 35.5 %all-to-all-start = ((bf16[8,3,4224]{2,1,0:T(4,128)(2,1)}), bf16[8,3,4224]{2,1,0:T(4,128)(2,1)S(1)}, u32[]{:S(2)}, u32[]{:S(2)}) async-start(bf16[8,3,4224]{2,1,0:T(4,128)(2,1)} %token_copies.1), calls=%async_computation | async-start | bytes 540672 | tf_op jit(solution)/shard_map/all_to_all | solution.py:29
  53.7 14.7 %collective-permute-start.7 = (bf16[64,3328]{1,0:T(8,128)(2,1)}, bf16[64,3328]{1,0:T(8,128)(2,1)S(1)}, u32[]{:S(2)}, u32[]{:S(2)}) collective-permute-start(bf16[64,3328]{1,0:T(8,128)(2,1)} %get-tuple-element.21), channel_id=1, source_target_pairs={{0,64},{64,128},{128,192},{192,0},{1,65},{65,129},{129,193},{193,1... | collective-permute-start | bytes 1277960 | tf_op jit(solution)/shard_map/ppermute | solution.py:25
  56.5 13.3 %collective-permute-start.8 = (bf16[64,3328]{1,0:T(8,128)(2,1)}, bf16[64,3328]{1,0:T(8,128)(2,1)S(1)}, u32[]{:S(2)}, u32[]{:S(2)}) collective-permute-start(bf16[64,3328]{1,0:T(8,128)(2,1)} %get-tuple-element.22), channel_id=1, source_target_pairs={{0,192},{64,0},{128,64},{192,128},{1,193},{65,1},{129,65},{193,129... | collective-permute-start | bytes 1277960 | tf_op jit(solution)/shard_map/ppermute | solution.py:25
  60.3 17.9 %collective-permute-start.9 = (bf16[64,3328]{1,0:T(8,128)(2,1)}, bf16[64,3328]{1,0:T(8,128)(2,1)S(1)}, u32[]{:S(2)}, u32[]{:S(2)}) collective-permute-start(bf16[64,3328]{1,0:T(8,128)(2,1)} %get-tuple-element.23), channel_id=1, source_target_pairs={{0,128},{64,192},{128,0},{192,64},{1,129},{65,193},{129,1},{193,65... | collective-permute-start | bytes 1277960 | tf_op jit(solution)/shard_map/ppermute | solution.py:25
  68.4 9.8 %copy-start.8 = (bf16[64,3328]{1,0:T(8,128)(2,1)}, bf16[64,3328]{1,0:T(8,128)(2,1)S(1)}, u32[]{:S(2)}) copy-start(bf16[64,3328]{1,0:T(8,128)(2,1)S(1)} %collective-permute-done.7.refs_1_) | copy-start | bytes 1277956
  69.9 8.3 %copy-start.9 = (bf16[64,3328]{1,0:T(8,128)(2,1)}, bf16[64,3328]{1,0:T(8,128)(2,1)S(1)}, u32[]{:S(2)}) copy-start(bf16[64,3328]{1,0:T(8,128)(2,1)S(1)} %collective-permute-done.8.refs_2_) | copy-start | bytes 1277956
  78.2 0.8 copy-start.10
  78.2 4.4 %copy-start.1 = (bf16[208,4096]{1,0:T(8,128)(2,1)}, bf16[208,4096]{1,0:T(8,128)(2,1)S(1)}, u32[]{:S(2)}) copy-start(bf16[208,4096]{1,0:T(8,128)(2,1)S(1)} %collective-permute-done.6.refs_8_) | copy-start | bytes 5111812
  83.3 152.7 %all-to-all-start.1 = ((bf16[4,4,64,832]{3,2,1,0:T(8,128)(2,1)}), bf16[4,4,64,832]{3,2,1,0:T(8,128)(2,1)S(1)}, u32[]{:S(2)}, u32[]{:S(2)}) async-start(bf16[4,4,64,832]{3,2,1,0:T(8,128)(2,1)} %cut_by_zi.1), calls=%async_computation.1 | async-start | bytes 3670016 | tf_op jit(solution)/shard_map/all_to_all | solution.py:29
  148.4 31.6 %copy-start = (bf16[96,4224]{1,0:T(8,128)(2,1)}, bf16[96,4224]{1,0:T(8,128)(2,1)S(1)}, u32[]{:S(2)}) copy-start(bf16[96,4224]{1,0:T(8,128)(2,1)S(1)} %all_gather.6.refs_0_) | copy-start | bytes 2433028
  148.4 13.1 %collective-permute-start = (bf16[48,4224]{1,0:T(8,128)(2,1)S(1)}, bf16[48,4224]{1,0:T(8,128)(2,1)S(1)}, u32[]{:S(2)}, u32[]{:S(2)}) collective-permute-start(bf16[48,4224]{1,0:T(8,128)(2,1)S(1)} %get-tuple-element.36), channel_id=1, source_target_pairs={{0,64},{64,128},{128,192},{192,0},{1,65},{65,129},{129,193},{193,1... | collective-permute-start | bytes 1216520 | tf_op jit(solution)/shard_map/ppermute | solution.py:25
  151.4 12.2 %collective-permute-start.3 = (bf16[48,4224]{1,0:T(8,128)(2,1)S(1)}, bf16[48,4224]{1,0:T(8,128)(2,1)S(1)}, u32[]{:S(2)}, u32[]{:S(2)}) collective-permute-start(bf16[48,4224]{1,0:T(8,128)(2,1)S(1)} %get-tuple-element.35), channel_id=1, source_target_pairs={{0,192},{64,0},{128,64},{192,128},{1,193},{65,1},{129,65},{193,129... | collective-permute-start | bytes 1216520 | tf_op jit(solution)/shard_map/ppermute | solution.py:25
  155.0 14.5 %collective-permute-start.1 = (bf16[48,4224]{1,0:T(8,128)(2,1)S(1)}, bf16[48,4224]{1,0:T(8,128)(2,1)S(1)}, u32[]{:S(2)}, u32[]{:S(2)}) collective-permute-start(bf16[48,4224]{1,0:T(8,128)(2,1)S(1)} %get-tuple-element.35), channel_id=1, source_target_pairs={{0,64},{64,128},{128,192},{192,0},{1,65},{65,129},{129,193},{193,1... | collective-permute-start | bytes 1216520 | tf_op jit(solution)/shard_map/ppermute | solution.py:25
  157.0 13.6 %collective-permute-start.2 = (bf16[48,4224]{1,0:T(8,128)(2,1)S(1)}, bf16[48,4224]{1,0:T(8,128)(2,1)S(1)}, u32[]{:S(2)}, u32[]{:S(2)}) collective-permute-start(bf16[48,4224]{1,0:T(8,128)(2,1)S(1)} %get-tuple-element.36), channel_id=1, source_target_pairs={{0,192},{64,0},{128,64},{192,128},{1,193},{65,1},{129,65},{193,129... | collective-permute-start | bytes 1216520 | tf_op jit(solution)/shard_map/ppermute | solution.py:25
  161.6 18.4 %copy-start.2 = (bf16[48,4224]{1,0:T(8,128)(2,1)}, bf16[48,4224]{1,0:T(8,128)(2,1)S(1)}, u32[]{:S(2)}) copy-start(bf16[48,4224]{1,0:T(8,128)(2,1)S(1)} %collective-permute-done.refs_1_) | copy-start | bytes 1216516
  161.6 16.6 %collective-permute-start.4 = (bf16[48,4224]{1,0:T(8,128)(2,1)S(1)}, bf16[48,4224]{1,0:T(8,128)(2,1)S(1)}, u32[]{:S(2)}, u32[]{:S(2)}) collective-permute-start(bf16[48,4224]{1,0:T(8,128)(2,1)S(1)} %collective-permute-done.refs_1_), channel_id=1, source_target_pairs={{0,64},{64,128},{128,192},{192,0},{1,65},{65,129},{129,193},{193,1... | collective-permute-start | bytes 1216520 | tf_op jit(solution)/shard_map/ppermute | solution.py:25
  163.6 16.5 %copy-start.3 = (bf16[48,4224]{1,0:T(8,128)(2,1)}, bf16[48,4224]{1,0:T(8,128)(2,1)S(1)}, u32[]{:S(2)}) copy-start(bf16[48,4224]{1,0:T(8,128)(2,1)S(1)} %collective-permute-done.3.refs_4_) | copy-start | bytes 1216516
  163.6 15.7 %collective-permute-start.5 = (bf16[48,4224]{1,0:T(8,128)(2,1)S(1)}, bf16[48,4224]{1,0:T(8,128)(2,1)S(1)}, u32[]{:S(2)}, u32[]{:S(2)}) collective-permute-start(bf16[48,4224]{1,0:T(8,128)(2,1)S(1)} %collective-permute-done.3.refs_4_), channel_id=1, source_target_pairs={{0,192},{64,0},{128,64},{192,128},{1,193},{65,1},{129,65},{193,129... | collective-permute-start | bytes 1216520 | tf_op jit(solution)/shard_map/ppermute | solution.py:25
  169.5 9.7 %copy-start.4 = (bf16[48,4224]{1,0:T(8,128)(2,1)}, bf16[48,4224]{1,0:T(8,128)(2,1)S(1)}, u32[]{:S(2)}) copy-start(bf16[48,4224]{1,0:T(8,128)(2,1)S(1)} %collective-permute-done.1.refs_2_) | copy-start | bytes 1216516
  170.6 8.7 %copy-start.5 = (bf16[48,4224]{1,0:T(8,128)(2,1)}, bf16[48,4224]{1,0:T(8,128)(2,1)S(1)}, u32[]{:S(2)}) copy-start(bf16[48,4224]{1,0:T(8,128)(2,1)S(1)} %collective-permute-done.2.refs_3_) | copy-start | bytes 1216516
  178.2 1.0 copy-start.6
  179.3 0.8 copy-start.7
  185.1 7.2 %copy-start.11 = (f32[208,384]{1,0:T(8,128)S(1)}, f32[208,384]{1,0:T(8,128)}, u32[]{:S(2)}) copy-start(f32[208,384]{1,0:T(8,128)} %get-tuple-element.25) | copy-start | bytes 958468
  185.1 7.2 %collective-permute-start.10 = (f32[208,384]{1,0:T(8,128)}, f32[208,384]{1,0:T(8,128)S(1)}, u32[]{:S(2)}, u32[]{:S(2)}) collective-permute-start(f32[208,384]{1,0:T(8,128)} %get-tuple-element.26), channel_id=1, source_target_pairs={{0,1},{1,0},{2,3},{3,2},{4,5},{5,4},{6,7},{7,6},{8,9},{9,8},{10,11... | collective-permute-start | bytes 958472 | tf_op jit(solution)/shard_map/ppermute | solution.py:25
  237.3 12.7 %collective-permute-start.11 = (bf16[384,512]{1,0:T(8,128)(2,1)S(1)}, bf16[384,512]{1,0:T(8,128)(2,1)S(1)}, u32[]{:S(2)}, u32[]{:S(2)}) collective-permute-start(bf16[384,512]{1,0:T(8,128)(2,1)S(1)} %pad_maximum_fusion), channel_id=1, source_target_pairs={{0,1},{1,0},{2,3},{3,2},{4,5},{5,4},{6,7},{7,6},{8,9},{9,8},{10,11... | collective-permute-start | bytes 1179656 | tf_op jit(solution)/shard_map/ppermute | solution.py:25

commit v12 on v11

--- a/solution.py
+++ b/solution.py
@@ -190,42 +190,6 @@
     )
 
 
-def values_kernel(*refs):
-    *chunk_refs, own_rows_ref, other_rows_ref, own_ref, other_ref = refs
-    step = pl.program_id(0)
-    columns = own_rows_ref.shape[0]
-    chunks = jnp.concatenate([ref[...] for ref in chunk_refs], 0)
-    rows = jnp.concatenate([own_rows_ref[...], other_rows_ref[...]], 0)
-    term = lax.dot_general(rows, chunks, (((1,), (1,)), ((), ())), preferred_element_type=F32)
-
-    @pl.when(step == 0)
-    def _():
-        own_ref[...] = term[:columns]
-        other_ref[...] = term[columns:]
-
-    @pl.when(step > 0)
-    def _():
-        own_ref[...] += term[:columns]
-        other_ref[...] += term[columns:]
-
-
-def values(chunks, own_rows, other_rows, steps=2):
-    columns, half = own_rows.shape
-    count = sum(chunk.shape[0] for chunk in chunks)
-    depth = half // steps
-    out = jax.ShapeDtypeStruct((columns, count), F32)
-    rows = pl.BlockSpec((columns, depth), lambda i: (0, i))
-    out_spec = pl.BlockSpec(out.shape, lambda i: (0, 0))
-    return pl.pallas_call(
-        values_kernel,
-        grid=(steps,),
-        in_specs=[pl.BlockSpec((chunk.shape[0], depth), lambda i: (0, i)) for chunk in chunks] + [rows, rows],
-        out_specs=[out_spec, out_spec],
-        out_shape=[out, out],
-        name="values",
-    )(*chunks, own_rows, other_rows)
-
-
 def placed_hidden(own_value, other_value, place):
     value = own_value + other_value
     gate_value, up_value = jnp.split(value, 2, axis=0)
@@ -261,7 +225,12 @@
 
     group = exchanged(group, "zi")
 
-    own_value, other_value = values(chunks, own_rows, other_rows)
+    tokens_all = jnp.concatenate([chunk[:, :half] for chunk in chunks], 0)
+
+    def values(rows):
+        return lax.dot_general(rows, tokens_all, (((1,), (1,)), ((), ())), preferred_element_type=F32)
+
+    other_value, own_value = values(other_rows), values(own_rows)
     other_value = shifted(other_value, "gy", 1)
     place = placement(chunks, half, x_at, own_tokens)
     placed = placed_hidden(own_value, other_value, place)

time: 304 us -> 311 us (1.023)
  waiting for transfers between devices: 27.7 us -> 33.5 us
  matrix products: 2.22 us -> 7.83 us
  Pallas kernels: 17.4 us -> 12.3 us
    dot_general x0 -> x2, matrix products: none -> 6.57 us  [values(): lax.dot_general(rows, tokens_all, (((1,), (1,)), ((), ())), preferred_ele...]
    ppermute x12, waiting for transfers between devices: 26.9 us -> 32.8 us  [shifted(): lax.ppermute(value, axis, [(i, (i + by) % count) for i in range(count)])]
    pallas_call x1 -> x0, Pallas kernels: 5.1 us -> none  [values(): pl.pallas_call(values_kernel, grid=(steps,), in_specs=[pl.BlockSpec((chun...]
  transfers between devices with their start and end apart: 14 -> 14, of which waited for: 9 -> 7; matrix products, arithmetic and copies ran while one was open for 0% -> 2% of each run, Pallas kernels for 5% -> 3%
where the time goes in v12:
time: 311 us; the launch traced here: 310 us
  blocking collectives  147 us (47%)
  starting transfers between devices  104 us (33%)
  waiting for transfers between devices  33.5 us (11%)
  Pallas kernels  12.3 us (4%)
  matrix products  7.83 us (3%)
  local copies, waits for them, and re-layouts  5.32 us (2%)
    ppermute x12, starting transfers between devices, shifted(): lax.ppermute(value, axis, [(i, (i + by) % count) for i in range(count)])  89 us
    all_gather x1, blocking collectives, block(): column = lax.all_gather(strided, 'zi', axis=0, tiled=True)  53.6 us
    all_to_all x2, blocking collectives, exchanged(): return lax.all_to_all(blocks, axes, split_axis=0, concat_axis=0, tiled=True)  51.7 us
    all_gather x1, blocking collectives, block(): gathered = lax.all_gather(placed, 'zo', axis=0, tiled=True)  41.6 us
    ppermute x12, waiting for transfers between devices, shifted(): lax.ppermute(value, axis, [(i, (i + by) % count) for i in range(count)])  32.8 us
    all_to_all x2, starting transfers between devices, exchanged(): return lax.all_to_all(blocks, axes, split_axis=0, concat_axis=0, tiled=True)  14.8 us
    dot_general x2, matrix products, values(): lax.dot_general(rows, tokens_all, (((1,), (1,)), ((), ())), preferred_ele...  6.57 us
  transfers between devices with their start and end apart: 14, of which 7 were waited for; matrix products, arithmetic and copies ran while one was open for 2% of the time, Pallas kernels for 3%

profile of v12, /device:TPU:33, one launch (start us, length us, event | category | flops | bytes accessed | tf_op | source)
XLA Modules:
  0.0 310.3 jit_solution(2034352718546702055)
XLA Ops:
  0.0 2.9 split_rows.1
  2.9 43.4 %collective-permute-start.6 = (bf16[208,4096]{1,0:T(8,128)(2,1)}, bf16[208,4096]{1,0:T(8,128)(2,1)}, u32[]{:S(2)}, u32[]{:S(2)}) collective-permute-start(bf16[208,4096]{1,0:T(8,128)(2,1)} %bitcast.32), channel_id=1, source_target_pairs={{0,1},{1,0},{2,3},{3,2},{4,5},{5,4},{6,7},{7,6},{8,9},{9,8},{10,11... | collective-permute-start | bytes 5111816 | tf_op jit(solution)/shard_map/ppermute | solution.py:25
  46.3 1.5 token_copies.1
  47.8 3.6 %all-to-all-start = ((bf16[8,3,4224]{2,1,0:T(4,128)(2,1)}), bf16[8,3,4224]{2,1,0:T(4,128)(2,1)S(1)}, u32[]{:S(2)}, u32[]{:S(2)}) async-start(bf16[8,3,4224]{2,1,0:T(4,128)(2,1)} %token_copies.1), calls=%async_computation | async-start | bytes 540672 | tf_op jit(solution)/shard_map/all_to_all | solution.py:29
  51.5 2.3 cut_by_x.1
  53.8 2.8 collective-permute-start.7
  56.6 3.7 %collective-permute-start.8 = (bf16[64,3328]{1,0:T(8,128)(2,1)}, bf16[64,3328]{1,0:T(8,128)(2,1)S(1)}, u32[]{:S(2)}, u32[]{:S(2)}) collective-permute-start(bf16[64,3328]{1,0:T(8,128)(2,1)} %get-tuple-element.20), channel_id=1, source_target_pairs={{0,192},{64,0},{128,64},{192,128},{1,193},{65,1},{129,65},{193,129... | collective-permute-start | bytes 1277960 | tf_op jit(solution)/shard_map/ppermute | solution.py:25
  60.3 3.3 %collective-permute-start.9 = (bf16[64,3328]{1,0:T(8,128)(2,1)}, bf16[64,3328]{1,0:T(8,128)(2,1)S(1)}, u32[]{:S(2)}, u32[]{:S(2)}) collective-permute-start(bf16[64,3328]{1,0:T(8,128)(2,1)} %get-tuple-element.21), channel_id=1, source_target_pairs={{0,128},{64,192},{128,0},{192,64},{1,129},{65,193},{129,1},{193,65... | collective-permute-start | bytes 1277960 | tf_op jit(solution)/shard_map/ppermute | solution.py:25
  63.6 4.9 %collective-permute-done.7.refs_1_ = bf16[64,3328]{1,0:T(8,128)(2,1)S(1)} collective-permute-done((bf16[64,3328]{1,0:T(8,128)(2,1)}, bf16[64,3328]{1,0:T(8,128)(2,1)S(1)}, u32[]{:S(2)}, u32[]{:S(2)}) %collective-permute-start.7) | collective-permute-done | bytes 426016 | tf_op jit(solution)/shard_map/ppermute | solution.py:25
  68.5 1.4 collective-permute-done.8.refs_2_
  69.9 8.3 %collective-permute-done.9.refs_3_ = bf16[64,3328]{1,0:T(8,128)(2,1)S(1)} collective-permute-done((bf16[64,3328]{1,0:T(8,128)(2,1)}, bf16[64,3328]{1,0:T(8,128)(2,1)S(1)}, u32[]{:S(2)}, u32[]{:S(2)}) %collective-permute-start.9) | collective-permute-done | bytes 426016 | tf_op jit(solution)/shard_map/ppermute | solution.py:25
  78.2 0.0 collective-permute-done.6
  78.2 0.8 copy-done.11
  79.0 3.6 %cut_by_zi.1 = bf16[4,4,64,832]{3,2,1,0:T(8,128)(2,1)} custom-call(s32[1]{0:T(128)} %bitcast.7.x_ref, s32[1]{0:T(128)} %bitcast.gy_ref, bf16[64,3328]{1,0:T(8,128)(2,1)} %get-tuple-element.23.refs_0_, bf16[64,3328]{1,0:T(8,128)(2,1)} %copy-done.9, bf16[64,3328]{1,0:T(8,128)(2,1)} %copy-done.10, bf16[64,3328]{1,0:T(8,128)(2,1)} %copy-done.11), custom_call_target="tpu_custom_call" | custom-call | tf_op jit(solution)/shard_map/cut_by_zi/pallas_call | solution.py:143
  82.7 0.7 all-to-all-done
  83.4 11.2 %all-to-all-start.1 = ((bf16[4,4,64,832]{3,2,1,0:T(8,128)(2,1)}), bf16[4,4,64,832]{3,2,1,0:T(8,128)(2,1)S(1)}, u32[]{:S(2)}, u32[]{:S(2)}) async-start(bf16[4,4,64,832]{3,2,1,0:T(8,128)(2,1)} %cut_by_zi.1), calls=%async_computation.1 | async-start | bytes 3670016 | tf_op jit(solution)/shard_map/all_to_all | solution.py:29
  94.6 0.2 reshape.32
  94.8 53.6 %all_gather.6.refs_0_ = bf16[96,4224]{1,0:T(8,128)(2,1)S(1)} all-gather(bf16[24,4224]{1,0:T(8,128)(2,1)S(1)} %reshape.32), channel_id=1, replica_groups=mesh['rep'=2,'x'=4,'zo'=8,'zi'=4,'gy'=2] {'zi'}, dimensions={0}, use_global_device_ids=true | all-gather | bytes 1013760 | tf_op jit(solution)/shard_map/all_gather | solution.py:215
  148.4 0.1 fusion.6
  148.5 4.4 %collective-permute-start.3 = (bf16[48,4224]{1,0:T(8,128)(2,1)S(1)}, bf16[48,4224]{1,0:T(8,128)(2,1)S(1)}, u32[]{:S(2)}, u32[]{:S(2)}) collective-permute-start(bf16[48,4224]{1,0:T(8,128)(2,1)S(1)} %get-tuple-element.31), channel_id=1, source_target_pairs={{0,192},{64,0},{128,64},{192,128},{1,193},{65,1},{129,65},{193,129... | collective-permute-start | bytes 1216520 | tf_op jit(solution)/shard_map/ppermute | solution.py:25
  152.9 2.0 collective-permute-start.1
  154.9 4.6 %collective-permute-start.2 = (bf16[48,4224]{1,0:T(8,128)(2,1)S(1)}, bf16[48,4224]{1,0:T(8,128)(2,1)S(1)}, u32[]{:S(2)}, u32[]{:S(2)}) collective-permute-start(bf16[48,4224]{1,0:T(8,128)(2,1)S(1)} %get-tuple-element.32), channel_id=1, source_target_pairs={{0,192},{64,0},{128,64},{192,128},{1,193},{65,1},{129,65},{193,129... | collective-permute-start | bytes 1216520 | tf_op jit(solution)/shard_map/ppermute | solution.py:25
  159.5 2.0 collective-permute-start
  161.4 0.1 slice_dynamic-update-slice_fusion
  161.5 4.6 %collective-permute-start.5 = (bf16[48,4224]{1,0:T(8,128)(2,1)S(1)}, bf16[48,4224]{1,0:T(8,128)(2,1)S(1)}, u32[]{:S(2)}, u32[]{:S(2)}) collective-permute-start(bf16[48,4224]{1,0:T(8,128)(2,1)S(1)} %collective-permute-done.3.refs_4_), channel_id=1, source_target_pairs={{0,192},{64,0},{128,64},{192,128},{1,193},{65,1},{129,65},{193,129... | collective-permute-start | bytes 1216520 | tf_op jit(solution)/shard_map/ppermute | solution.py:25
  166.2 7.7 %collective-permute-done.refs_1_ = bf16[48,4224]{1,0:T(8,128)(2,1)S(1)} collective-permute-done((bf16[48,4224]{1,0:T(8,128)(2,1)S(1)}, bf16[48,4224]{1,0:T(8,128)(2,1)S(1)}, u32[]{:S(2)}, u32[]{:S(2)}) %collective-permute-start) | collective-permute-done | bytes 405536 | tf_op jit(solution)/shard_map/ppermute | solution.py:25
  173.8 1.9 collective-permute-start.4
  176.0 9.2 %collective-permute-done.4.refs_5_ = bf16[48,4224]{1,0:T(8,128)(2,1)S(1)} collective-permute-done((bf16[48,4224]{1,0:T(8,128)(2,1)S(1)}, bf16[48,4224]{1,0:T(8,128)(2,1)S(1)}, u32[]{:S(2)}, u32[]{:S(2)}) %collective-permute-start.4) | collective-permute-done | bytes 405536 | tf_op jit(solution)/shard_map/ppermute | solution.py:25
  185.3 0.7 copy-done.8
  185.9 0.7 copy-done.7
  186.7 1.6 copy-done.1
  188.3 3.4 %fusion.9 = f32[208,384]{1,0:T(8,128)} fusion(bf16[208,4096]{1,0:T(8,128)(2,1)} %collective-permute-done.6, bf16[384,4096]{1,0:T(8,128)(2,1)S(1)} %slice_dynamic-update-slice_fusion.1), kind=kOutput, calls=%fused_computation.20 | convolution fusion | flops 654311424 | bytes 5169152 | tf_op jit(solution)/shard_map/dot_general | solution.py:231
  191.7 5.6 %collective-permute-start.10 = (f32[208,384]{1,0:T(8,128)}, f32[208,384]{1,0:T(8,128)}, u32[]{:S(2)}, u32[]{:S(2)}) collective-permute-start(f32[208,384]{1,0:T(8,128)} %fusion.9), channel_id=1, source_target_pairs={{0,1},{1,0},{2,3},{3,2},{4,5},{5,4},{6,7},{7,6},{8,9},{9,8},{10,11... | collective-permute-start | bytes 958472 | tf_op jit(solution)/shard_map/ppermute | solution.py:25
  197.4 1.9 placement.1
  199.3 3.2 %convolution_add_fusion = f32[208,384]{1,0:T(8,128)S(1)} fusion(f32[208,384]{1,0:T(8,128)} %collective-permute-done.10, bf16[208,4096]{1,0:T(8,128)(2,1)S(1)} %bitcast.26, bf16[384,4096]{1,0:T(8,128)(2,1)} %copy-done.1), kind=kOutput, calls=%fused_computation | convolution fusion | flops 654391296 | bytes 5488640 | tf_op jit(solution)/shard_map/dot_general | solution.py:231
  202.5 0.2 convolution_convert_fusion
  202.8 41.6 %all_gather.7 = bf16[832,384]{1,0:T(8,128)(2,1)S(1)} all-gather(bf16[104,384]{1,0:T(8,128)(2,1)S(1)} %convolution_convert_fusion), channel_id=1, replica_groups=mesh['rep'=2,'x'=4,'zo'=8,'zi'=4,'gy'=2] {'zo'}, dimensions={0}, use_global_device_ids=true | all-gather | bytes 718848 | tf_op jit(solution)/shard_map/all_gather | solution.py:238
  244.3 1.0 fusion.8
  245.4 0.1 fusion.7
  245.5 10.7 %collective-permute-start.11 = (bf16[384,512]{1,0:T(8,128)(2,1)S(1)}, bf16[384,512]{1,0:T(8,128)(2,1)S(1)}, u32[]{:S(2)}, u32[]{:S(2)}) collective-permute-start(bf16[384,512]{1,0:T(8,128)(2,1)S(1)} %pad_maximum_fusion), channel_id=1, source_target_pairs={{0,1},{1,0},{2,3},{3,2},{4,5},{5,4},{6,7},{7,6},{8,9},{9,8},{10,11... | collective-permute-start | bytes 1179656 | tf_op jit(solution)/shard_map/ppermute | solution.py:25
  256.2 0.1 fusion.5
  256.3 1.3 collective-permute-done.11
  257.6 0.1 fusion
  257.6 18.9 %all_to_all.20 = bf16[16,24,512]{2,1,0:T(8,128)(2,1)S(1)} all-to-all(bf16[16,24,512]{2,1,0:T(8,128)(2,1)S(1)} %bitcast.30), channel_id=1, replica_groups=mesh['rep'=2,'x'=4,'zo'=8,'zi'=4,'gy'=2] {'x','zi'}, dimensions={0} | all-to-all | bytes 786432 | tf_op jit(solution)/shard_map/all_to_all | solution.py:29
  276.6 0.1 reduce_sum.12
  276.7 32.8 %all_to_all.21 = bf16[8,3,512]{2,1,0:T(4,128)(2,1)S(1)} all-to-all(bf16[8,3,512]{2,1,0:T(4,128)(2,1)S(1)} %reshape.37), channel_id=1, replica_groups=mesh['rep'=2,'x'=4,'zo'=8,'zi'=4,'gy'=2] {'zo'}, dimensions={0} | all-to-all | bytes 49152 | tf_op jit(solution)/shard_map/all_to_all | solution.py:29
  309.4 0.1 reshape.38
  309.6 0.7 reshape.39
  (38 shorter events, 0.3 us)
Async XLA Ops:
  2.9 75.3 %collective-permute-start.6 = (bf16[208,4096]{1,0:T(8,128)(2,1)}, bf16[208,4096]{1,0:T(8,128)(2,1)}, u32[]{:S(2)}, u32[]{:S(2)}) collective-permute-start(bf16[208,4096]{1,0:T(8,128)(2,1)} %bitcast.32), channel_id=1, source_target_pairs={{0,1},{1,0},{2,3},{3,2},{4,5},{5,4},{6,7},{7,6},{8,9},{9,8},{10,11... | collective-permute-start | bytes 5111816 | tf_op jit(solution)/shard_map/ppermute | solution.py:25
  47.8 35.5 %all-to-all-start = ((bf16[8,3,4224]{2,1,0:T(4,128)(2,1)}), bf16[8,3,4224]{2,1,0:T(4,128)(2,1)S(1)}, u32[]{:S(2)}, u32[]{:S(2)}) async-start(bf16[8,3,4224]{2,1,0:T(4,128)(2,1)} %token_copies.1), calls=%async_computation | async-start | bytes 540672 | tf_op jit(solution)/shard_map/all_to_all | solution.py:29
  53.8 14.7 %collective-permute-start.7 = (bf16[64,3328]{1,0:T(8,128)(2,1)}, bf16[64,3328]{1,0:T(8,128)(2,1)S(1)}, u32[]{:S(2)}, u32[]{:S(2)}) collective-permute-start(bf16[64,3328]{1,0:T(8,128)(2,1)} %get-tuple-element.19), channel_id=1, source_target_pairs={{0,64},{64,128},{128,192},{192,0},{1,65},{65,129},{129,193},{193,1... | collective-permute-start | bytes 1277960 | tf_op jit(solution)/shard_map/ppermute | solution.py:25
  56.6 13.3 %collective-permute-start.8 = (bf16[64,3328]{1,0:T(8,128)(2,1)}, bf16[64,3328]{1,0:T(8,128)(2,1)S(1)}, u32[]{:S(2)}, u32[]{:S(2)}) collective-permute-start(bf16[64,3328]{1,0:T(8,128)(2,1)} %get-tuple-element.20), channel_id=1, source_target_pairs={{0,192},{64,0},{128,64},{192,128},{1,193},{65,1},{129,65},{193,129... | collective-permute-start | bytes 1277960 | tf_op jit(solution)/shard_map/ppermute | solution.py:25
  60.3 17.9 %collective-permute-start.9 = (bf16[64,3328]{1,0:T(8,128)(2,1)}, bf16[64,3328]{1,0:T(8,128)(2,1)S(1)}, u32[]{:S(2)}, u32[]{:S(2)}) collective-permute-start(bf16[64,3328]{1,0:T(8,128)(2,1)} %get-tuple-element.21), channel_id=1, source_target_pairs={{0,128},{64,192},{128,0},{192,64},{1,129},{65,193},{129,1},{193,65... | collective-permute-start | bytes 1277960 | tf_op jit(solution)/shard_map/ppermute | solution.py:25
  68.5 9.8 %copy-start.9 = (bf16[64,3328]{1,0:T(8,128)(2,1)}, bf16[64,3328]{1,0:T(8,128)(2,1)S(1)}, u32[]{:S(2)}) copy-start(bf16[64,3328]{1,0:T(8,128)(2,1)S(1)} %collective-permute-done.7.refs_1_) | copy-start | bytes 1277956
  69.9 8.3 %copy-start.10 = (bf16[64,3328]{1,0:T(8,128)(2,1)}, bf16[64,3328]{1,0:T(8,128)(2,1)S(1)}, u32[]{:S(2)}) copy-start(bf16[64,3328]{1,0:T(8,128)(2,1)S(1)} %collective-permute-done.8.refs_2_) | copy-start | bytes 1277956
  78.2 0.8 copy-start.11
  83.4 160.9 %all-to-all-start.1 = ((bf16[4,4,64,832]{3,2,1,0:T(8,128)(2,1)}), bf16[4,4,64,832]{3,2,1,0:T(8,128)(2,1)S(1)}, u32[]{:S(2)}, u32[]{:S(2)}) async-start(bf16[4,4,64,832]{3,2,1,0:T(8,128)(2,1)} %cut_by_zi.1), calls=%async_computation.1 | async-start | bytes 3670016 | tf_op jit(solution)/shard_map/all_to_all | solution.py:29
  148.4 27.6 %copy-start = (bf16[96,4224]{1,0:T(8,128)(2,1)}, bf16[96,4224]{1,0:T(8,128)(2,1)S(1)}, u32[]{:S(2)}) copy-start(bf16[96,4224]{1,0:T(8,128)(2,1)S(1)} %all_gather.6.refs_0_) | copy-start | bytes 2433028
  148.5 13.1 %collective-permute-start.3 = (bf16[48,4224]{1,0:T(8,128)(2,1)S(1)}, bf16[48,4224]{1,0:T(8,128)(2,1)S(1)}, u32[]{:S(2)}, u32[]{:S(2)}) collective-permute-start(bf16[48,4224]{1,0:T(8,128)(2,1)S(1)} %get-tuple-element.31), channel_id=1, source_target_pairs={{0,192},{64,0},{128,64},{192,128},{1,193},{65,1},{129,65},{193,129... | collective-permute-start | bytes 1216520 | tf_op jit(solution)/shard_map/ppermute | solution.py:25
  152.9 22.9 %collective-permute-start.1 = (bf16[48,4224]{1,0:T(8,128)(2,1)S(1)}, bf16[48,4224]{1,0:T(8,128)(2,1)S(1)}, u32[]{:S(2)}, u32[]{:S(2)}) collective-permute-start(bf16[48,4224]{1,0:T(8,128)(2,1)S(1)} %get-tuple-element.31), channel_id=1, source_target_pairs={{0,64},{64,128},{128,192},{192,0},{1,65},{65,129},{129,193},{193,1... | collective-permute-start | bytes 1216520 | tf_op jit(solution)/shard_map/ppermute | solution.py:25
  154.9 21.0 %collective-permute-start.2 = (bf16[48,4224]{1,0:T(8,128)(2,1)S(1)}, bf16[48,4224]{1,0:T(8,128)(2,1)S(1)}, u32[]{:S(2)}, u32[]{:S(2)}) collective-permute-start(bf16[48,4224]{1,0:T(8,128)(2,1)S(1)} %get-tuple-element.32), channel_id=1, source_target_pairs={{0,192},{64,0},{128,64},{192,128},{1,193},{65,1},{129,65},{193,129... | collective-permute-start | bytes 1216520 | tf_op jit(solution)/shard_map/ppermute | solution.py:25
  159.5 14.3 %collective-permute-start = (bf16[48,4224]{1,0:T(8,128)(2,1)S(1)}, bf16[48,4224]{1,0:T(8,128)(2,1)S(1)}, u32[]{:S(2)}, u32[]{:S(2)}) collective-permute-start(bf16[48,4224]{1,0:T(8,128)(2,1)S(1)} %get-tuple-element.32), channel_id=1, source_target_pairs={{0,64},{64,128},{128,192},{192,0},{1,65},{65,129},{129,193},{193,1... | collective-permute-start | bytes 1216520 | tf_op jit(solution)/shard_map/ppermute | solution.py:25
  161.5 23.7 %copy-start.3 = (bf16[48,4224]{1,0:T(8,128)(2,1)}, bf16[48,4224]{1,0:T(8,128)(2,1)S(1)}, u32[]{:S(2)}) copy-start(bf16[48,4224]{1,0:T(8,128)(2,1)S(1)} %collective-permute-done.3.refs_4_) | copy-start | bytes 1216516
  161.5 23.7 %collective-permute-start.5 = (bf16[48,4224]{1,0:T(8,128)(2,1)S(1)}, bf16[48,4224]{1,0:T(8,128)(2,1)S(1)}, u32[]{:S(2)}, u32[]{:S(2)}) collective-permute-start(bf16[48,4224]{1,0:T(8,128)(2,1)S(1)} %collective-permute-done.3.refs_4_), channel_id=1, source_target_pairs={{0,192},{64,0},{128,64},{192,128},{1,193},{65,1},{129,65},{193,129... | collective-permute-start | bytes 1216520 | tf_op jit(solution)/shard_map/ppermute | solution.py:25
  173.8 11.4 %copy-start.6 = (bf16[48,4224]{1,0:T(8,128)(2,1)}, bf16[48,4224]{1,0:T(8,128)(2,1)S(1)}, u32[]{:S(2)}) copy-start(bf16[48,4224]{1,0:T(8,128)(2,1)S(1)} %collective-permute-done.refs_1_) | copy-start | bytes 1216516
  173.8 11.4 %collective-permute-start.4 = (bf16[48,4224]{1,0:T(8,128)(2,1)S(1)}, bf16[48,4224]{1,0:T(8,128)(2,1)S(1)}, u32[]{:S(2)}, u32[]{:S(2)}) collective-permute-start(bf16[48,4224]{1,0:T(8,128)(2,1)S(1)} %collective-permute-done.refs_1_), channel_id=1, source_target_pairs={{0,64},{64,128},{128,192},{192,0},{1,65},{65,129},{129,193},{193,1... | collective-permute-start | bytes 1216520 | tf_op jit(solution)/shard_map/ppermute | solution.py:25
  175.8 9.4 %copy-start.4 = (bf16[48,4224]{1,0:T(8,128)(2,1)}, bf16[48,4224]{1,0:T(8,128)(2,1)S(1)}, u32[]{:S(2)}) copy-start(bf16[48,4224]{1,0:T(8,128)(2,1)S(1)} %collective-permute-done.1.refs_2_) | copy-start | bytes 1216516
  175.9 9.4 %copy-start.5 = (bf16[48,4224]{1,0:T(8,128)(2,1)}, bf16[48,4224]{1,0:T(8,128)(2,1)S(1)}, u32[]{:S(2)}) copy-start(bf16[48,4224]{1,0:T(8,128)(2,1)S(1)} %collective-permute-done.2.refs_3_) | copy-start | bytes 1216516
  185.2 0.7 copy-start.8
  185.9 0.7 copy-start.7
  186.7 1.6 copy-start.1
  191.7 7.6 %copy-start.2 = (bf16[2,104,4096]{2,1,0:T(8,128)(2,1)S(1)}, bf16[2,104,4096]{2,1,0:T(8,128)(2,1)}, u32[]{:S(2)}) copy-start(bf16[2,104,4096]{2,1,0:T(8,128)(2,1)} %get-tuple-element.16) | copy-start | bytes 5111812
  191.7 7.6 %collective-permute-start.10 = (f32[208,384]{1,0:T(8,128)}, f32[208,384]{1,0:T(8,128)}, u32[]{:S(2)}, u32[]{:S(2)}) collective-permute-start(f32[208,384]{1,0:T(8,128)} %fusion.9), channel_id=1, source_target_pairs={{0,1},{1,0},{2,3},{3,2},{4,5},{5,4},{6,7},{7,6},{8,9},{9,8},{10,11... | collective-permute-start | bytes 958472 | tf_op jit(solution)/shard_map/ppermute | solution.py:25
  199.3 3.2 %copy-start.12 = (bf16[384,384]{1,0:T(8,128)(2,1)S(1)}, bf16[384,384]{1,0:T(8,128)(2,1)}, u32[]{:S(2)}) copy-start(bf16[384,384]{1,0:T(8,128)(2,1)} %placement.1) | copy-start | bytes 884740
  245.5 12.1 %collective-permute-start.11 = (bf16[384,512]{1,0:T(8,128)(2,1)S(1)}, bf16[384,512]{1,0:T(8,128)(2,1)S(1)}, u32[]{:S(2)}, u32[]{:S(2)}) collective-permute-start(bf16[384,512]{1,0:T(8,128)(2,1)S(1)} %pad_maximum_fusion), channel_id=1, source_target_pairs={{0,1},{1,0},{2,3},{3,2},{4,5},{5,4},{6,7},{7,6},{8,9},{9,8},{10,11... | collective-permute-start | bytes 1179656 | tf_op jit(solution)/shard_map/ppermute | solution.py:25

commit v13 on v12

--- a/solution.py
+++ b/solution.py
@@ -225,13 +225,11 @@
 
     group = exchanged(group, "zi")
 
+    rows = jnp.concatenate([own_rows, other_rows], 0)
     tokens_all = jnp.concatenate([chunk[:, :half] for chunk in chunks], 0)
-
-    def values(rows):
-        return lax.dot_general(rows, tokens_all, (((1,), (1,)), ((), ())), preferred_element_type=F32)
-
-    other_value, own_value = values(other_rows), values(own_rows)
-    other_value = shifted(other_value, "gy", 1)
+    value = lax.dot_general(rows, tokens_all, (((1,), (1,)), ((), ())), preferred_element_type=F32)
+    own_value, other_value = jnp.split(value, 2, axis=0)
+    other_value = shifted(other_value.astype(BF16), "gy", 1)
     place = placement(chunks, half, x_at, own_tokens)
     placed = placed_hidden(own_value, other_value, place)
 

time: 311 us -> 306 us (0.984)
  blocking collectives: 147 us -> 154 us
  waiting for transfers between devices: 33.5 us -> 28.9 us
    all_to_all x2, blocking collectives: 51.7 us -> 56.7 us  [exchanged(): return lax.all_to_all(blocks, axes, split_axis=0, concat_axis=0, tiled=True)]
    ppermute x12, waiting for transfers between devices: 32.8 us -> 28.2 us  [shifted(): lax.ppermute(value, axis, [(i, (i + by) % count) for i in range(count)])]
    dot_general x2 -> x1, matrix products: 6.57 us -> 3.39 us  [block(): lax.dot_general(rows, tokens_all, (((1,), (1,)), ((), ())), preferred_ele...]
  transfers between devices with their start and end apart: 14 -> 14, of which waited for: 7 -> 8; matrix products, arithmetic and copies ran while one was open for 2% -> 2% of each run, Pallas kernels for 3% -> 3%
where the time goes in v13:
time: 306 us; the launch traced here: 305 us
  blocking collectives  154 us (50%)
  starting transfers between devices  101 us (33%)
  waiting for transfers between devices  28.9 us (9%)
  Pallas kernels  12.3 us (4%)
  matrix products  5.61 us (2%)
    ppermute x12, starting transfers between devices, shifted(): lax.ppermute(value, axis, [(i, (i + by) % count) for i in range(count)])  86.2 us
    all_to_all x2, blocking collectives, exchanged(): return lax.all_to_all(blocks, axes, split_axis=0, concat_axis=0, tiled=True)  56.7 us
    all_gather x1, blocking collectives, block(): column = lax.all_gather(strided, 'zi', axis=0, tiled=True)  53.6 us
    all_gather x1, blocking collectives, block(): gathered = lax.all_gather(placed, 'zo', axis=0, tiled=True)  43.1 us
    ppermute x12, waiting for transfers between devices, shifted(): lax.ppermute(value, axis, [(i, (i + by) % count) for i in range(count)])  28.2 us
    all_to_all x2, starting transfers between devices, exchanged(): return lax.all_to_all(blocks, axes, split_axis=0, concat_axis=0, tiled=True)  14.8 us
  transfers between devices with their start and end apart: 14, of which 8 were waited for; matrix products, arithmetic and copies ran while one was open for 2% of the time, Pallas kernels for 3%

profile of v13, /device:TPU:33, one launch (start us, length us, event | category | flops | bytes accessed | tf_op | source)
XLA Modules:
  0.0 305.0 jit_solution(16051334423827806347)
XLA Ops:
  0.0 2.9 split_rows.1
  2.9 43.4 %collective-permute-start = (bf16[208,4096]{1,0:T(8,128)(2,1)}, bf16[208,4096]{1,0:T(8,128)(2,1)}, u32[]{:S(2)}, u32[]{:S(2)}) collective-permute-start(bf16[208,4096]{1,0:T(8,128)(2,1)} %bitcast.29), channel_id=1, source_target_pairs={{0,1},{1,0},{2,3},{3,2},{4,5},{5,4},{6,7},{7,6},{8,9},{9,8},{10,11... | collective-permute-start | bytes 5111816 | tf_op jit(solution)/shard_map/ppermute | solution.py:25
  46.3 1.5 token_copies.1
  47.8 3.6 %all-to-all-start = ((bf16[8,3,4224]{2,1,0:T(4,128)(2,1)}), bf16[8,3,4224]{2,1,0:T(4,128)(2,1)S(1)}, u32[]{:S(2)}, u32[]{:S(2)}) async-start(bf16[8,3,4224]{2,1,0:T(4,128)(2,1)} %token_copies.1), calls=%async_computation | async-start | bytes 540672 | tf_op jit(solution)/shard_map/all_to_all | solution.py:29
  51.4 2.3 cut_by_x.1
  53.8 2.8 collective-permute-start.1
  56.6 3.7 %collective-permute-start.2 = (bf16[64,3328]{1,0:T(8,128)(2,1)}, bf16[64,3328]{1,0:T(8,128)(2,1)S(1)}, u32[]{:S(2)}, u32[]{:S(2)}) collective-permute-start(bf16[64,3328]{1,0:T(8,128)(2,1)} %get-tuple-element.20), channel_id=1, source_target_pairs={{0,192},{64,0},{128,64},{192,128},{1,193},{65,1},{129,65},{193,129... | collective-permute-start | bytes 1277960 | tf_op jit(solution)/shard_map/ppermute | solution.py:25
  60.3 3.3 %collective-permute-start.3 = (bf16[64,3328]{1,0:T(8,128)(2,1)}, bf16[64,3328]{1,0:T(8,128)(2,1)S(1)}, u32[]{:S(2)}, u32[]{:S(2)}) collective-permute-start(bf16[64,3328]{1,0:T(8,128)(2,1)} %get-tuple-element.21), channel_id=1, source_target_pairs={{0,128},{64,192},{128,0},{192,64},{1,129},{65,193},{129,1},{193,65... | collective-permute-start | bytes 1277960 | tf_op jit(solution)/shard_map/ppermute | solution.py:25
  63.6 4.9 %collective-permute-done.1.refs_1_ = bf16[64,3328]{1,0:T(8,128)(2,1)S(1)} collective-permute-done((bf16[64,3328]{1,0:T(8,128)(2,1)}, bf16[64,3328]{1,0:T(8,128)(2,1)S(1)}, u32[]{:S(2)}, u32[]{:S(2)}) %collective-permute-start.1) | collective-permute-done | bytes 426016 | tf_op jit(solution)/shard_map/ppermute | solution.py:25
  68.5 1.4 collective-permute-done.2.refs_2_
  69.9 8.3 %collective-permute-done.3.refs_3_ = bf16[64,3328]{1,0:T(8,128)(2,1)S(1)} collective-permute-done((bf16[64,3328]{1,0:T(8,128)(2,1)}, bf16[64,3328]{1,0:T(8,128)(2,1)S(1)}, u32[]{:S(2)}, u32[]{:S(2)}) %collective-permute-start.3) | collective-permute-done | bytes 426016 | tf_op jit(solution)/shard_map/ppermute | solution.py:25
  78.2 0.0 collective-permute-done
  78.2 0.7 copy-done.9
  79.0 3.6 %cut_by_zi.1 = bf16[4,4,64,832]{3,2,1,0:T(8,128)(2,1)} custom-call(s32[1]{0:T(128)} %bitcast.7.x_ref, s32[1]{0:T(128)} %bitcast.gy_ref, bf16[64,3328]{1,0:T(8,128)(2,1)} %get-tuple-element.23.refs_0_, bf16[64,3328]{1,0:T(8,128)(2,1)} %copy-done.7, bf16[64,3328]{1,0:T(8,128)(2,1)} %copy-done.8, bf16[64,3328]{1,0:T(8,128)(2,1)} %copy-done.9), custom_call_target="tpu_custom_call" | custom-call | tf_op jit(solution)/shard_map/cut_by_zi/pallas_call | solution.py:143
  82.6 0.7 all-to-all-done
  83.3 11.2 %all-to-all-start.1 = ((bf16[4,4,64,832]{3,2,1,0:T(8,128)(2,1)}), bf16[4,4,64,832]{3,2,1,0:T(8,128)(2,1)S(1)}, u32[]{:S(2)}, u32[]{:S(2)}) async-start(bf16[4,4,64,832]{3,2,1,0:T(8,128)(2,1)} %cut_by_zi.1), calls=%async_computation.1 | async-start | bytes 3670016 | tf_op jit(solution)/shard_map/all_to_all | solution.py:29
  94.6 0.2 reshape.34
  94.7 53.6 %all_gather.6.refs_0_ = bf16[96,4224]{1,0:T(8,128)(2,1)S(1)} all-gather(bf16[24,4224]{1,0:T(8,128)(2,1)S(1)} %reshape.34), channel_id=1, replica_groups=mesh['rep'=2,'x'=4,'zo'=8,'zi'=4,'gy'=2] {'zi'}, dimensions={0}, use_global_device_ids=true | all-gather | bytes 1013760 | tf_op jit(solution)/shard_map/all_gather | solution.py:215
  148.4 0.1 fusion.11
  148.5 2.9 collective-permute-start.4
  151.4 3.7 %collective-permute-start.6 = (bf16[48,4224]{1,0:T(8,128)(2,1)S(1)}, bf16[48,4224]{1,0:T(8,128)(2,1)S(1)}, u32[]{:S(2)}, u32[]{:S(2)}) collective-permute-start(bf16[48,4224]{1,0:T(8,128)(2,1)S(1)} %get-tuple-element.32), channel_id=1, source_target_pairs={{0,192},{64,0},{128,64},{192,128},{1,193},{65,1},{129,65},{193,129... | collective-permute-start | bytes 1216520 | tf_op jit(solution)/shard_map/ppermute | solution.py:25
  155.0 2.1 collective-permute-start.5
  157.1 4.6 %collective-permute-start.7 = (bf16[48,4224]{1,0:T(8,128)(2,1)S(1)}, bf16[48,4224]{1,0:T(8,128)(2,1)S(1)}, u32[]{:S(2)}, u32[]{:S(2)}) collective-permute-start(bf16[48,4224]{1,0:T(8,128)(2,1)S(1)} %get-tuple-element.31), channel_id=1, source_target_pairs={{0,192},{64,0},{128,64},{192,128},{1,193},{65,1},{129,65},{193,129... | collective-permute-start | bytes 1216520 | tf_op jit(solution)/shard_map/ppermute | solution.py:25
  161.7 0.1 slice_dynamic-update-slice_fusion
  161.8 0.0 collective-permute-done.4.refs_1_
  161.8 2.0 collective-permute-start.8
  163.8 6.7 %collective-permute-done.7.refs_4_ = bf16[48,4224]{1,0:T(8,128)(2,1)S(1)} collective-permute-done((bf16[48,4224]{1,0:T(8,128)(2,1)S(1)}, bf16[48,4224]{1,0:T(8,128)(2,1)S(1)}, u32[]{:S(2)}, u32[]{:S(2)}) %collective-permute-start.7) | collective-permute-done | bytes 405536 | tf_op jit(solution)/shard_map/ppermute | solution.py:25
  170.4 5.3 %collective-permute-start.9 = (bf16[48,4224]{1,0:T(8,128)(2,1)S(1)}, bf16[48,4224]{1,0:T(8,128)(2,1)S(1)}, u32[]{:S(2)}, u32[]{:S(2)}) collective-permute-start(bf16[48,4224]{1,0:T(8,128)(2,1)S(1)} %collective-permute-done.7.refs_4_), channel_id=1, source_target_pairs={{0,192},{64,0},{128,64},{192,128},{1,193},{65,1},{129,65},{193,129... | collective-permute-start | bytes 1216520 | tf_op jit(solution)/shard_map/ppermute | solution.py:25
  175.9 0.0 collective-permute-done.6.refs_3_
  176.0 2.2 collective-permute-done.8.refs_5_
  178.2 3.4 %collective-permute-done.9.refs_6_ = bf16[48,4224]{1,0:T(8,128)(2,1)S(1)} collective-permute-done((bf16[48,4224]{1,0:T(8,128)(2,1)S(1)}, bf16[48,4224]{1,0:T(8,128)(2,1)S(1)}, u32[]{:S(2)}, u32[]{:S(2)}) %collective-permute-start.9) | collective-permute-done | bytes 405536 | tf_op jit(solution)/shard_map/ppermute | solution.py:25
  181.7 0.7 copy-done.6
  182.4 3.4 %fusion = f32[416,384]{1,0:T(8,128)S(1)} fusion(bf16[384,4096]{1,0:T(8,128)(2,1)S(1)} %slice_dynamic-update-slice_fusion.1, bf16[208,4096]{1,0:T(8,128)(2,1)} %collective-permute-done, bf16[208,4096]{1,0:T(8,128)(2,1)S(1)} %bitcast.28), kind=kOutput, calls=%fused_computation | convolution fusion | flops 1315438592 | bytes 7192576 | tf_op jit(solution)/shard_map/dot_general | solution.py:230
  185.9 5.6 %collective-permute-start.10 = (bf16[208,384]{1,0:T(8,128)(2,1)S(1)}, bf16[208,384]{1,0:T(8,128)(2,1)S(1)}, u32[]{:S(2)}, u32[]{:S(2)}) collective-permute-start(bf16[208,384]{1,0:T(8,128)(2,1)S(1)} %split.39), channel_id=1, source_target_pairs={{0,1},{1,0},{2,3},{3,2},{4,5},{5,4},{6,7},{7,6},{8,9},{9,8},{10,11... | collective-permute-start | bytes 479240 | tf_op jit(solution)/shard_map/ppermute | solution.py:25
  191.5 2.0 placement.1
  193.5 1.2 convolution_convert_fusion
  194.7 43.1 %all_gather.7 = bf16[832,384]{1,0:T(8,128)(2,1)S(1)} all-gather(bf16[104,384]{1,0:T(8,128)(2,1)S(1)} %convolution_convert_fusion), channel_id=1, replica_groups=mesh['rep'=2,'x'=4,'zo'=8,'zi'=4,'gy'=2] {'zo'}, dimensions={0}, use_global_device_ids=true | all-gather | bytes 718848 | tf_op jit(solution)/shard_map/all_gather | solution.py:236
  237.8 1.0 fusion.13
  238.9 0.1 fusion.12
  239.0 6.9 %collective-permute-start.11 = (bf16[384,512]{1,0:T(8,128)(2,1)S(1)}, bf16[384,512]{1,0:T(8,128)(2,1)S(1)}, u32[]{:S(2)}, u32[]{:S(2)}) collective-permute-start(bf16[384,512]{1,0:T(8,128)(2,1)S(1)} %pad_maximum_fusion), channel_id=1, source_target_pairs={{0,1},{1,0},{2,3},{3,2},{4,5},{5,4},{6,7},{7,6},{8,9},{9,8},{10,11... | collective-permute-start | bytes 1179656 | tf_op jit(solution)/shard_map/ppermute | solution.py:25
  245.9 0.1 fusion.10
  246.0 1.3 collective-permute-done.11
  247.2 0.1 fusion.4
  247.3 23.0 %all_to_all.20 = bf16[16,24,512]{2,1,0:T(8,128)(2,1)S(1)} all-to-all(bf16[16,24,512]{2,1,0:T(8,128)(2,1)S(1)} %bitcast.26), channel_id=1, replica_groups=mesh['rep'=2,'x'=4,'zo'=8,'zi'=4,'gy'=2] {'x','zi'}, dimensions={0} | all-to-all | bytes 786432 | tf_op jit(solution)/shard_map/all_to_all | solution.py:29
  270.3 0.1 reduce_sum.12
  270.4 33.8 %all_to_all.21 = bf16[8,3,512]{2,1,0:T(4,128)(2,1)S(1)} all-to-all(bf16[8,3,512]{2,1,0:T(4,128)(2,1)S(1)} %reshape.37), channel_id=1, replica_groups=mesh['rep'=2,'x'=4,'zo'=8,'zi'=4,'gy'=2] {'zo'}, dimensions={0} | all-to-all | bytes 49152 | tf_op jit(solution)/shard_map/all_to_all | solution.py:29
  304.2 0.1 reshape.38
  304.3 0.7 reshape.39
  (35 shorter events, 0.4 us)
Async XLA Ops:
  2.9 75.3 %collective-permute-start = (bf16[208,4096]{1,0:T(8,128)(2,1)}, bf16[208,4096]{1,0:T(8,128)(2,1)}, u32[]{:S(2)}, u32[]{:S(2)}) collective-permute-start(bf16[208,4096]{1,0:T(8,128)(2,1)} %bitcast.29), channel_id=1, source_target_pairs={{0,1},{1,0},{2,3},{3,2},{4,5},{5,4},{6,7},{7,6},{8,9},{9,8},{10,11... | collective-permute-start | bytes 5111816 | tf_op jit(solution)/shard_map/ppermute | solution.py:25
  47.8 35.5 %all-to-all-start = ((bf16[8,3,4224]{2,1,0:T(4,128)(2,1)}), bf16[8,3,4224]{2,1,0:T(4,128)(2,1)S(1)}, u32[]{:S(2)}, u32[]{:S(2)}) async-start(bf16[8,3,4224]{2,1,0:T(4,128)(2,1)} %token_copies.1), calls=%async_computation | async-start | bytes 540672 | tf_op jit(solution)/shard_map/all_to_all | solution.py:29
  53.8 14.7 %collective-permute-start.1 = (bf16[64,3328]{1,0:T(8,128)(2,1)}, bf16[64,3328]{1,0:T(8,128)(2,1)S(1)}, u32[]{:S(2)}, u32[]{:S(2)}) collective-permute-start(bf16[64,3328]{1,0:T(8,128)(2,1)} %get-tuple-element.19), channel_id=1, source_target_pairs={{0,64},{64,128},{128,192},{192,0},{1,65},{65,129},{129,193},{193,1... | collective-permute-start | bytes 1277960 | tf_op jit(solution)/shard_map/ppermute | solution.py:25
  56.6 13.3 %collective-permute-start.2 = (bf16[64,3328]{1,0:T(8,128)(2,1)}, bf16[64,3328]{1,0:T(8,128)(2,1)S(1)}, u32[]{:S(2)}, u32[]{:S(2)}) collective-permute-start(bf16[64,3328]{1,0:T(8,128)(2,1)} %get-tuple-element.20), channel_id=1, source_target_pairs={{0,192},{64,0},{128,64},{192,128},{1,193},{65,1},{129,65},{193,129... | collective-permute-start | bytes 1277960 | tf_op jit(solution)/shard_map/ppermute | solution.py:25
  60.3 17.9 %collective-permute-start.3 = (bf16[64,3328]{1,0:T(8,128)(2,1)}, bf16[64,3328]{1,0:T(8,128)(2,1)S(1)}, u32[]{:S(2)}, u32[]{:S(2)}) collective-permute-start(bf16[64,3328]{1,0:T(8,128)(2,1)} %get-tuple-element.21), channel_id=1, source_target_pairs={{0,128},{64,192},{128,0},{192,64},{1,129},{65,193},{129,1},{193,65... | collective-permute-start | bytes 1277960 | tf_op jit(solution)/shard_map/ppermute | solution.py:25
  68.5 9.8 %copy-start.7 = (bf16[64,3328]{1,0:T(8,128)(2,1)}, bf16[64,3328]{1,0:T(8,128)(2,1)S(1)}, u32[]{:S(2)}) copy-start(bf16[64,3328]{1,0:T(8,128)(2,1)S(1)} %collective-permute-done.1.refs_1_) | copy-start | bytes 1277956
  69.9 8.3 %copy-start.8 = (bf16[64,3328]{1,0:T(8,128)(2,1)}, bf16[64,3328]{1,0:T(8,128)(2,1)S(1)}, u32[]{:S(2)}) copy-start(bf16[64,3328]{1,0:T(8,128)(2,1)S(1)} %collective-permute-done.2.refs_2_) | copy-start | bytes 1277956
  78.2 0.8 copy-start.9
  83.3 154.5 %all-to-all-start.1 = ((bf16[4,4,64,832]{3,2,1,0:T(8,128)(2,1)}), bf16[4,4,64,832]{3,2,1,0:T(8,128)(2,1)S(1)}, u32[]{:S(2)}, u32[]{:S(2)}) async-start(bf16[4,4,64,832]{3,2,1,0:T(8,128)(2,1)} %cut_by_zi.1), calls=%async_computation.1 | async-start | bytes 3670016 | tf_op jit(solution)/shard_map/all_to_all | solution.py:29
  148.4 27.6 %copy-start = (bf16[96,4224]{1,0:T(8,128)(2,1)}, bf16[96,4224]{1,0:T(8,128)(2,1)S(1)}, u32[]{:S(2)}) copy-start(bf16[96,4224]{1,0:T(8,128)(2,1)S(1)} %all_gather.6.refs_0_) | copy-start | bytes 2433028
  148.5 13.4 %collective-permute-start.4 = (bf16[48,4224]{1,0:T(8,128)(2,1)S(1)}, bf16[48,4224]{1,0:T(8,128)(2,1)S(1)}, u32[]{:S(2)}, u32[]{:S(2)}) collective-permute-start(bf16[48,4224]{1,0:T(8,128)(2,1)S(1)} %get-tuple-element.32), channel_id=1, source_target_pairs={{0,64},{64,128},{128,192},{192,0},{1,65},{65,129},{129,193},{193,1... | collective-permute-start | bytes 1216520 | tf_op jit(solution)/shard_map/ppermute | solution.py:25
  151.4 24.5 %collective-permute-start.6 = (bf16[48,4224]{1,0:T(8,128)(2,1)S(1)}, bf16[48,4224]{1,0:T(8,128)(2,1)S(1)}, u32[]{:S(2)}, u32[]{:S(2)}) collective-permute-start(bf16[48,4224]{1,0:T(8,128)(2,1)S(1)} %get-tuple-element.32), channel_id=1, source_target_pairs={{0,192},{64,0},{128,64},{192,128},{1,193},{65,1},{129,65},{193,129... | collective-permute-start | bytes 1216520 | tf_op jit(solution)/shard_map/ppermute | solution.py:25
  155.0 27.4 %copy-start.10 = (bf16[2,104,4096]{2,1,0:T(8,128)(2,1)S(1)}, bf16[2,104,4096]{2,1,0:T(8,128)(2,1)}, u32[]{:S(2)}) copy-start(bf16[2,104,4096]{2,1,0:T(8,128)(2,1)} %get-tuple-element.16) | copy-start | bytes 5111812
  155.0 20.8 %collective-permute-start.5 = (bf16[48,4224]{1,0:T(8,128)(2,1)S(1)}, bf16[48,4224]{1,0:T(8,128)(2,1)S(1)}, u32[]{:S(2)}, u32[]{:S(2)}) collective-permute-start(bf16[48,4224]{1,0:T(8,128)(2,1)S(1)} %get-tuple-element.31), channel_id=1, source_target_pairs={{0,64},{64,128},{128,192},{192,0},{1,65},{65,129},{129,193},{193,1... | collective-permute-start | bytes 1216520 | tf_op jit(solution)/shard_map/ppermute | solution.py:25
  157.1 13.3 %collective-permute-start.7 = (bf16[48,4224]{1,0:T(8,128)(2,1)S(1)}, bf16[48,4224]{1,0:T(8,128)(2,1)S(1)}, u32[]{:S(2)}, u32[]{:S(2)}) collective-permute-start(bf16[48,4224]{1,0:T(8,128)(2,1)S(1)} %get-tuple-element.31), channel_id=1, source_target_pairs={{0,192},{64,0},{128,64},{192,128},{1,193},{65,1},{129,65},{193,129... | collective-permute-start | bytes 1216520 | tf_op jit(solution)/shard_map/ppermute | solution.py:25
  161.8 24.0 %copy-start.1 = (bf16[48,4224]{1,0:T(8,128)(2,1)}, bf16[48,4224]{1,0:T(8,128)(2,1)S(1)}, u32[]{:S(2)}) copy-start(bf16[48,4224]{1,0:T(8,128)(2,1)S(1)} %collective-permute-done.4.refs_1_) | copy-start | bytes 1216516
  161.8 16.4 %collective-permute-start.8 = (bf16[48,4224]{1,0:T(8,128)(2,1)S(1)}, bf16[48,4224]{1,0:T(8,128)(2,1)S(1)}, u32[]{:S(2)}, u32[]{:S(2)}) collective-permute-start(bf16[48,4224]{1,0:T(8,128)(2,1)S(1)} %collective-permute-done.4.refs_1_), channel_id=1, source_target_pairs={{0,64},{64,128},{128,192},{192,0},{1,65},{65,129},{129,193},{193,1... | collective-permute-start | bytes 1216520 | tf_op jit(solution)/shard_map/ppermute | solution.py:25
  170.4 15.4 %copy-start.4 = (bf16[48,4224]{1,0:T(8,128)(2,1)}, bf16[48,4224]{1,0:T(8,128)(2,1)S(1)}, u32[]{:S(2)}) copy-start(bf16[48,4224]{1,0:T(8,128)(2,1)S(1)} %collective-permute-done.7.refs_4_) | copy-start | bytes 1216516
  170.4 11.2 %collective-permute-start.9 = (bf16[48,4224]{1,0:T(8,128)(2,1)S(1)}, bf16[48,4224]{1,0:T(8,128)(2,1)S(1)}, u32[]{:S(2)}, u32[]{:S(2)}) collective-permute-start(bf16[48,4224]{1,0:T(8,128)(2,1)S(1)} %collective-permute-done.7.refs_4_), channel_id=1, source_target_pairs={{0,192},{64,0},{128,64},{192,128},{1,193},{65,1},{129,65},{193,129... | collective-permute-start | bytes 1216520 | tf_op jit(solution)/shard_map/ppermute | solution.py:25
  175.8 10.0 %copy-start.3 = (bf16[48,4224]{1,0:T(8,128)(2,1)}, bf16[48,4224]{1,0:T(8,128)(2,1)S(1)}, u32[]{:S(2)}) copy-start(bf16[48,4224]{1,0:T(8,128)(2,1)S(1)} %collective-permute-done.5.refs_2_) | copy-start | bytes 1216516
  175.9 10.0 %copy-start.2 = (bf16[48,4224]{1,0:T(8,128)(2,1)}, bf16[48,4224]{1,0:T(8,128)(2,1)S(1)}, u32[]{:S(2)}) copy-start(bf16[48,4224]{1,0:T(8,128)(2,1)S(1)} %collective-permute-done.6.refs_3_) | copy-start | bytes 1216516
  178.2 3.5 %copy-start.5 = (bf16[48,4224]{1,0:T(8,128)(2,1)}, bf16[48,4224]{1,0:T(8,128)(2,1)S(1)}, u32[]{:S(2)}) copy-start(bf16[48,4224]{1,0:T(8,128)(2,1)S(1)} %collective-permute-done.8.refs_5_) | copy-start | bytes 1216516
  181.6 0.8 copy-start.6
  185.9 7.6 %collective-permute-start.10 = (bf16[208,384]{1,0:T(8,128)(2,1)S(1)}, bf16[208,384]{1,0:T(8,128)(2,1)S(1)}, u32[]{:S(2)}, u32[]{:S(2)}) collective-permute-start(bf16[208,384]{1,0:T(8,128)(2,1)S(1)} %split.39), channel_id=1, source_target_pairs={{0,1},{1,0},{2,3},{3,2},{4,5},{5,4},{6,7},{7,6},{8,9},{9,8},{10,11... | collective-permute-start | bytes 479240 | tf_op jit(solution)/shard_map/ppermute | solution.py:25
  239.0 8.2 %collective-permute-start.11 = (bf16[384,512]{1,0:T(8,128)(2,1)S(1)}, bf16[384,512]{1,0:T(8,128)(2,1)S(1)}, u32[]{:S(2)}, u32[]{:S(2)}) collective-permute-start(bf16[384,512]{1,0:T(8,128)(2,1)S(1)} %pad_maximum_fusion), channel_id=1, source_target_pairs={{0,1},{1,0},{2,3},{3,2},{4,5},{5,4},{6,7},{7,6},{8,9},{9,8},{10,11... | collective-permute-start | bytes 1179656 | tf_op jit(solution)/shard_map/ppermute | solution.py:25
